TPU v7x, 256 devices: a whole 4x4x8 slice. The times are simulated.
256 devices in a mesh: section: 4 (over x), depth: 64 (over z, y, core).
Axes of the slice: x: 4, y: 4, z: 8, core: 2. Of those that a mesh axis runs over, the one named last changes fastest.
Arguments:
- activations: float32 [4, 4, 128, 64, 256], P('section', None, 'depth'), may hold values from -6 to 6
- filters: float32 [4, 27, 64, 64], P('section'), may hold values from -0.15625 to 0.15625
- cotangent: float32 [4, 128, 64, 256], P(None, 'depth'), may hold values from -6 to 6
Outputs:
- input_grads: float32 [4, 4, 128, 64, 256], P('section', None, 'depth')
- filter_grads: float32 [4, 27, 64, 64], P('section')
All inputs are finite; a program needn't handle non-finite values.
Results may differ from a plain program's by a relative error of at most 0.0003.
Values sent between devices are 32-bit elements; how exact they have to be, the bound alone decides.
No kernel may reach another device: no remote copies, remote signals or barrier semaphores. Data moves between devices by JAX's collectives and lax.ppermute only.
A program may use at most 128 MiB of HBM per device.

v0:
```python
import math

import jax
import jax.numpy as jnp
from jax import lax
from jax.experimental import pallas as pl
from jax.experimental.pallas import tpu as pltpu
from jax.sharding import Mesh
from jax.sharding import PartitionSpec as P


H = 16
W = 16
C = 64
DEPTH = ("depth_0", "depth_1", "depth_2")
PLANE = ("depth_0", "depth_1")
CORE = "depth_2"
N = 4
F32 = jnp.float32
BF16 = jnp.bfloat16
LIMIT = 24 * 2**20
VMEM = pl.BlockSpec(memory_space=pltpu.VMEM)
SMEM = pl.BlockSpec(memory_space=pltpu.SMEM)


def run(body, args, outs, scratch=(), flops=0):
    nbytes = sum(a.size * a.dtype.itemsize for a in args)
    return pl.pallas_call(
        body,
        out_shape=[jax.ShapeDtypeStruct(s, t) for s, t in outs],
        in_specs=[SMEM] + [VMEM] * (len(args) - 1),
        out_specs=[VMEM] * len(outs),
        scratch_shapes=[pltpu.VMEM(s, t) for s, t in scratch],
        cost_estimate=pl.CostEstimate(flops=flops, bytes_accessed=nbytes, transcendentals=0),
        compiler_params=pltpu.CompilerParams(vmem_limit_bytes=LIMIT),
    )(*args)


def split(x):
    high = x.astype(BF16)
    return high, (x - high.astype(F32)).astype(BF16)


def columns():
    return lax.broadcasted_iota(jnp.int32, (C, H * W), 1)


def across(x):
    place = columns()
    left = jnp.where(place % W == 0, 0.0, pltpu.roll(x, 1, 1))
    right = jnp.where(place % W == W - 1, 0.0, pltpu.roll(x, H * W - 1, 1))
    return jnp.concatenate([left, x, right], axis=0)


def down(x):
    return jnp.where(columns() < W, 0.0, pltpu.roll(x, W, 1))


def up(x):
    return jnp.where(columns() >= H * W - W, 0.0, pltpu.roll(x, H * W - W, 1))


def dot(a, b):
    return jnp.dot(a, b, preferred_element_type=F32)


def conv(taps, high, low):
    first = dot(taps, high)
    z = first[:192] + first[192:] + dot(taps[:192], low)
    return z[C : 2 * C] + down(z[:C]) + up(z[2 * C :])


def silu_slope(preact):
    gate = 1.0 / (1.0 + jnp.exp(-preact))
    return gate * (1.0 + preact * (1.0 - gate))


def prepare_body(s_ref, f_ref, forward_ref, mine_ref, yours_ref, back):
    for b in range(3):
        rows = slice(b * C, b * C + C)
        low_rows = slice(192 + b * C, 192 + b * C + C)
        taps = [f_ref[0, a * 9 + b * 3 + cc] for a in range(3) for cc in range(3)]
        high, low = split(jnp.concatenate(taps, axis=1))
        forward_ref[rows] = high
        forward_ref[low_rows] = low
        taps = [f_ref[0, (2 - a) * 9 + (2 - b) * 3 + 2 - cc] for a in range(3) for cc in range(3)]
        back[rows] = jnp.concatenate(taps, axis=0).T
    c = s_ref[1]
    mine_ref[...] = back[pl.ds(pl.multiple_of(c * 96, 32), 96)]
    yours_ref[...] = back[pl.ds(pl.multiple_of((1 - c) * 96, 32), 96)]


def slope_body(s_ref, act_ref, left_ref, right_ref, taps_ref, d0, d1, d2, d3, vh_ref, vl_ref):
    s = s_ref[0]
    for k, out in enumerate((d0, d1, d2, d3)):
        m = (s + k) % N
        for e in range(4):
            if e == 0:
                x = left_ref[m]
            elif e == 3:
                x = right_ref[m]
            else:
                x = act_ref[m, e - 1]
            high, low = split(across(x))
            vh_ref[k, e] = high
            vl_ref[k, e] = low
        for d in range(2):
            z = conv(taps_ref[...], vh_ref[k, d : d + 3].reshape(576, 256), vl_ref[k, d : d + 3].reshape(576, 256))
            out[d] = silu_slope(z)


def chosen(index, refs, *at):
    out = refs[0][at]
    for k in range(1, len(refs)):
        out = jnp.where(index == k, refs[k][at], out)
    return out


def pick_body(s_ref, d0, d1, d2, d3, cot_ref, s3_ref, to_right, to_left):
    m = s_ref[0]
    refs = (d0, d1, d2, d3)
    for d in range(2):
        top = cot_ref[m, d] * chosen((m + N - 3) % N, refs, d)
        s3_ref[d] = top
        to_right[d] = top
        to_left[d] = top
    to_right[2] = chosen((m + N - 2) % N, refs, 1)
    to_left[2] = chosen((m + N - 2) % N, refs, 0)


def taps_body(s_ref, mine_ref, yours_ref, below_ref, above_ref, far0_ref, far1_ref, other_ref, out_ref):
    s = s_ref[0]
    c = s_ref[1]

    def put(layer, row, x):
        high, low = split(x)
        size = x.shape[0]
        out_ref[layer, pl.ds(row, size)] = high
        out_ref[layer, pl.ds(192 + row, size)] = low

    mine = pl.multiple_of(c * 96, 32)
    yours = pl.multiple_of((1 - c) * 96, 32)
    put(s, mine, mine_ref[...])
    put(s, yours, yours_ref[...])
    put((s + 3) % N, mine, below_ref[...])
    put((s + 1) % N, mine, above_ref[...])
    put((s + 2) % N, mine, jnp.concatenate([far0_ref[...], far1_ref[...]], axis=0))
    put((s + 3) % N, yours, other_ref[0:96])
    put((s + 1) % N, yours, other_ref[96:192])
    put((s + 2) % N, yours, other_ref[192:288])


def two_layers(layer, m, left_ref, right_ref, factors, mid_ref, taps_ref, ig_a, slope_a, vh, vl, wh, wl):
    for e in range(6):
        x = left_ref[e] if e < 2 else (mid_ref[e - 2] if e < 4 else right_ref[e - 4])
        high, low = split(across(x))
        vh[e] = high
        vl[e] = low
    for d in range(4):
        g = conv(taps_ref[layer], vh[d : d + 3].reshape(576, 256), vl[d : d + 3].reshape(576, 256))
        if d == 0:
            factor = left_ref[2]
        elif d == 3:
            factor = right_ref[2]
        else:
            factor = chosen((m + N - layer + 1) % N, factors, d - 1)
        slope = g * factor
        if 0 < d < 3:
            ig_a[d - 1] = g
            slope_a[d - 1] = slope
        high, low = split(across(slope))
        wh[d] = high
        wl[d] = low
    return [
        conv(taps_ref[layer - 1], wh[d : d + 3].reshape(576, 256), wl[d : d + 3].reshape(576, 256)) for d in range(2)
    ]


def top_body(s_ref, left_ref, right_ref, d0, d1, d2, d3, s3_ref, taps_ref, *refs):
    ig3, s2, ig2, s1, to_right, to_left, vh, vl, wh, wl = refs
    m = s_ref[0]
    factors = (d0, d1, d2, d3)
    grads = two_layers(3, m, left_ref, right_ref, factors, s3_ref, taps_ref, ig3, s2, vh, vl, wh, wl)
    for d, g in enumerate(grads):
        ig2[d] = g
        slope = g * chosen((m + N - 1) % N, factors, d)
        s1[d] = slope
        to_right[d] = slope
        to_left[d] = slope
    to_right[2] = chosen(m, factors, 1)
    to_left[2] = chosen(m, factors, 0)


def low_body(s_ref, left_ref, right_ref, d0, d1, d2, d3, s3, s2, s1, ig3, ig2, taps_ref, *refs):
    o, p, s0, ig1, ig0, vh, vl, wh, wl = refs[:4], refs[4:8], *refs[8:]
    m = s_ref[0]
    grads = two_layers(1, m, left_ref, right_ref, (d0, d1, d2, d3), s1, taps_ref, ig1, s0, vh, vl, wh, wl)
    for d in range(2):
        ig0[d] = grads[d]
        for k in range(N):
            o[k][d] = chosen((m + k) % N, (s0, s1, s2, s3), d)
            p[k][d] = chosen((m + k) % N, (ig0, ig1, ig2, ig3), d)


def filter_body(s_ref, g0, g1, g2, g3, vh_ref, vl_ref, keep_ref, send_ref, acc):
    c = s_ref[1]
    nt = (((1,), (1,)), ((), ()))
    for k, ref in enumerate((g0, g1, g2, g3)):
        for d in range(2):
            x = ref[d]
            high, low = split(jnp.concatenate([up(x), x, down(x)], axis=0))
            v = (N - k) % N
            right_high = vh_ref[v, d : d + 3].reshape(576, 256)
            right_low = vl_ref[v, d : d + 3].reshape(576, 256)
            first = lax.dot_general(jnp.concatenate([high, low], axis=0), right_high, nt, preferred_element_type=F32)
            z = first[:192] + first[192:] + lax.dot_general(high, right_low, nt, preferred_element_type=F32)
            if k == 0 and d == 0:
                acc[...] = z
            else:
                acc[...] += z

    def piece(row, size):
        if row < 768:
            j = row // 192
            return acc[row - j * 192 : row - j * 192 + size, j * 128 : (j + 1) * 128]
        r = row - 768
        return jnp.concatenate([acc[r : r + size, 512:576], acc[r + 96 : r + 96 + size, 512:576]], axis=1)

    for half in range(2):

        def fill(ref):
            row = 432 * half
            stop = row + 432
            while row < stop:
                size = min((row // 192 + 1) * 192 if row < 768 else 864, stop) - row
                ref[row - 432 * half : row - 432 * half + size] = piece(row, size)
                row += size
            ref[432:512] = jnp.zeros((80, 128), F32)

        @pl.when(c == half)
        def _():
            fill(keep_ref)

        @pl.when(c != half)
        def _():
            fill(send_ref)


def finish_body(s_ref, own_ref, other_ref, out_ref, full):
    c = s_ref[1]
    full[pl.ds(pl.multiple_of(c * 432, 8), 432)] = own_ref[0:432]
    full[pl.ds(pl.multiple_of((1 - c) * 432, 8), 432)] = other_ref[0:432]
    for a in range(3):
        for b in range(3):
            for cc in range(3):
                block = a * 3 + cc
                if block < 8:
                    x = full[(block // 2) * 192 + b * C : (block // 2) * 192 + b * C + C]
                    x = x[:, (block % 2) * C : (block % 2) * C + C]
                    out_ref[0, a * 9 + b * 3 + cc] = x
                else:
                    for part in range(2):
                        row = b * C + part * 32
                        side = 0 if row < 96 else 1
                        x = full[768 + row - 96 * side : 768 + row - 96 * side + 32, side * C : side * C + C]
                        out_ref[0, a * 9 + b * 3 + cc, part * 32 : part * 32 + 32] = x


def gather_body(s_ref, x0, x1, x2, x3, out_ref):
    s = s_ref[0]
    for k, ref in enumerate((x0, x1, x2, x3)):
        out_ref[0, (s + N - k) % N] = ref[...]


def shift(x, by):
    return lax.ppermute(x, "section", [(i, (i + by) % N) for i in range(N)])


def handed(parts):
    return [parts[0]] + [shift(parts[k], k) for k in (1, 2, 3)]


def swapped(x):
    return lax.ppermute(x, CORE, [(0, 1), (1, 0)])


def neighbours(to_right, to_left):
    count = lax.axis_size(DEPTH)
    left = lax.ppermute(to_right, DEPTH, [(i, i + 1) for i in range(count - 1)])
    right = lax.ppermute(to_left, DEPTH, [(i + 1, i) for i in range(count - 1)])
    return left, right


def window(activations, filters, cotangent):
    s = lax.axis_index("section")
    c = lax.axis_index(CORE)
    place = jnp.stack([s, c]).astype(jnp.int32)
    act = activations[0]
    plane = (C, H * W)
    two = ((2, *plane), F32)
    three = ((3, *plane), F32)

    left, right = neighbours(act[:, 1], act[:, 0])
    forward, mine, yours = run(
        prepare_body,
        (place, filters),
        [((384, 576), BF16), ((96, 576), F32), ((96, 576), F32)],
        [((192, 576), F32)],
        flops=10**6,
    )
    *factors, vh, vl = run(
        slope_body,
        (place, act, left, right, forward),
        [two] * 4 + [((N, 4, 192, 256), BF16)] * 2,
        flops=2 * 8 * 192 * 576 * 256 * 3,
    )
    factors = handed(factors)

    below = shift(mine, 1)
    above = shift(mine, -1)
    far0 = shift(below[:48], 1)
    far1 = shift(above[48:], -1)
    other = swapped(jnp.concatenate([below, above, far0, far1], axis=0))
    (taps,) = run(
        taps_body, (place, mine, yours, below, above, far0, far1, other), [((N, 384, 576), BF16)], flops=10**6
    )

    s3, to_right, to_left = run(pick_body, (place, *factors, cotangent), [two, three, three], flops=10**6)
    left, right = neighbours(to_right, to_left)
    scratch = [((6, 192, 256), BF16)] * 2 + [((4, 192, 256), BF16)] * 2
    ig3, s2, ig2, s1, to_right, to_left = run(
        top_body,
        (place, left, right, *factors, s3, taps),
        [two, two, two, two, three, three],
        scratch,
        flops=2 * 6 * 192 * 576 * 256 * 3,
    )
    left, right = neighbours(to_right, to_left)
    packed = run(
        low_body,
        (place, left, right, *factors, s3, s2, s1, ig3, ig2, taps),
        [two] * 8,
        [((2, *plane), F32)] * 3 + scratch,
        flops=2 * 6 * 192 * 576 * 256 * 3,
    )
    slopes = handed(packed[:4])
    slopes, grads = lax.optimization_barrier((slopes, packed[4:]))
    grads = handed(grads)

    keep, send = run(
        filter_body,
        (place, *slopes, vh, vl),
        [((512, 128), F32)] * 2,
        [((192, 576), F32)],
        flops=2 * 8 * 192 * 576 * 256 * 3,
    )
    part = (keep + swapped(send)).reshape(32, 16, 128)
    (input_grads,) = run(gather_body, (place, *grads), [((1, N, 2, *plane), F32)], flops=10**6)
    part, input_grads = lax.optimization_barrier((part, input_grads))
    part = lax.all_to_all(part, PLANE, 0, 0, tiled=True)
    scaling = 1.0 / math.sqrt(N * 2 * lax.axis_size(DEPTH) * H * W)
    total = jnp.sum(part, axis=0) * scaling
    part = lax.all_to_all(jnp.broadcast_to(total[None], (32, 16, 128)), PLANE, 0, 0, tiled=True).reshape(512, 128)
    other_part = swapped(part)
    (filter_grads,) = run(
        finish_body, (place, part, other_part), [((1, 27, C, C), F32)], [((864, 128), F32)], flops=10**6
    )
    return input_grads, filter_grads


def solution(mesh):
    finer = Mesh(
        mesh.devices.reshape(mesh.shape["section"], 8, 4, 2),
        ("section", "depth_0", "depth_1", "depth_2"),
    )
    placed = (
        P("section", None, DEPTH, None, None),
        P("section", None, None, None),
        P(None, DEPTH, None, None),
    )
    return jax.shard_map(
        window,
        mesh=finer,
        in_specs=placed,
        out_specs=(P("section", None, DEPTH, None, None), P("section", None, None, None)),
        check_vma=False,
    )
```

profile of v0, /device:TPU:2, one launch (start us, length us, event | category | flops | bytes accessed | tf_op | source)
XLA Modules:
  0.0 135.9 jit_solution(11733605708056504826)
XLA Ops:
  0.6 0.1 pad_add_fusion.s_ref
  0.7 0.0 copy-start
  0.7 1.2 copy-done
  1.9 1.0 shard_map.50
  2.9 2.3 %collective-permute-start.8 = (f32[96,576]{1,0:T(8,128)S(1)}, f32[96,576]{1,0:T(8,128)S(1)}, u32[]{:S(2)}, u32[]{:S(2)}) collective-permute-start(f32[96,576]{1,0:T(8,128)S(1)} %get-tuple-element.48.mine_ref), channel_id=1, source_target_pairs={{0,192},{64,0},{128,64},{192,128},{1,193},{65,1},{129,65},{193,129... | collective-permute-start | bytes 663560 | tf_op jit(solution)/shard_map/ppermute | solution.py:276
  5.2 0.0 collective-permute-start.7
  5.2 1.1 copy.9
  6.3 0.0 copy-start.1
  6.3 4.4 %collective-permute-done.8.above_ref = f32[96,576]{1,0:T(8,128)S(1)} collective-permute-done((f32[96,576]{1,0:T(8,128)S(1)}, f32[96,576]{1,0:T(8,128)S(1)}, u32[]{:S(2)}, u32[]{:S(2)}) %collective-permute-start.8) | collective-permute-done | bytes 221216 | tf_op jit(solution)/shard_map/ppermute | solution.py:276
  10.7 0.9 collective-permute-start.10
  11.5 0.4 collective-permute-done.7.below_ref
  11.9 0.9 collective-permute-start.9
  12.9 1.3 collective-permute-start.1
  14.2 3.0 %collective-permute-start = (f32[4,64,256]{2,1,0:T(8,128)S(1)}, f32[4,64,256]{2,1,0:T(8,128)S(1)}, u32[]{:S(2)}, u32[]{:S(2)}) collective-permute-start(f32[4,64,256]{2,1,0:T(8,128)S(1)} %get-tuple-element.79), channel_id=1, source_target_pairs={{0,1},{1,2},{2,3},{3,4},{4,5},{5,6},{6,7},{7,8},{8,9},{9,10},{10,1... | collective-permute-start | bytes 786440 | tf_op jit(solution)/shard_map/ppermute | solution.py:289
  17.3 0.0 collective-permute-done.10.far1_ref
  17.3 0.9 collective-permute-done.9.far0_ref
  18.2 0.4 collective-permute-start.11
  18.6 0.0 collective-permute-done.1.right_ref
  18.6 0.0 collective-permute-done.left_ref
  18.6 0.0 copy-done.1
  18.6 0.0 copy-start.2
  18.6 2.8 %shard_map.51 = (f32[2,64,256]{2,1,0:T(8,128)S(1)}, f32[2,64,256]{2,1,0:T(8,128)S(1)}, f32[2,64,256]{2,1,0:T(8,128)S(1)}, f32[2,64,256]{2,1,0:T(8,128)S(1)}, bf1...) custom-call(s32[2]{0:T(128)S(1)} %pad_add_fusion.s_ref, f32[4,2,64,256]{3,2,1,0:T(8,128)S(1)} %bitcast.14, ...), custom_call_target="tpu_custom_call" | custom-call | flops 1358954496 | bytes 1490952 | tf_op jit(solution)/shard_map/pallas_call | solution.py:28
  21.4 2.0 %collective-permute-start.2 = (f32[2,64,256]{2,1,0:T(8,128)S(1)}, f32[2,64,256]{2,1,0:T(8,128)S(1)}, u32[]{:S(2)}, u32[]{:S(2)}) collective-permute-start(f32[2,64,256]{2,1,0:T(8,128)S(1)} %get-tuple-element.42), channel_id=1, source_target_pairs={{0,64},{64,128},{128,192},{192,0},{1,65},{65,129},{129,193},{193,1... | collective-permute-start | bytes 393224 | tf_op jit(solution)/shard_map/ppermute | solution.py:276
  23.4 3.2 %collective-permute-start.3 = (f32[2,64,256]{2,1,0:T(8,128)S(1)}, f32[2,64,256]{2,1,0:T(8,128)S(1)}, u32[]{:S(2)}, u32[]{:S(2)}) collective-permute-start(f32[2,64,256]{2,1,0:T(8,128)S(1)} %get-tuple-element.43), channel_id=1, source_target_pairs={{0,128},{64,192},{128,0},{192,64},{1,129},{65,193},{129,1},{193,65... | collective-permute-start | bytes 393224 | tf_op jit(solution)/shard_map/ppermute | solution.py:276
  26.6 2.1 %collective-permute-start.4 = (f32[2,64,256]{2,1,0:T(8,128)S(1)}, f32[2,64,256]{2,1,0:T(8,128)S(1)}, u32[]{:S(2)}, u32[]{:S(2)}) collective-permute-start(f32[2,64,256]{2,1,0:T(8,128)S(1)} %get-tuple-element.44), channel_id=1, source_target_pairs={{0,192},{64,0},{128,64},{192,128},{1,193},{65,1},{129,65},{193,129... | collective-permute-start | bytes 393224 | tf_op jit(solution)/shard_map/ppermute | solution.py:276
  28.7 0.0 collective-permute-done.2.d1
  28.7 1.2 collective-permute-done.3.d2
  29.9 3.6 %collective-permute-done.4.d3 = f32[2,64,256]{2,1,0:T(8,128)S(1)} collective-permute-done((f32[2,64,256]{2,1,0:T(8,128)S(1)}, f32[2,64,256]{2,1,0:T(8,128)S(1)}, u32[]{:S(2)}, u32[]{:S(2)}) %collective-permute-start.4) | collective-permute-done | bytes 131104 | tf_op jit(solution)/shard_map/ppermute | solution.py:276
  33.5 0.0 copy-done.2
  33.5 0.6 shard_map.52
  34.1 2.6 %collective-permute-start.5 = (f32[3,64,256]{2,1,0:T(8,128)S(1)}, f32[3,64,256]{2,1,0:T(8,128)S(1)}, u32[]{:S(2)}, u32[]{:S(2)}) collective-permute-start(f32[3,64,256]{2,1,0:T(8,128)S(1)} %get-tuple-element.45), channel_id=1, source_target_pairs={{0,1},{1,2},{2,3},{3,4},{4,5},{5,6},{6,7},{7,8},{8,9},{9,10},{10,1... | collective-permute-start | bytes 589832 | tf_op jit(solution)/shard_map/ppermute | solution.py:289
  36.7 1.3 collective-permute-start.6
  38.0 0.0 collective-permute-done.11.other_ref
  38.0 0.8 shard_map.53.taps_ref
  38.8 0.0 collective-permute-done.5.left_ref
  38.8 4.2 %collective-permute-done.6.right_ref = f32[3,64,256]{2,1,0:T(8,128)S(1)} collective-permute-done((f32[3,64,256]{2,1,0:T(8,128)S(1)}, f32[3,64,256]{2,1,0:T(8,128)S(1)}, u32[]{:S(2)}, u32[]{:S(2)}) %collective-permute-start.6) | collective-permute-done | bytes 196640 | tf_op jit(solution)/shard_map/ppermute | solution.py:290
  43.0 2.6 %shard_map.54 = (f32[2,64,256]{2,1,0:T(8,128)S(1)}, f32[2,64,256]{2,1,0:T(8,128)S(1)}, f32[2,64,256]{2,1,0:T(8,128)S(1)}, f32[2,64,256]{2,1,0:T(8,128)S(1)}, f32...) custom-call(s32[2]{0:T(128)S(1)} %pad_add_fusion.s_ref, f32[3,64,256]{2,1,0:T(8,128)S(1)} %collective-permute-done.5.left_ref, ...), custom_call_target="tpu_custom_call" | custom-call | flops 1019215872 | bytes 2818056 | tf_op jit(solution)/shard_map/pallas_call | solution.py:28
  45.6 6.1 %collective-permute-start.12 = (f32[3,64,256]{2,1,0:T(8,128)S(1)}, f32[3,64,256]{2,1,0:T(8,128)S(1)}, u32[]{:S(2)}, u32[]{:S(2)}) collective-permute-start(f32[3,64,256]{2,1,0:T(8,128)S(1)} %get-tuple-element.50), channel_id=1, source_target_pairs={{0,1},{1,2},{2,3},{3,4},{4,5},{5,6},{6,7},{7,8},{8,9},{9,10},{10,1... | collective-permute-start | bytes 589832 | tf_op jit(solution)/shard_map/ppermute | solution.py:289
  51.7 1.5 %collective-permute-start.13 = (f32[3,64,256]{2,1,0:T(8,128)S(1)}, f32[3,64,256]{2,1,0:T(8,128)S(1)}, u32[]{:S(2)}, u32[]{:S(2)}) collective-permute-start(f32[3,64,256]{2,1,0:T(8,128)S(1)} %get-tuple-element.51), channel_id=1, source_target_pairs={{1,0},{2,1},{3,2},{4,3},{5,4},{6,5},{7,6},{8,7},{9,8},{10,9},{11,1... | collective-permute-start | bytes 589832 | tf_op jit(solution)/shard_map/ppermute | solution.py:290
  53.1 0.0 collective-permute-done.12.left_ref
  53.2 1.8 %collective-permute-done.13.right_ref = f32[3,64,256]{2,1,0:T(8,128)S(1)} collective-permute-done((f32[3,64,256]{2,1,0:T(8,128)S(1)}, f32[3,64,256]{2,1,0:T(8,128)S(1)}, u32[]{:S(2)}, u32[]{:S(2)}) %collective-permute-start.13) | collective-permute-done | bytes 196640 | tf_op jit(solution)/shard_map/ppermute | solution.py:290
  55.0 2.6 %shard_map.55 = (f32[2,64,256]{2,1,0:T(8,128)S(1)}, f32[2,64,256]{2,1,0:T(8,128)S(1)}, f32[2,64,256]{2,1,0:T(8,128)S(1)}, f32[2,64,256]{2,1,0:T(8,128)S(1)}, f32...) custom-call(s32[2]{0:T(128)S(1)} %pad_add_fusion.s_ref, ...), custom_call_target="tpu_custom_call" | custom-call | flops 1019215872 | bytes 3342344 | tf_op jit(solution)/shard_map/pallas_call | solution.py:28
  57.6 1.1 collective-permute-start.14
  58.8 3.1 %collective-permute-start.15 = (f32[2,64,256]{2,1,0:T(8,128)S(1)}, f32[2,64,256]{2,1,0:T(8,128)S(1)}, u32[]{:S(2)}, u32[]{:S(2)}) collective-permute-start(f32[2,64,256]{2,1,0:T(8,128)S(1)} %get-tuple-element.58), channel_id=1, source_target_pairs={{0,128},{64,192},{128,0},{192,64},{1,129},{65,193},{129,1},{193,65... | collective-permute-start | bytes 393224 | tf_op jit(solution)/shard_map/ppermute | solution.py:276
  61.8 1.6 %collective-permute-start.16 = (f32[2,64,256]{2,1,0:T(8,128)S(1)}, f32[2,64,256]{2,1,0:T(8,128)S(1)}, u32[]{:S(2)}, u32[]{:S(2)}) collective-permute-start(f32[2,64,256]{2,1,0:T(8,128)S(1)} %get-tuple-element.59), channel_id=1, source_target_pairs={{0,192},{64,0},{128,64},{192,128},{1,193},{65,1},{129,65},{193,129... | collective-permute-start | bytes 393224 | tf_op jit(solution)/shard_map/ppermute | solution.py:276
  63.4 0.0 collective-permute-done.14.g1
  63.4 1.9 %collective-permute-done.15.g2 = f32[2,64,256]{2,1,0:T(8,128)S(1)} collective-permute-done((f32[2,64,256]{2,1,0:T(8,128)S(1)}, f32[2,64,256]{2,1,0:T(8,128)S(1)}, u32[]{:S(2)}, u32[]{:S(2)}) %collective-permute-start.15) | collective-permute-done | bytes 131104 | tf_op jit(solution)/shard_map/ppermute | solution.py:276
  65.2 3.0 %collective-permute-done.16.g3 = f32[2,64,256]{2,1,0:T(8,128)S(1)} collective-permute-done((f32[2,64,256]{2,1,0:T(8,128)S(1)}, f32[2,64,256]{2,1,0:T(8,128)S(1)}, u32[]{:S(2)}, u32[]{:S(2)}) %collective-permute-start.16) | collective-permute-done | bytes 131104 | tf_op jit(solution)/shard_map/ppermute | solution.py:276
  68.2 2.9 %shard_map.56 = (f32[512,128]{1,0:T(8,128)S(1)}, f32[512,128]{1,0:T(8,128)S(1)}) custom-call(s32[2]{0:T(128)S(1)} %pad_add_fusion.s_ref, f32[2,64,256]{2,1,0:T(8,128)S(1)} %get-tuple-element.64.g0, f32[2,64,256]{2,1,0:T(8,128)S(1)} %collective-permute-done.14.g1, f32[2,64,256]{2,1,0:T(8,128)S(1)} %collective-permute-done.15.g2, ...), custom_call_target="tpu_custom_call" | custom-call | flops 1358954496 | bytes 3670024 | tf_op jit(solution)/shard_map/pallas_call | solution.py:28
  71.2 1.3 collective-permute-start.17
  72.4 0.6 collective-permute-start.18
  73.0 3.0 %collective-permute-start.19 = (f32[2,64,256]{2,1,0:T(8,128)S(1)}, f32[2,64,256]{2,1,0:T(8,128)S(1)}, u32[]{:S(2)}, u32[]{:S(2)}) collective-permute-start(f32[2,64,256]{2,1,0:T(8,128)S(1)} %get-tuple-element.74), channel_id=1, source_target_pairs={{0,128},{64,192},{128,0},{192,64},{1,129},{65,193},{129,1},{193,65... | collective-permute-start | bytes 393224 | tf_op jit(solution)/shard_map/ppermute | solution.py:276
  76.1 1.9 %collective-permute-start.20 = (f32[2,64,256]{2,1,0:T(8,128)S(1)}, f32[2,64,256]{2,1,0:T(8,128)S(1)}, u32[]{:S(2)}, u32[]{:S(2)}) collective-permute-start(f32[2,64,256]{2,1,0:T(8,128)S(1)} %get-tuple-element.75), channel_id=1, source_target_pairs={{0,192},{64,0},{128,64},{192,128},{1,193},{65,1},{129,65},{193,129... | collective-permute-start | bytes 393224 | tf_op jit(solution)/shard_map/ppermute | solution.py:276
  78.0 0.0 collective-permute-done.18.x1
  78.0 2.9 %collective-permute-done.19.x2 = f32[2,64,256]{2,1,0:T(8,128)S(1)} collective-permute-done((f32[2,64,256]{2,1,0:T(8,128)S(1)}, f32[2,64,256]{2,1,0:T(8,128)S(1)}, u32[]{:S(2)}, u32[]{:S(2)}) %collective-permute-start.19) | collective-permute-done | bytes 131104 | tf_op jit(solution)/shard_map/ppermute | solution.py:276
  80.9 1.7 %collective-permute-done.20.x3 = f32[2,64,256]{2,1,0:T(8,128)S(1)} collective-permute-done((f32[2,64,256]{2,1,0:T(8,128)S(1)}, f32[2,64,256]{2,1,0:T(8,128)S(1)}, u32[]{:S(2)}, u32[]{:S(2)}) %collective-permute-start.20) | collective-permute-done | bytes 131104 | tf_op jit(solution)/shard_map/ppermute | solution.py:276
  82.6 1.4 %shard_map.57 = f32[1,4,2,64,256]{4,3,2,1,0:T(8,128)} custom-call(s32[2]{0:T(128)S(1)} %pad_add_fusion.s_ref, f32[2,64,256]{2,1,0:T(8,128)S(1)} %get-tuple-element.72.x0, f32[2,64,256]{2,1,0:T(8,128)S(1)} %collective-permute-done.18.x1, f32[2,64,256]{2,1,0:T(8,128)S(1)} %collective-permute-done.19.x2, f32[2,64,256]{2,1,0:T(8,128)S(1)} %collective-permute-done.20.x3), custom_call_target="tpu_custom_call" | custom-call | flops 1000000 | bytes 524296 | tf_op jit(solution)/shard_map/pallas_call | solution.py:28
  84.0 0.0 collective-permute-done.17
  84.0 32.3 %all_to_all.10 = f32[32,16,128]{2,1,0:T(8,128)S(1)} all-to-all(f32[32,16,128]{2,1,0:T(8,128)S(1)} %bitcast.16), channel_id=1, replica_groups=mesh['section'=4,'depth_0'=8,'depth_1'=4,'depth_2'=2] {'depth_0','depth_1'}, dimensions={0} | all-to-all | bytes 524288 | tf_op jit(solution)/shard_map/all_to_all | solution.py:360
  116.4 16.3 %all_to_all.11 = f32[32,16,128]{2,1,0:T(8,128)S(1)} all-to-all(f32[32,16,128]{2,1,0:T(8,128)S(1)} %broadcast_in_dim.2), channel_id=1, replica_groups=mesh['section'=4,'depth_0'=8,'depth_1'=4,'depth_2'=2] {'depth_0','depth_1'}, dimensions={0} | all-to-all | bytes 524288 | tf_op jit(solution)/shard_map/all_to_all | solution.py:363
  132.7 0.0 collective-permute-start.21
  132.7 1.5 %collective-permute-done.21.other_ref = f32[512,128]{1,0:T(8,128)S(1)} collective-permute-done((f32[512,128]{1,0:T(8,128)S(1)}, f32[512,128]{1,0:T(8,128)S(1)}, u32[]{:S(2)}, u32[]{:S(2)}) %collective-permute-start.21) | collective-permute-done | bytes 262176 | tf_op jit(solution)/shard_map/ppermute | solution.py:284
  134.3 1.7 %shard_map.58 = f32[1,27,64,64]{3,2,1,0:T(8,128)} custom-call(s32[2]{0:T(128)S(1)} %pad_add_fusion.s_ref, f32[512,128]{1,0:T(8,128)S(1)} %bitcast.13, f32[512,128]{1,0:T(8,128)S(1)} %collective-permute-done.21.other_ref), custom_call_target="tpu_custom_call" | custom-call | flops 1000000 | bytes 524296 | tf_op jit(solution)/shard_map/pallas_call | solution.py:28
  (8 shorter events, 0.2 us)
Async XLA Ops:
  0.7 1.2 copy-start
  2.9 7.8 %collective-permute-start.8 = (f32[96,576]{1,0:T(8,128)S(1)}, f32[96,576]{1,0:T(8,128)S(1)}, u32[]{:S(2)}, u32[]{:S(2)}) collective-permute-start(f32[96,576]{1,0:T(8,128)S(1)} %get-tuple-element.48.mine_ref), channel_id=1, source_target_pairs={{0,192},{64,0},{128,64},{192,128},{1,193},{65,1},{129,65},{193,129... | collective-permute-start | bytes 663560 | tf_op jit(solution)/shard_map/ppermute | solution.py:276
  5.2 6.7 %collective-permute-start.7 = (f32[96,576]{1,0:T(8,128)S(1)}, f32[96,576]{1,0:T(8,128)S(1)}, u32[]{:S(2)}, u32[]{:S(2)}) collective-permute-start(f32[96,576]{1,0:T(8,128)S(1)} %get-tuple-element.48.mine_ref), channel_id=1, source_target_pairs={{0,64},{64,128},{128,192},{192,0},{1,65},{65,129},{129,193},{193,1... | collective-permute-start | bytes 663560 | tf_op jit(solution)/shard_map/ppermute | solution.py:276
  6.3 12.3 %copy-start.1 = (f32[1,4,2,64,256]{4,3,2,1,0:T(8,128)S(1)}, f32[1,4,2,64,256]{4,3,2,1,0:T(8,128)}, u32[]{:S(2)}) copy-start(f32[1,4,2,64,256]{4,3,2,1,0:T(8,128)} %param.3) | copy-start | bytes 1572868
  10.7 6.6 %collective-permute-start.10 = (f32[48,576]{1,0:T(8,128)S(1)}, f32[48,576]{1,0:T(8,128)S(1)}, u32[]{:S(2)}, u32[]{:S(2)}) collective-permute-start(f32[48,576]{1,0:T(8,128)S(1)} %slice.19), channel_id=1, source_target_pairs={{0,192},{64,0},{128,64},{192,128},{1,193},{65,1},{129,65},{193,129... | collective-permute-start | bytes 331784 | tf_op jit(solution)/shard_map/ppermute | solution.py:276
  11.9 6.3 %collective-permute-start.9 = (f32[48,576]{1,0:T(8,128)S(1)}, f32[48,576]{1,0:T(8,128)S(1)}, u32[]{:S(2)}, u32[]{:S(2)}) collective-permute-start(f32[48,576]{1,0:T(8,128)S(1)} %slice.18), channel_id=1, source_target_pairs={{0,64},{64,128},{128,192},{192,0},{1,65},{65,129},{129,193},{193,1... | collective-permute-start | bytes 331784 | tf_op jit(solution)/shard_map/ppermute | solution.py:276
  12.9 5.7 %collective-permute-start.1 = (f32[4,64,256]{2,1,0:T(8,128)S(1)}, f32[4,64,256]{2,1,0:T(8,128)S(1)}, u32[]{:S(2)}, u32[]{:S(2)}) collective-permute-start(f32[4,64,256]{2,1,0:T(8,128)S(1)} %get-tuple-element.78), channel_id=1, source_target_pairs={{1,0},{2,1},{3,2},{4,3},{5,4},{6,5},{7,6},{8,7},{9,8},{10,9},{11,1... | collective-permute-start | bytes 786440 | tf_op jit(solution)/shard_map/ppermute | solution.py:290
  14.2 4.4 %collective-permute-start = (f32[4,64,256]{2,1,0:T(8,128)S(1)}, f32[4,64,256]{2,1,0:T(8,128)S(1)}, u32[]{:S(2)}, u32[]{:S(2)}) collective-permute-start(f32[4,64,256]{2,1,0:T(8,128)S(1)} %get-tuple-element.79), channel_id=1, source_target_pairs={{0,1},{1,2},{2,3},{3,4},{4,5},{5,6},{6,7},{7,8},{8,9},{9,10},{10,1... | collective-permute-start | bytes 786440 | tf_op jit(solution)/shard_map/ppermute | solution.py:289
  18.2 19.8 %collective-permute-start.11 = (f32[288,576]{1,0:T(8,128)S(1)}, f32[288,576]{1,0:T(8,128)S(1)}, u32[]{:S(2)}, u32[]{:S(2)}) collective-permute-start(f32[288,576]{1,0:T(8,128)S(1)} %pad_maximum_fusion), channel_id=1, source_target_pairs={{0,1},{1,0},{2,3},{3,2},{4,5},{5,4},{6,7},{7,6},{8,9},{9,8},{10,11... | collective-permute-start | bytes 1990664 | tf_op jit(solution)/shard_map/ppermute | solution.py:284
  18.6 14.9 %copy-start.2 = (f32[4,2,64,256]{3,2,1,0:T(8,128)S(1)}, f32[4,2,64,256]{3,2,1,0:T(8,128)}, u32[]{:S(2)}) copy-start(f32[4,2,64,256]{3,2,1,0:T(8,128)} %cot_ref.1) | copy-start | bytes 1572868
  21.4 7.3 %collective-permute-start.2 = (f32[2,64,256]{2,1,0:T(8,128)S(1)}, f32[2,64,256]{2,1,0:T(8,128)S(1)}, u32[]{:S(2)}, u32[]{:S(2)}) collective-permute-start(f32[2,64,256]{2,1,0:T(8,128)S(1)} %get-tuple-element.42), channel_id=1, source_target_pairs={{0,64},{64,128},{128,192},{192,0},{1,65},{65,129},{129,193},{193,1... | collective-permute-start | bytes 393224 | tf_op jit(solution)/shard_map/ppermute | solution.py:276
  23.4 6.5 %collective-permute-start.3 = (f32[2,64,256]{2,1,0:T(8,128)S(1)}, f32[2,64,256]{2,1,0:T(8,128)S(1)}, u32[]{:S(2)}, u32[]{:S(2)}) collective-permute-start(f32[2,64,256]{2,1,0:T(8,128)S(1)} %get-tuple-element.43), channel_id=1, source_target_pairs={{0,128},{64,192},{128,0},{192,64},{1,129},{65,193},{129,1},{193,65... | collective-permute-start | bytes 393224 | tf_op jit(solution)/shard_map/ppermute | solution.py:276
  26.6 7.0 %collective-permute-start.4 = (f32[2,64,256]{2,1,0:T(8,128)S(1)}, f32[2,64,256]{2,1,0:T(8,128)S(1)}, u32[]{:S(2)}, u32[]{:S(2)}) collective-permute-start(f32[2,64,256]{2,1,0:T(8,128)S(1)} %get-tuple-element.44), channel_id=1, source_target_pairs={{0,192},{64,0},{128,64},{192,128},{1,193},{65,1},{129,65},{193,129... | collective-permute-start | bytes 393224 | tf_op jit(solution)/shard_map/ppermute | solution.py:276
  34.1 4.7 %collective-permute-start.5 = (f32[3,64,256]{2,1,0:T(8,128)S(1)}, f32[3,64,256]{2,1,0:T(8,128)S(1)}, u32[]{:S(2)}, u32[]{:S(2)}) collective-permute-start(f32[3,64,256]{2,1,0:T(8,128)S(1)} %get-tuple-element.45), channel_id=1, source_target_pairs={{0,1},{1,2},{2,3},{3,4},{4,5},{5,6},{6,7},{7,8},{8,9},{9,10},{10,1... | collective-permute-start | bytes 589832 | tf_op jit(solution)/shard_map/ppermute | solution.py:289
  36.7 6.3 %collective-permute-start.6 = (f32[3,64,256]{2,1,0:T(8,128)S(1)}, f32[3,64,256]{2,1,0:T(8,128)S(1)}, u32[]{:S(2)}, u32[]{:S(2)}) collective-permute-start(f32[3,64,256]{2,1,0:T(8,128)S(1)} %get-tuple-element.46), channel_id=1, source_target_pairs={{1,0},{2,1},{3,2},{4,3},{5,4},{6,5},{7,6},{8,7},{9,8},{10,9},{11,1... | collective-permute-start | bytes 589832 | tf_op jit(solution)/shard_map/ppermute | solution.py:290
  45.6 7.6 %collective-permute-start.12 = (f32[3,64,256]{2,1,0:T(8,128)S(1)}, f32[3,64,256]{2,1,0:T(8,128)S(1)}, u32[]{:S(2)}, u32[]{:S(2)}) collective-permute-start(f32[3,64,256]{2,1,0:T(8,128)S(1)} %get-tuple-element.50), channel_id=1, source_target_pairs={{0,1},{1,2},{2,3},{3,4},{4,5},{5,6},{6,7},{7,8},{8,9},{9,10},{10,1... | collective-permute-start | bytes 589832 | tf_op jit(solution)/shard_map/ppermute | solution.py:289
  51.7 3.3 %collective-permute-start.13 = (f32[3,64,256]{2,1,0:T(8,128)S(1)}, f32[3,64,256]{2,1,0:T(8,128)S(1)}, u32[]{:S(2)}, u32[]{:S(2)}) collective-permute-start(f32[3,64,256]{2,1,0:T(8,128)S(1)} %get-tuple-element.51), channel_id=1, source_target_pairs={{1,0},{2,1},{3,2},{4,3},{5,4},{6,5},{7,6},{8,7},{9,8},{10,9},{11,1... | collective-permute-start | bytes 589832 | tf_op jit(solution)/shard_map/ppermute | solution.py:290
  57.6 5.7 %collective-permute-start.14 = (f32[2,64,256]{2,1,0:T(8,128)S(1)}, f32[2,64,256]{2,1,0:T(8,128)S(1)}, u32[]{:S(2)}, u32[]{:S(2)}) collective-permute-start(f32[2,64,256]{2,1,0:T(8,128)S(1)} %get-tuple-element.57), channel_id=1, source_target_pairs={{0,64},{64,128},{128,192},{192,0},{1,65},{65,129},{129,193},{193,1... | collective-permute-start | bytes 393224 | tf_op jit(solution)/shard_map/ppermute | solution.py:276
  58.8 6.5 %collective-permute-start.15 = (f32[2,64,256]{2,1,0:T(8,128)S(1)}, f32[2,64,256]{2,1,0:T(8,128)S(1)}, u32[]{:S(2)}, u32[]{:S(2)}) collective-permute-start(f32[2,64,256]{2,1,0:T(8,128)S(1)} %get-tuple-element.58), channel_id=1, source_target_pairs={{0,128},{64,192},{128,0},{192,64},{1,129},{65,193},{129,1},{193,65... | collective-permute-start | bytes 393224 | tf_op jit(solution)/shard_map/ppermute | solution.py:276
  61.8 6.4 %collective-permute-start.16 = (f32[2,64,256]{2,1,0:T(8,128)S(1)}, f32[2,64,256]{2,1,0:T(8,128)S(1)}, u32[]{:S(2)}, u32[]{:S(2)}) collective-permute-start(f32[2,64,256]{2,1,0:T(8,128)S(1)} %get-tuple-element.59), channel_id=1, source_target_pairs={{0,192},{64,0},{128,64},{192,128},{1,193},{65,1},{129,65},{193,129... | collective-permute-start | bytes 393224 | tf_op jit(solution)/shard_map/ppermute | solution.py:276
  71.2 12.8 %collective-permute-start.17 = (f32[512,128]{1,0:T(8,128)S(1)}, f32[512,128]{1,0:T(8,128)S(1)}, u32[]{:S(2)}, u32[]{:S(2)}) collective-permute-start(f32[512,128]{1,0:T(8,128)S(1)} %get-tuple-element.71), channel_id=1, source_target_pairs={{0,1},{1,0},{2,3},{3,2},{4,5},{5,4},{6,7},{7,6},{8,9},{9,8},{10,11... | collective-permute-start | bytes 786440 | tf_op jit(solution)/shard_map/ppermute | solution.py:284
  72.4 5.5 %collective-permute-start.18 = (f32[2,64,256]{2,1,0:T(8,128)S(1)}, f32[2,64,256]{2,1,0:T(8,128)S(1)}, u32[]{:S(2)}, u32[]{:S(2)}) collective-permute-start(f32[2,64,256]{2,1,0:T(8,128)S(1)} %get-tuple-element.73), channel_id=1, source_target_pairs={{0,64},{64,128},{128,192},{192,0},{1,65},{65,129},{129,193},{193,1... | collective-permute-start | bytes 393224 | tf_op jit(solution)/shard_map/ppermute | solution.py:276
  73.0 7.9 %collective-permute-start.19 = (f32[2,64,256]{2,1,0:T(8,128)S(1)}, f32[2,64,256]{2,1,0:T(8,128)S(1)}, u32[]{:S(2)}, u32[]{:S(2)}) collective-permute-start(f32[2,64,256]{2,1,0:T(8,128)S(1)} %get-tuple-element.74), channel_id=1, source_target_pairs={{0,128},{64,192},{128,0},{192,64},{1,129},{65,193},{129,1},{193,65... | collective-permute-start | bytes 393224 | tf_op jit(solution)/shard_map/ppermute | solution.py:276
  76.1 6.5 %collective-permute-start.20 = (f32[2,64,256]{2,1,0:T(8,128)S(1)}, f32[2,64,256]{2,1,0:T(8,128)S(1)}, u32[]{:S(2)}, u32[]{:S(2)}) collective-permute-start(f32[2,64,256]{2,1,0:T(8,128)S(1)} %get-tuple-element.75), channel_id=1, source_target_pairs={{0,192},{64,0},{128,64},{192,128},{1,193},{65,1},{129,65},{193,129... | collective-permute-start | bytes 393224 | tf_op jit(solution)/shard_map/ppermute | solution.py:276
  132.7 1.5 %collective-permute-start.21 = (f32[512,128]{1,0:T(8,128)S(1)}, f32[512,128]{1,0:T(8,128)S(1)}, u32[]{:S(2)}, u32[]{:S(2)}) collective-permute-start(f32[512,128]{1,0:T(8,128)S(1)} %bitcast.12), channel_id=1, source_target_pairs={{0,1},{1,0},{2,3},{3,2},{4,5},{5,4},{6,7},{7,6},{8,9},{9,8},{10,11... | collective-permute-start | bytes 786440 | tf_op jit(solution)/shard_map/ppermute | solution.py:284
where the time goes:
time: 138 us; the launch traced here: 136 us
  blocking collectives  48.7 us (35%)
  starting transfers between devices  40 us (29%)
  waiting for transfers between devices  27.5 us (20%)
  Pallas kernels  16.4 us (12%)
  local copies, waits for them, and re-layouts  2.33 us (2%)
    all_to_all x1, blocking collectives, window(): part = lax.all_to_all(part, PLANE, 0, 0, tiled=True)  32.3 us
    ppermute x13, starting transfers between devices, shift(): return lax.ppermute(x, 'section', [(i, (i + by) % N) for i in range(N)])  22.7 us
    ppermute x13, waiting for transfers between devices, shift(): return lax.ppermute(x, 'section', [(i, (i + by) % N) for i in range(N)])  19.9 us
    pallas_call x9, Pallas kernels, run(): pl.pallas_call(body, out_shape=[jax.ShapeDtypeStruct(s, t) for s, t in ou...  16.4 us
    all_to_all x1, blocking collectives, window(): lax.all_to_all(jnp.broadcast_to(total[None], (32, 16, 128)), PLANE, 0, 0,...  16.3 us
    ppermute x3, starting transfers between devices, neighbours(): left = lax.ppermute(to_right, DEPTH, [(i, i + 1) for i in range(count - 1)])  11.7 us
    ppermute x3, waiting for transfers between devices, neighbours(): right = lax.ppermute(to_left, DEPTH, [(i + 1, i) for i in range(count - 1)])  6.01 us
    ppermute x3, starting transfers between devices, neighbours(): right = lax.ppermute(to_left, DEPTH, [(i + 1, i) for i in range(count - 1)])  4.06 us
  transfers between devices with their start and end apart: 22, of which 12 were waited for; matrix products, arithmetic and copies ran while one was open for 1% of the time, Pallas kernels for 4%

commit v1 on v0

v1 whole, which is shorter than its diff:
```python
import functools
import math

import jax
import jax.numpy as jnp
from jax import lax
from jax.experimental import pallas as pl
from jax.experimental.pallas import tpu as pltpu
from jax.sharding import Mesh
from jax.sharding import PartitionSpec as P


H = 16
W = 16
C = 64
DEPTH = ("depth_0", "depth_1", "depth_2")
PLANE = ("depth_0", "depth_1")
CORE = "depth_2"
N = 4
F32 = jnp.float32
BF16 = jnp.bfloat16
LIMIT = 24 * 2**20
VMEM = pl.BlockSpec(memory_space=pltpu.VMEM)
SMEM = pl.BlockSpec(memory_space=pltpu.SMEM)


def run(body, args, outs, scratch=(), flops=0):
    nbytes = sum(a.size * a.dtype.itemsize for a in args)
    return pl.pallas_call(
        body,
        out_shape=[jax.ShapeDtypeStruct(s, t) for s, t in outs],
        in_specs=[SMEM] + [VMEM] * (len(args) - 1),
        out_specs=[VMEM] * len(outs),
        scratch_shapes=[pltpu.VMEM(s, t) for s, t in scratch],
        cost_estimate=pl.CostEstimate(flops=flops, bytes_accessed=nbytes, transcendentals=0),
        compiler_params=pltpu.CompilerParams(vmem_limit_bytes=LIMIT),
    )(*args)


def split(x):
    high = x.astype(BF16)
    return high, (x - high.astype(F32)).astype(BF16)


def columns():
    return lax.broadcasted_iota(jnp.int32, (C, H * W), 1)


def across(x):
    place = columns()
    left = jnp.where(place % W == 0, 0.0, pltpu.roll(x, 1, 1))
    right = jnp.where(place % W == W - 1, 0.0, pltpu.roll(x, H * W - 1, 1))
    return jnp.concatenate([left, x, right], axis=0)


def down(x):
    return jnp.where(columns() < W, 0.0, pltpu.roll(x, W, 1))


def up(x):
    return jnp.where(columns() >= H * W - W, 0.0, pltpu.roll(x, H * W - W, 1))


def dot(a, b):
    return jnp.dot(a, b, preferred_element_type=F32)


def conv(taps, high, low):
    first = dot(taps, high)
    z = first[:192] + first[192:] + dot(taps[:192], low)
    return z[C : 2 * C] + down(z[:C]) + up(z[2 * C :])


def silu_slope(preact):
    gate = 1.0 / (1.0 + jnp.exp(-preact))
    return gate * (1.0 + preact * (1.0 - gate))


def prepare_body(s_ref, f_ref, forward_ref, mine_ref, yours_ref, back):
    for b in range(3):
        rows = slice(b * C, b * C + C)
        low_rows = slice(192 + b * C, 192 + b * C + C)
        taps = [f_ref[0, a * 9 + b * 3 + cc] for a in range(3) for cc in range(3)]
        high, low = split(jnp.concatenate(taps, axis=1))
        forward_ref[rows] = high
        forward_ref[low_rows] = low
        taps = [f_ref[0, (2 - a) * 9 + (2 - b) * 3 + 2 - cc] for a in range(3) for cc in range(3)]
        back[rows] = jnp.concatenate(taps, axis=0).T
    c = s_ref[1]
    mine_ref[...] = back[pl.ds(pl.multiple_of(c * 96, 32), 96)]
    yours_ref[...] = back[pl.ds(pl.multiple_of((1 - c) * 96, 32), 96)]


def slope_body(ks, s_ref, act_ref, inner_ref, outer_ref, taps_ref, *refs):
    c = s_ref[1]
    for i, k in enumerate(ks):
        m = s_ref[0] ^ k
        out, vh_ref, vl_ref = refs[3 * i : 3 * i + 3]
        for e in range(4):
            if e == 0:
                x = jnp.where(c == 0, outer_ref[m], inner_ref[m])
            elif e == 3:
                x = jnp.where(c == 0, inner_ref[m], outer_ref[m])
            else:
                x = act_ref[m, e - 1]
            high, low = split(across(x))
            vh_ref[e] = high
            vl_ref[e] = low
        for d in range(2):
            z = conv(taps_ref[...], vh_ref[d : d + 3].reshape(576, 256), vl_ref[d : d + 3].reshape(576, 256))
            out[d] = silu_slope(z)


def chosen(index, refs, *at):
    out = refs[0][at]
    for k in range(1, len(refs)):
        out = jnp.where(index == k, refs[k][at], out)
    return out


def ends(c, planes, face_at, inner_ref, outer_ref):
    for d in range(2):
        inner_ref[d] = planes[d]
        outer_ref[d] = planes[d]
    first, last = face_at(0), face_at(1)
    inner_ref[2] = jnp.where(c == 0, last, first)
    outer_ref[2] = jnp.where(c == 0, first, last)


def pick_body(s_ref, d0, d1, d2, d3, cot_ref, s3_ref, inner_ref, outer_ref):
    m = s_ref[0]
    refs = (d0, d1, d2, d3)
    top = [cot_ref[m, d] * chosen(m ^ 3, refs, d) for d in range(2)]
    for d in range(2):
        s3_ref[d] = top[d]
    ends(s_ref[1], top, lambda d: chosen(m ^ 2, refs, d), inner_ref, outer_ref)


def taps_body(s_ref, mine_ref, yours_ref, one_ref, three_ref, far0_ref, far1_ref, other_ref, out_ref):
    s = s_ref[0]
    c = s_ref[1]

    def put(layer, row, x):
        high, low = split(x)
        size = x.shape[0]
        out_ref[layer, pl.ds(row, size)] = high
        out_ref[layer, pl.ds(192 + row, size)] = low

    mine = pl.multiple_of(c * 96, 32)
    yours = pl.multiple_of((1 - c) * 96, 32)
    put(s, mine, mine_ref[...])
    put(s, yours, yours_ref[...])
    put(s ^ 1, mine, one_ref[...])
    put(s ^ 3, mine, three_ref[...])
    put(s ^ 2, mine, jnp.concatenate([far0_ref[...], far1_ref[...]], axis=0))
    put(s ^ 1, yours, other_ref[0:96])
    put(s ^ 3, yours, other_ref[96:192])
    put(s ^ 2, yours, other_ref[192:288])


def upper(layer, s_ref, inner_ref, outer_ref, factors, mid_ref, taps_ref, ig_ref, vh, vl, wh, wl):
    m = s_ref[0]
    c = s_ref[1]

    def left(e):
        return jnp.where(c == 0, outer_ref[e], inner_ref[e])

    def right(e):
        return jnp.where(c == 0, inner_ref[e], outer_ref[e])

    for e in range(6):
        x = left(e) if e < 2 else (mid_ref[e - 2] if e < 4 else right(e - 4))
        high, low = split(across(x))
        vh[e] = high
        vl[e] = low
    slopes = []
    for d in range(4):
        g = conv(taps_ref[layer], vh[d : d + 3].reshape(576, 256), vl[d : d + 3].reshape(576, 256))
        if d == 0:
            factor = left(2)
        elif d == 3:
            factor = right(2)
        else:
            factor = chosen(m ^ (layer - 1), factors, d - 1)
        slope = g * factor
        if 0 < d < 3:
            ig_ref[d - 1] = g
            slopes.append(slope)
        high, low = split(across(slope))
        wh[d] = high
        wl[d] = low
    return slopes


def lower(layer, taps_ref, wh, wl):
    return [conv(taps_ref[layer], wh[d : d + 3].reshape(576, 256), wl[d : d + 3].reshape(576, 256)) for d in range(2)]


def top_body(s_ref, inner_in, outer_in, d0, d1, d2, d3, s3_ref, taps_ref, *refs):
    ig3, s2, ig2, s1, inner_ref, outer_ref, vh, vl, wh, wl = refs
    m = s_ref[0]
    factors = (d0, d1, d2, d3)
    for d, x in enumerate(upper(3, s_ref, inner_in, outer_in, factors, s3_ref, taps_ref, ig3, vh, vl, wh, wl)):
        s2[d] = x
    grads = lower(2, taps_ref, wh, wl)
    slopes = [grads[d] * chosen(m ^ 1, factors, d) for d in range(2)]
    for d in range(2):
        ig2[d] = grads[d]
        s1[d] = slopes[d]
    ends(s_ref[1], slopes, lambda d: chosen(m, factors, d), inner_ref, outer_ref)


def low_body(s_ref, inner_in, outer_in, d0, d1, d2, d3, s3, s2, s1, taps_ref, *refs):
    o, ig1, wh, wl, s0, vh, vl = refs[:4], *refs[4:]
    m = s_ref[0]
    for d, x in enumerate(upper(1, s_ref, inner_in, outer_in, (d0, d1, d2, d3), s1, taps_ref, ig1, vh, vl, wh, wl)):
        s0[d] = x
    for d in range(2):
        for k in range(N):
            o[k][d] = chosen(m ^ k, (s0, s1, s2, s3), d)


def last_body(s_ref, wh, wl, ig3, ig2, ig1, taps_ref, p0, p1, p2, p3, ig0):
    m = s_ref[0]
    for d, g in enumerate(lower(0, taps_ref, wh, wl)):
        ig0[d] = g
    for d in range(2):
        for k, p in enumerate((p0, p1, p2, p3)):
            p[d] = chosen(m ^ k, (ig0, ig1, ig2, ig3), d)


def filter_term(ref, vh_ref, vl_ref):
    nt = (((1,), (1,)), ((), ()))
    total = None
    for d in range(2):
        x = ref[d]
        high, low = split(jnp.concatenate([up(x), x, down(x)], axis=0))
        right_high = vh_ref[d : d + 3].reshape(576, 256)
        right_low = vl_ref[d : d + 3].reshape(576, 256)
        first = lax.dot_general(jnp.concatenate([high, low], axis=0), right_high, nt, preferred_element_type=F32)
        z = first[:192] + first[192:] + lax.dot_general(high, right_low, nt, preferred_element_type=F32)
        total = z if total is None else total + z
    return total


def filter_body(s_ref, *refs):
    keep_ref, send_ref, acc = refs[12:]
    c = s_ref[1]
    for k in range(N):
        term = filter_term(*refs[3 * k : 3 * k + 3])
        acc[...] = term if k == 0 else acc[...] + term

    def piece(row, size):
        if row < 768:
            j = row // 192
            return acc[row - j * 192 : row - j * 192 + size, j * 128 : (j + 1) * 128]
        r = row - 768
        return jnp.concatenate([acc[r : r + size, 512:576], acc[r + 96 : r + 96 + size, 512:576]], axis=1)

    for half in range(2):

        def fill(ref):
            row = 432 * half
            stop = row + 432
            while row < stop:
                size = min((row // 192 + 1) * 192 if row < 768 else 864, stop) - row
                ref[row - 432 * half : row - 432 * half + size] = piece(row, size)
                row += size
            ref[432:512] = jnp.zeros((80, 128), F32)

        @pl.when(c == half)
        def _():
            fill(keep_ref)

        @pl.when(c != half)
        def _():
            fill(send_ref)


def finish_body(s_ref, own_ref, other_ref, out_ref, full):
    c = s_ref[1]
    full[pl.ds(pl.multiple_of(c * 432, 8), 432)] = own_ref[0:432]
    full[pl.ds(pl.multiple_of((1 - c) * 432, 8), 432)] = other_ref[0:432]
    for a in range(3):
        for b in range(3):
            for cc in range(3):
                block = a * 3 + cc
                if block < 8:
                    x = full[(block // 2) * 192 + b * C : (block // 2) * 192 + b * C + C]
                    x = x[:, (block % 2) * C : (block % 2) * C + C]
                    out_ref[0, a * 9 + b * 3 + cc] = x
                else:
                    for part in range(2):
                        row = b * C + part * 32
                        side = 0 if row < 96 else 1
                        x = full[768 + row - 96 * side : 768 + row - 96 * side + 32, side * C : side * C + C]
                        out_ref[0, a * 9 + b * 3 + cc, part * 32 : part * 32 + 32] = x


def gather_body(s_ref, x0, x1, x2, x3, out_ref):
    s = s_ref[0]
    for k, ref in enumerate((x0, x1, x2, x3)):
        out_ref[0, s ^ k] = ref[...]


def met(x, k):
    return lax.ppermute(x, "section", [(i, i ^ k) for i in range(N)])


def handed(parts):
    return [parts[0]] + [met(parts[k], k) for k in (1, 2, 3)]


def swapped(x):
    return lax.ppermute(x, CORE, [(0, 1), (1, 0)])


def neighbours(inner, outer):
    count = lax.axis_size(DEPTH)
    inner = swapped(inner)
    pairs = [(i, i + 1) for i in range(1, count - 1, 2)]
    outer = lax.ppermute(outer, DEPTH, pairs + [(j, i) for i, j in pairs])
    return inner, outer


def window(activations, filters, cotangent):
    s = lax.axis_index("section")
    c = lax.axis_index(CORE)
    place = jnp.stack([s, c]).astype(jnp.int32)
    act = activations[0]
    plane = (C, H * W)
    two = ((2, *plane), F32)
    three = ((3, *plane), F32)

    inner = lax.dynamic_index_in_dim(act, 1 - c, 1, keepdims=False)
    outer = lax.dynamic_index_in_dim(act, c, 1, keepdims=False)
    inner, outer = neighbours(inner, outer)
    forward, mine, yours = run(
        prepare_body,
        (place, filters),
        [((384, 576), BF16), ((96, 576), F32), ((96, 576), F32)],
        [((192, 576), F32)],
        flops=10**6,
    )
    factors, shifted = [None] * N, [None] * N
    for ks in ((2,), (1, 3), (0,)):
        out = run(
            functools.partial(slope_body, ks),
            (place, act, inner, outer, forward),
            [two, ((4, 192, 256), BF16), ((4, 192, 256), BF16)] * len(ks),
            flops=2 * 2 * 192 * 576 * 256 * 3 * len(ks),
        )
        for i, k in enumerate(ks):
            factors[k], *shifted[k] = out[3 * i : 3 * i + 3]
    factors = handed(factors)

    one = met(mine, 1)
    three_half = met(mine, 3)
    far0 = met(three_half[:48], 1)
    far1 = met(one[48:], 3)
    other = swapped(jnp.concatenate([one, three_half, far0, far1], axis=0))
    (taps,) = run(
        taps_body, (place, mine, yours, one, three_half, far0, far1, other), [((N, 384, 576), BF16)], flops=10**6
    )

    s3, inner, outer = run(pick_body, (place, *factors, cotangent), [two, three, three], flops=10**6)
    inner, outer = neighbours(inner, outer)
    scratch = [((6, 192, 256), BF16)] * 2 + [((4, 192, 256), BF16)] * 2
    ig3, s2, ig2, s1, inner, outer = run(
        top_body,
        (place, inner, outer, *factors, s3, taps),
        [two, two, two, two, three, three],
        scratch,
        flops=2 * 6 * 192 * 576 * 256 * 3,
    )
    inner, outer = neighbours(inner, outer)
    *packed, ig1, wh, wl = run(
        low_body,
        (place, inner, outer, *factors, s3, s2, s1, taps),
        [two] * 5 + [((4, 192, 256), BF16)] * 2,
        [((2, *plane), F32)] + scratch[:2],
        flops=2 * 4 * 192 * 576 * 256 * 3,
    )
    slopes = handed(packed)
    packed = run(
        last_body,
        (place, wh, wl, ig3, ig2, ig1, taps),
        [two] * 4,
        [((2, *plane), F32)],
        flops=2 * 2 * 192 * 576 * 256 * 3,
    )
    grads = handed(packed)

    keep, send = run(
        filter_body,
        (place, *(x for k in range(N) for x in (slopes[k], *shifted[k]))),
        [((512, 128), F32)] * 2,
        [((192, 576), F32)],
        flops=2 * 8 * 192 * 576 * 256 * 3,
    )
    part = (keep + swapped(send)).reshape(32, 16, 128)
    part = lax.all_to_all(part, PLANE, 0, 0, tiled=True)
    scaling = 1.0 / math.sqrt(N * 2 * lax.axis_size(DEPTH) * H * W)
    total = jnp.sum(part, axis=0) * scaling
    part = lax.all_to_all(jnp.broadcast_to(total[None], (32, 16, 128)), PLANE, 0, 0, tiled=True).reshape(512, 128)
    other_part = swapped(part)
    (filter_grads,) = run(
        finish_body, (place, part, other_part), [((1, 27, C, C), F32)], [((864, 128), F32)], flops=10**6
    )
    (input_grads,) = run(gather_body, (place, *grads), [((1, N, 2, *plane), F32)], flops=10**6)
    return input_grads, filter_grads


def solution(mesh):
    finer = Mesh(
        mesh.devices.reshape(mesh.shape["section"], 8, 4, 2),
        ("section", "depth_0", "depth_1", "depth_2"),
    )
    placed = (
        P("section", None, DEPTH, None, None),
        P("section", None, None, None),
        P(None, DEPTH, None, None),
    )
    return jax.shard_map(
        window,
        mesh=finer,
        in_specs=placed,
        out_specs=(P("section", None, DEPTH, None, None), P("section", None, None, None)),
        check_vma=False,
    )
```

time: 138 us -> 135 us (0.978)
  the two profiles are of different devices: /device:TPU:2 before, /device:TPU:1 now
where the time goes in v1:
time: 135 us; the launch traced here: 134 us
  blocking collectives  45.7 us (34%)
  starting transfers between devices  36.5 us (27%)
  waiting for transfers between devices  29.9 us (22%)
  Pallas kernels  18.9 us (14%)
  local copies, waits for them, and re-layouts  2.33 us (2%)
    all_to_all x1, blocking collectives, window(): part = lax.all_to_all(part, PLANE, 0, 0, tiled=True)  30.7 us
    ppermute x13, waiting for transfers between devices, met(): return lax.ppermute(x, 'section', [(i, i ^ k) for i in range(N)])  19.3 us
    pallas_call x12, Pallas kernels, run(): pl.pallas_call(body, out_shape=[jax.ShapeDtypeStruct(s, t) for s, t in ou...  18.9 us
    ppermute x13, starting transfers between devices, met(): return lax.ppermute(x, 'section', [(i, i ^ k) for i in range(N)])  17.8 us
    all_to_all x1, blocking collectives, window(): lax.all_to_all(jnp.broadcast_to(total[None], (32, 16, 128)), PLANE, 0, 0,...  15.1 us
    ppermute x3, starting transfers between devices, neighbours(): outer = lax.ppermute(outer, DEPTH, pairs + [(j, i) for i, j in pairs])  14.4 us
    ppermute x3, waiting for transfers between devices, neighbours(): outer = lax.ppermute(outer, DEPTH, pairs + [(j, i) for i, j in pairs])  9.02 us
    ppermute x6, starting transfers between devices, swapped(): return lax.ppermute(x, CORE, [(0, 1), (1, 0)])  4.36 us
  transfers between devices with their start and end apart: 22, of which 13 were waited for; matrix products, arithmetic and copies ran while one was open for 1% of the time, Pallas kernels for 7%

profile of v1, /device:TPU:1, one launch (start us, length us, event | category | flops | bytes accessed | tf_op | source)
XLA Modules:
  0.0 134.4 jit_solution(1494097958872114445)
XLA Ops:
  0.6 0.0 copy-start
  0.6 0.1 pad_add_fusion.s_ref
  0.7 1.2 copy-done.1
  1.9 1.0 shard_map.50
  2.9 3.4 %collective-permute-start.8 = (f32[96,576]{1,0:T(8,128)S(1)}, f32[96,576]{1,0:T(8,128)S(1)}, u32[]{:S(2)}, u32[]{:S(2)}) collective-permute-start(f32[96,576]{1,0:T(8,128)S(1)} %get-tuple-element.47.mine_ref), channel_id=1, source_target_pairs={{0,192},{64,128},{128,64},{192,0},{1,193},{65,129},{129,65},{193,1... | collective-permute-start | bytes 663560 | tf_op jit(solution)/shard_map/ppermute | solution.py:307
  6.3 0.0 collective-permute-start.7
  6.3 4.6 %collective-permute-done.8.three_ref = f32[96,576]{1,0:T(8,128)S(1)} collective-permute-done((f32[96,576]{1,0:T(8,128)S(1)}, f32[96,576]{1,0:T(8,128)S(1)}, u32[]{:S(2)}, u32[]{:S(2)}) %collective-permute-start.8) | collective-permute-done | bytes 221216 | tf_op jit(solution)/shard_map/ppermute | solution.py:307
  11.0 1.0 collective-permute-start.9
  12.0 0.9 collective-permute-done.7.one_ref
  12.9 1.7 %collective-permute-start.10 = (f32[48,576]{1,0:T(8,128)S(1)}, f32[48,576]{1,0:T(8,128)S(1)}, u32[]{:S(2)}, u32[]{:S(2)}) collective-permute-start(f32[48,576]{1,0:T(8,128)S(1)} %slice.9), channel_id=1, source_target_pairs={{0,192},{64,128},{128,64},{192,0},{1,193},{65,129},{129,65},{193,1... | collective-permute-start | bytes 331784 | tf_op jit(solution)/shard_map/ppermute | solution.py:307
  14.6 1.1 dynamic-slice_bitcast_fusion
  15.7 4.9 %collective-permute-start.1 = (f32[4,64,256]{2,1,0:T(8,128)S(1)}, f32[4,64,256]{2,1,0:T(8,128)S(1)}, u32[]{:S(2)}, u32[]{:S(2)}) collective-permute-start(f32[4,64,256]{2,1,0:T(8,128)S(1)} %get-tuple-element.76), channel_id=1, source_target_pairs={{1,2},{3,4},{5,6},{7,8},{9,10},{11,12},{13,14},{15,16},{17,18},{19... | collective-permute-start | bytes 786440 | tf_op jit(solution)/shard_map/ppermute | solution.py:322
  20.6 0.1 collective-permute-start
  20.7 0.0 collective-permute-done.9.far0_ref
  20.7 0.0 collective-permute-done.10.far1_ref
  20.7 0.1 pad_maximum_fusion
  20.8 0.8 collective-permute-start.11
  21.5 3.1 %collective-permute-done.1.outer_ref = f32[4,64,256]{2,1,0:T(8,128)S(1)} collective-permute-done((f32[4,64,256]{2,1,0:T(8,128)S(1)}, f32[4,64,256]{2,1,0:T(8,128)S(1)}, u32[]{:S(2)}, u32[]{:S(2)}) %collective-permute-start.1) | collective-permute-done | bytes 262176 | tf_op jit(solution)/shard_map/ppermute | solution.py:322
  24.6 0.0 collective-permute-done.inner_ref
  24.6 1.4 %shard_map.53 = (f32[2,64,256]{2,1,0:T(8,128)S(1)}, bf16[4,192,256]{2,1,0:T(8,128)(2,1)S(1)}, bf16[4,192,256]{2,1,0:T(8,128)(2,1)S(1)}) custom-call(s32[2]{0:T(128)S(1)} %pad_add_fusion.s_ref, f32[4,2,64,256]{3,2,1,0:T(8,128)S(1)} %bitcast.9, f32[4,64,256]{2,1,0:T(8,128)S(1)} %collective-permute-done.inner_ref, ...), custom_call_target="tpu_custom_call" | custom-call | flops 339738624 | bytes 1490952 | tf_op jit(solution)/shard_map/pallas_call | solution.py:29
  26.0 0.0 copy-start.2
  26.1 1.3 collective-permute-start.3
  27.3 1.9 %shard_map.52 = (f32[2,64,256]{2,1,0:T(8,128)S(1)}, bf16[4,192,256]{2,1,0:T(8,128)(2,1)S(1)}, bf16[4,192,256]{2,1,0:T(8,128)(2,1)S(1)}, f32[2,64,256]{2,1,0:T(8,...) custom-call(s32[2]{0:T(128)S(1)} %pad_add_fusion.s_ref, f32[4,2,64,256]{3,2,1,0:T(8,128)S(1)} %bitcast.10, ...), custom_call_target="tpu_custom_call" | custom-call | flops 679477248 | bytes 1490952 | tf_op jit(solution)/shard_map/pallas_call | solution.py:29
  29.2 0.8 collective-permute-start.2
  30.0 1.7 %collective-permute-start.4 = (f32[2,64,256]{2,1,0:T(8,128)S(1)}, f32[2,64,256]{2,1,0:T(8,128)S(1)}, u32[]{:S(2)}, u32[]{:S(2)}) collective-permute-start(f32[2,64,256]{2,1,0:T(8,128)S(1)} %get-tuple-element.43), channel_id=1, source_target_pairs={{0,192},{64,128},{128,64},{192,0},{1,193},{65,129},{129,65},{193,1... | collective-permute-start | bytes 393224 | tf_op jit(solution)/shard_map/ppermute | solution.py:307
  31.7 1.4 %shard_map.51 = (f32[2,64,256]{2,1,0:T(8,128)S(1)}, bf16[4,192,256]{2,1,0:T(8,128)(2,1)S(1)}, bf16[4,192,256]{2,1,0:T(8,128)(2,1)S(1)}) custom-call(s32[2]{0:T(128)S(1)} %pad_add_fusion.s_ref, f32[4,2,64,256]{3,2,1,0:T(8,128)S(1)} %bitcast.11, f32[4,64,256]{2,1,0:T(8,128)S(1)} %collective-permute-done.inner_ref, ...), custom_call_target="tpu_custom_call" | custom-call | flops 339738624 | bytes 1490952 | tf_op jit(solution)/shard_map/pallas_call | solution.py:29
  33.1 0.0 collective-permute-done.3.d2
  33.1 0.4 collective-permute-done.2.d1
  33.5 1.7 %collective-permute-done.4.d3 = f32[2,64,256]{2,1,0:T(8,128)S(1)} collective-permute-done((f32[2,64,256]{2,1,0:T(8,128)S(1)}, f32[2,64,256]{2,1,0:T(8,128)S(1)}, u32[]{:S(2)}, u32[]{:S(2)}) %collective-permute-start.4) | collective-permute-done | bytes 131104 | tf_op jit(solution)/shard_map/ppermute | solution.py:307
  35.2 0.6 shard_map.54
  35.8 0.1 collective-permute-start.5
  35.9 5.2 %collective-permute-start.6 = (f32[3,64,256]{2,1,0:T(8,128)S(1)}, f32[3,64,256]{2,1,0:T(8,128)S(1)}, u32[]{:S(2)}, u32[]{:S(2)}) collective-permute-start(f32[3,64,256]{2,1,0:T(8,128)S(1)} %get-tuple-element.45), channel_id=1, source_target_pairs={{1,2},{3,4},{5,6},{7,8},{9,10},{11,12},{13,14},{15,16},{17,18},{19... | collective-permute-start | bytes 589832 | tf_op jit(solution)/shard_map/ppermute | solution.py:322
  41.1 0.0 collective-permute-done.11.other_ref
  41.1 0.8 shard_map.55.taps_ref
  42.0 0.0 collective-permute-done.5.inner_in
  42.0 2.5 %collective-permute-done.6.outer_in = f32[3,64,256]{2,1,0:T(8,128)S(1)} collective-permute-done((f32[3,64,256]{2,1,0:T(8,128)S(1)}, f32[3,64,256]{2,1,0:T(8,128)S(1)}, u32[]{:S(2)}, u32[]{:S(2)}) %collective-permute-start.6) | collective-permute-done | bytes 196640 | tf_op jit(solution)/shard_map/ppermute | solution.py:322
  44.5 2.6 %shard_map.56 = (f32[2,64,256]{2,1,0:T(8,128)S(1)}, f32[2,64,256]{2,1,0:T(8,128)S(1)}, f32[2,64,256]{2,1,0:T(8,128)S(1)}, f32[2,64,256]{2,1,0:T(8,128)S(1)}, f32...) custom-call(s32[2]{0:T(128)S(1)} %pad_add_fusion.s_ref, f32[3,64,256]{2,1,0:T(8,128)S(1)} %collective-permute-done.5.inner_in, ...), custom_call_target="tpu_custom_call" | custom-call | flops 1019215872 | bytes 2818056 | tf_op jit(solution)/shard_map/pallas_call | solution.py:29
  47.0 0.1 collective-permute-start.12
  47.1 4.3 %collective-permute-start.13 = (f32[3,64,256]{2,1,0:T(8,128)S(1)}, f32[3,64,256]{2,1,0:T(8,128)S(1)}, u32[]{:S(2)}, u32[]{:S(2)}) collective-permute-start(f32[3,64,256]{2,1,0:T(8,128)S(1)} %get-tuple-element.50), channel_id=1, source_target_pairs={{1,2},{3,4},{5,6},{7,8},{9,10},{11,12},{13,14},{15,16},{17,18},{19... | collective-permute-start | bytes 589832 | tf_op jit(solution)/shard_map/ppermute | solution.py:322
  51.4 0.0 collective-permute-done.12.inner_in
  51.4 3.4 %collective-permute-done.13.outer_in = f32[3,64,256]{2,1,0:T(8,128)S(1)} collective-permute-done((f32[3,64,256]{2,1,0:T(8,128)S(1)}, f32[3,64,256]{2,1,0:T(8,128)S(1)}, u32[]{:S(2)}, u32[]{:S(2)}) %collective-permute-start.13) | collective-permute-done | bytes 196640 | tf_op jit(solution)/shard_map/ppermute | solution.py:322
  54.9 2.0 %shard_map.57 = (f32[2,64,256]{2,1,0:T(8,128)S(1)}, f32[2,64,256]{2,1,0:T(8,128)S(1)}, f32[2,64,256]{2,1,0:T(8,128)S(1)}, f32[2,64,256]{2,1,0:T(8,128)S(1)}, f32...) custom-call(s32[2]{0:T(128)S(1)} %pad_add_fusion.s_ref, ...), custom_call_target="tpu_custom_call" | custom-call | flops 679477248 | bytes 3080200 | tf_op jit(solution)/shard_map/pallas_call | solution.py:29
  56.9 0.6 collective-permute-start.17
  57.5 2.4 %collective-permute-start.18 = (f32[2,64,256]{2,1,0:T(8,128)S(1)}, f32[2,64,256]{2,1,0:T(8,128)S(1)}, u32[]{:S(2)}, u32[]{:S(2)}) collective-permute-start(f32[2,64,256]{2,1,0:T(8,128)S(1)} %get-tuple-element.68), channel_id=1, source_target_pairs={{0,128},{64,192},{128,0},{192,64},{1,129},{65,193},{129,1},{193,65... | collective-permute-start | bytes 393224 | tf_op jit(solution)/shard_map/ppermute | solution.py:307
  59.8 1.0 collective-permute-start.19
  60.8 0.0 collective-permute-done.17.refs_3_
  60.8 2.8 %collective-permute-done.18.refs_6_ = f32[2,64,256]{2,1,0:T(8,128)S(1)} collective-permute-done((f32[2,64,256]{2,1,0:T(8,128)S(1)}, f32[2,64,256]{2,1,0:T(8,128)S(1)}, u32[]{:S(2)}, u32[]{:S(2)}) %collective-permute-start.18) | collective-permute-done | bytes 131104 | tf_op jit(solution)/shard_map/ppermute | solution.py:307
  63.6 1.4 %collective-permute-done.19.refs_9_ = f32[2,64,256]{2,1,0:T(8,128)S(1)} collective-permute-done((f32[2,64,256]{2,1,0:T(8,128)S(1)}, f32[2,64,256]{2,1,0:T(8,128)S(1)}, u32[]{:S(2)}, u32[]{:S(2)}) %collective-permute-start.19) | collective-permute-done | bytes 131104 | tf_op jit(solution)/shard_map/ppermute | solution.py:307
  65.0 2.9 %shard_map.60 = (f32[512,128]{1,0:T(8,128)S(1)}, f32[512,128]{1,0:T(8,128)S(1)}) custom-call(s32[2]{0:T(128)S(1)} %pad_add_fusion.s_ref, f32[2,64,256]{2,1,0:T(8,128)S(1)} %get-tuple-element.62.refs_0_, bf16[4,192,256]{2,1,0:T(8,128)(2,1)S(1)} %get-tuple-element.63.refs_1_, bf16[4,192,256]{2,1,0:T(8,128)(2,1)S(1)} %get-tuple-element.64.refs_2_, ...), custom_call_target="tpu_custom_call" | custom-call | flops 1358954496 | bytes 3670024 | tf_op jit(solution)/shard_map/pallas_call | solution.py:29
  67.9 0.1 collective-permute-start.20
  68.0 1.5 %collective-permute-done.20 = f32[512,128]{1,0:T(8,128)S(1)} collective-permute-done((f32[512,128]{1,0:T(8,128)S(1)}, f32[512,128]{1,0:T(8,128)S(1)}, u32[]{:S(2)}, u32[]{:S(2)}) %collective-permute-start.20) | collective-permute-done | bytes 262176 | tf_op jit(solution)/shard_map/ppermute | solution.py:315
  69.6 30.7 %all_to_all.10 = f32[32,16,128]{2,1,0:T(8,128)S(1)} all-to-all(f32[32,16,128]{2,1,0:T(8,128)S(1)} %bitcast.14), channel_id=1, replica_groups=mesh['section'=4,'depth_0'=8,'depth_1'=4,'depth_2'=2] {'depth_0','depth_1'}, dimensions={0} | all-to-all | bytes 524288 | tf_op jit(solution)/shard_map/all_to_all | solution.py:402
  100.3 15.1 %all_to_all.11 = f32[32,16,128]{2,1,0:T(8,128)S(1)} all-to-all(f32[32,16,128]{2,1,0:T(8,128)S(1)} %broadcast_in_dim.2), channel_id=1, replica_groups=mesh['section'=4,'depth_0'=8,'depth_1'=4,'depth_2'=2] {'depth_0','depth_1'}, dimensions={0} | all-to-all | bytes 524288 | tf_op jit(solution)/shard_map/all_to_all | solution.py:405
  115.4 3.2 %collective-permute-start.21 = (f32[512,128]{1,0:T(8,128)S(1)}, f32[512,128]{1,0:T(8,128)S(1)}, u32[]{:S(2)}, u32[]{:S(2)}) collective-permute-start(f32[512,128]{1,0:T(8,128)S(1)} %bitcast.12), channel_id=1, source_target_pairs={{0,1},{1,0},{2,3},{3,2},{4,5},{5,4},{6,7},{7,6},{8,9},{9,8},{10,11... | collective-permute-start | bytes 786440 | tf_op jit(solution)/shard_map/ppermute | solution.py:315
  118.6 1.3 shard_map.58
  119.9 0.1 collective-permute-start.14
  120.0 2.4 %collective-permute-start.15 = (f32[2,64,256]{2,1,0:T(8,128)S(1)}, f32[2,64,256]{2,1,0:T(8,128)S(1)}, u32[]{:S(2)}, u32[]{:S(2)}) collective-permute-start(f32[2,64,256]{2,1,0:T(8,128)S(1)} %get-tuple-element.60), channel_id=1, source_target_pairs={{0,128},{64,192},{128,0},{192,64},{1,129},{65,193},{129,1},{193,65... | collective-permute-start | bytes 393224 | tf_op jit(solution)/shard_map/ppermute | solution.py:307
  122.4 1.4 %collective-permute-start.16 = (f32[2,64,256]{2,1,0:T(8,128)S(1)}, f32[2,64,256]{2,1,0:T(8,128)S(1)}, u32[]{:S(2)}, u32[]{:S(2)}) collective-permute-start(f32[2,64,256]{2,1,0:T(8,128)S(1)} %get-tuple-element.61), channel_id=1, source_target_pairs={{0,192},{64,128},{128,64},{192,0},{1,193},{65,129},{129,65},{193,1... | collective-permute-start | bytes 393224 | tf_op jit(solution)/shard_map/ppermute | solution.py:307
  123.8 1.2 collective-permute-done.14.x1
  125.0 3.8 %collective-permute-done.15.x2 = f32[2,64,256]{2,1,0:T(8,128)S(1)} collective-permute-done((f32[2,64,256]{2,1,0:T(8,128)S(1)}, f32[2,64,256]{2,1,0:T(8,128)S(1)}, u32[]{:S(2)}, u32[]{:S(2)}) %collective-permute-start.15) | collective-permute-done | bytes 131104 | tf_op jit(solution)/shard_map/ppermute | solution.py:307
  128.9 2.5 %collective-permute-done.16.x3 = f32[2,64,256]{2,1,0:T(8,128)S(1)} collective-permute-done((f32[2,64,256]{2,1,0:T(8,128)S(1)}, f32[2,64,256]{2,1,0:T(8,128)S(1)}, u32[]{:S(2)}, u32[]{:S(2)}) %collective-permute-start.16) | collective-permute-done | bytes 131104 | tf_op jit(solution)/shard_map/ppermute | solution.py:307
  131.4 1.4 %shard_map.59 = f32[1,4,2,64,256]{4,3,2,1,0:T(8,128)} custom-call(s32[2]{0:T(128)S(1)} %pad_add_fusion.s_ref, f32[2,64,256]{2,1,0:T(8,128)S(1)} %get-tuple-element.58.x0, f32[2,64,256]{2,1,0:T(8,128)S(1)} %collective-permute-done.14.x1, f32[2,64,256]{2,1,0:T(8,128)S(1)} %collective-permute-done.15.x2, f32[2,64,256]{2,1,0:T(8,128)S(1)} %collective-permute-done.16.x3), custom_call_target="tpu_custom_call" | custom-call | flops 1000000 | bytes 524296 | tf_op jit(solution)/shard_map/pallas_call | solution.py:29
  132.8 0.0 collective-permute-done.21.other_ref
  132.8 1.7 %shard_map.61 = f32[1,27,64,64]{3,2,1,0:T(8,128)} custom-call(s32[2]{0:T(128)S(1)} %pad_add_fusion.s_ref, f32[512,128]{1,0:T(8,128)S(1)} %bitcast.13, f32[512,128]{1,0:T(8,128)S(1)} %collective-permute-done.21.other_ref), custom_call_target="tpu_custom_call" | custom-call | flops 1000000 | bytes 524296 | tf_op jit(solution)/shard_map/pallas_call | solution.py:29
  (9 shorter events, 0.1 us)
Async XLA Ops:
  0.6 24.0 %copy-start = (f32[1,4,2,64,256]{4,3,2,1,0:T(8,128)S(1)}, f32[1,4,2,64,256]{4,3,2,1,0:T(8,128)}, u32[]{:S(2)}) copy-start(f32[1,4,2,64,256]{4,3,2,1,0:T(8,128)} %param.3) | copy-start | bytes 1572868
  0.7 1.2 copy-start.1
  2.9 8.0 %collective-permute-start.8 = (f32[96,576]{1,0:T(8,128)S(1)}, f32[96,576]{1,0:T(8,128)S(1)}, u32[]{:S(2)}, u32[]{:S(2)}) collective-permute-start(f32[96,576]{1,0:T(8,128)S(1)} %get-tuple-element.47.mine_ref), channel_id=1, source_target_pairs={{0,192},{64,128},{128,64},{192,0},{1,193},{65,129},{129,65},{193,1... | collective-permute-start | bytes 663560 | tf_op jit(solution)/shard_map/ppermute | solution.py:307
  6.3 6.6 %collective-permute-start.7 = (f32[96,576]{1,0:T(8,128)S(1)}, f32[96,576]{1,0:T(8,128)S(1)}, u32[]{:S(2)}, u32[]{:S(2)}) collective-permute-start(f32[96,576]{1,0:T(8,128)S(1)} %get-tuple-element.47.mine_ref), channel_id=1, source_target_pairs={{0,64},{64,0},{128,192},{192,128},{1,65},{65,1},{129,193},{193,129... | collective-permute-start | bytes 663560 | tf_op jit(solution)/shard_map/ppermute | solution.py:307
  11.0 9.7 %collective-permute-start.9 = (f32[48,576]{1,0:T(8,128)S(1)}, f32[48,576]{1,0:T(8,128)S(1)}, u32[]{:S(2)}, u32[]{:S(2)}) collective-permute-start(f32[48,576]{1,0:T(8,128)S(1)} %slice.8), channel_id=1, source_target_pairs={{0,64},{64,0},{128,192},{192,128},{1,65},{65,1},{129,193},{193,129... | collective-permute-start | bytes 331784 | tf_op jit(solution)/shard_map/ppermute | solution.py:307
  12.9 7.8 %collective-permute-start.10 = (f32[48,576]{1,0:T(8,128)S(1)}, f32[48,576]{1,0:T(8,128)S(1)}, u32[]{:S(2)}, u32[]{:S(2)}) collective-permute-start(f32[48,576]{1,0:T(8,128)S(1)} %slice.9), channel_id=1, source_target_pairs={{0,192},{64,128},{128,64},{192,0},{1,193},{65,129},{129,65},{193,1... | collective-permute-start | bytes 331784 | tf_op jit(solution)/shard_map/ppermute | solution.py:307
  15.7 8.9 %collective-permute-start.1 = (f32[4,64,256]{2,1,0:T(8,128)S(1)}, f32[4,64,256]{2,1,0:T(8,128)S(1)}, u32[]{:S(2)}, u32[]{:S(2)}) collective-permute-start(f32[4,64,256]{2,1,0:T(8,128)S(1)} %get-tuple-element.76), channel_id=1, source_target_pairs={{1,2},{3,4},{5,6},{7,8},{9,10},{11,12},{13,14},{15,16},{17,18},{19... | collective-permute-start | bytes 786440 | tf_op jit(solution)/shard_map/ppermute | solution.py:322
  20.6 4.0 %collective-permute-start = (f32[4,64,256]{2,1,0:T(8,128)S(1)}, f32[4,64,256]{2,1,0:T(8,128)S(1)}, u32[]{:S(2)}, u32[]{:S(2)}) collective-permute-start(f32[4,64,256]{2,1,0:T(8,128)S(1)} %get-tuple-element.77), channel_id=1, source_target_pairs={{0,1},{1,0},{2,3},{3,2},{4,5},{5,4},{6,7},{7,6},{8,9},{9,8},{10,11... | collective-permute-start | bytes 786440 | tf_op jit(solution)/shard_map/ppermute | solution.py:315
  20.8 20.4 %collective-permute-start.11 = (f32[288,576]{1,0:T(8,128)S(1)}, f32[288,576]{1,0:T(8,128)S(1)}, u32[]{:S(2)}, u32[]{:S(2)}) collective-permute-start(f32[288,576]{1,0:T(8,128)S(1)} %pad_maximum_fusion), channel_id=1, source_target_pairs={{0,1},{1,0},{2,3},{3,2},{4,5},{5,4},{6,7},{7,6},{8,9},{9,8},{10,11... | collective-permute-start | bytes 1990664 | tf_op jit(solution)/shard_map/ppermute | solution.py:315
  26.0 9.1 %copy-start.2 = (f32[4,2,64,256]{3,2,1,0:T(8,128)S(1)}, f32[4,2,64,256]{3,2,1,0:T(8,128)}, u32[]{:S(2)}) copy-start(f32[4,2,64,256]{3,2,1,0:T(8,128)} %cot_ref.1) | copy-start | bytes 1572868
  26.1 7.1 %collective-permute-start.3 = (f32[2,64,256]{2,1,0:T(8,128)S(1)}, f32[2,64,256]{2,1,0:T(8,128)S(1)}, u32[]{:S(2)}, u32[]{:S(2)}) collective-permute-start(f32[2,64,256]{2,1,0:T(8,128)S(1)} %get-tuple-element.42), channel_id=1, source_target_pairs={{0,128},{64,192},{128,0},{192,64},{1,129},{65,193},{129,1},{193,65... | collective-permute-start | bytes 393224 | tf_op jit(solution)/shard_map/ppermute | solution.py:307
  29.2 4.3 %collective-permute-start.2 = (f32[2,64,256]{2,1,0:T(8,128)S(1)}, f32[2,64,256]{2,1,0:T(8,128)S(1)}, u32[]{:S(2)}, u32[]{:S(2)}) collective-permute-start(f32[2,64,256]{2,1,0:T(8,128)S(1)} %get-tuple-element.41), channel_id=1, source_target_pairs={{0,64},{64,0},{128,192},{192,128},{1,65},{65,1},{129,193},{193,129... | collective-permute-start | bytes 393224 | tf_op jit(solution)/shard_map/ppermute | solution.py:307
  30.0 5.2 %collective-permute-start.4 = (f32[2,64,256]{2,1,0:T(8,128)S(1)}, f32[2,64,256]{2,1,0:T(8,128)S(1)}, u32[]{:S(2)}, u32[]{:S(2)}) collective-permute-start(f32[2,64,256]{2,1,0:T(8,128)S(1)} %get-tuple-element.43), channel_id=1, source_target_pairs={{0,192},{64,128},{128,64},{192,0},{1,193},{65,129},{129,65},{193,1... | collective-permute-start | bytes 393224 | tf_op jit(solution)/shard_map/ppermute | solution.py:307
  35.8 6.2 %collective-permute-start.5 = (f32[3,64,256]{2,1,0:T(8,128)S(1)}, f32[3,64,256]{2,1,0:T(8,128)S(1)}, u32[]{:S(2)}, u32[]{:S(2)}) collective-permute-start(f32[3,64,256]{2,1,0:T(8,128)S(1)} %get-tuple-element.44), channel_id=1, source_target_pairs={{0,1},{1,0},{2,3},{3,2},{4,5},{5,4},{6,7},{7,6},{8,9},{9,8},{10,11... | collective-permute-start | bytes 589832 | tf_op jit(solution)/shard_map/ppermute | solution.py:315
  35.9 8.6 %collective-permute-start.6 = (f32[3,64,256]{2,1,0:T(8,128)S(1)}, f32[3,64,256]{2,1,0:T(8,128)S(1)}, u32[]{:S(2)}, u32[]{:S(2)}) collective-permute-start(f32[3,64,256]{2,1,0:T(8,128)S(1)} %get-tuple-element.45), channel_id=1, source_target_pairs={{1,2},{3,4},{5,6},{7,8},{9,10},{11,12},{13,14},{15,16},{17,18},{19... | collective-permute-start | bytes 589832 | tf_op jit(solution)/shard_map/ppermute | solution.py:322
  47.0 4.4 %collective-permute-start.12 = (f32[3,64,256]{2,1,0:T(8,128)S(1)}, f32[3,64,256]{2,1,0:T(8,128)S(1)}, u32[]{:S(2)}, u32[]{:S(2)}) collective-permute-start(f32[3,64,256]{2,1,0:T(8,128)S(1)} %get-tuple-element.49), channel_id=1, source_target_pairs={{0,1},{1,0},{2,3},{3,2},{4,5},{5,4},{6,7},{7,6},{8,9},{9,8},{10,11... | collective-permute-start | bytes 589832 | tf_op jit(solution)/shard_map/ppermute | solution.py:315
  47.1 7.7 %collective-permute-start.13 = (f32[3,64,256]{2,1,0:T(8,128)S(1)}, f32[3,64,256]{2,1,0:T(8,128)S(1)}, u32[]{:S(2)}, u32[]{:S(2)}) collective-permute-start(f32[3,64,256]{2,1,0:T(8,128)S(1)} %get-tuple-element.50), channel_id=1, source_target_pairs={{1,2},{3,4},{5,6},{7,8},{9,10},{11,12},{13,14},{15,16},{17,18},{19... | collective-permute-start | bytes 589832 | tf_op jit(solution)/shard_map/ppermute | solution.py:322
  56.9 3.9 %collective-permute-start.17 = (f32[2,64,256]{2,1,0:T(8,128)S(1)}, f32[2,64,256]{2,1,0:T(8,128)S(1)}, u32[]{:S(2)}, u32[]{:S(2)}) collective-permute-start(f32[2,64,256]{2,1,0:T(8,128)S(1)} %get-tuple-element.65), channel_id=1, source_target_pairs={{0,64},{64,0},{128,192},{192,128},{1,65},{65,1},{129,193},{193,129... | collective-permute-start | bytes 393224 | tf_op jit(solution)/shard_map/ppermute | solution.py:307
  57.5 6.2 %collective-permute-start.18 = (f32[2,64,256]{2,1,0:T(8,128)S(1)}, f32[2,64,256]{2,1,0:T(8,128)S(1)}, u32[]{:S(2)}, u32[]{:S(2)}) collective-permute-start(f32[2,64,256]{2,1,0:T(8,128)S(1)} %get-tuple-element.68), channel_id=1, source_target_pairs={{0,128},{64,192},{128,0},{192,64},{1,129},{65,193},{129,1},{193,65... | collective-permute-start | bytes 393224 | tf_op jit(solution)/shard_map/ppermute | solution.py:307
  59.8 5.2 %collective-permute-start.19 = (f32[2,64,256]{2,1,0:T(8,128)S(1)}, f32[2,64,256]{2,1,0:T(8,128)S(1)}, u32[]{:S(2)}, u32[]{:S(2)}) collective-permute-start(f32[2,64,256]{2,1,0:T(8,128)S(1)} %get-tuple-element.71), channel_id=1, source_target_pairs={{0,192},{64,128},{128,64},{192,0},{1,193},{65,129},{129,65},{193,1... | collective-permute-start | bytes 393224 | tf_op jit(solution)/shard_map/ppermute | solution.py:307
  67.9 1.6 %collective-permute-start.20 = (f32[512,128]{1,0:T(8,128)S(1)}, f32[512,128]{1,0:T(8,128)S(1)}, u32[]{:S(2)}, u32[]{:S(2)}) collective-permute-start(f32[512,128]{1,0:T(8,128)S(1)} %get-tuple-element.75), channel_id=1, source_target_pairs={{0,1},{1,0},{2,3},{3,2},{4,5},{5,4},{6,7},{7,6},{8,9},{9,8},{10,11... | collective-permute-start | bytes 786440 | tf_op jit(solution)/shard_map/ppermute | solution.py:315
  115.4 17.4 %collective-permute-start.21 = (f32[512,128]{1,0:T(8,128)S(1)}, f32[512,128]{1,0:T(8,128)S(1)}, u32[]{:S(2)}, u32[]{:S(2)}) collective-permute-start(f32[512,128]{1,0:T(8,128)S(1)} %bitcast.12), channel_id=1, source_target_pairs={{0,1},{1,0},{2,3},{3,2},{4,5},{5,4},{6,7},{7,6},{8,9},{9,8},{10,11... | collective-permute-start | bytes 786440 | tf_op jit(solution)/shard_map/ppermute | solution.py:315
  119.9 5.1 %collective-permute-start.14 = (f32[2,64,256]{2,1,0:T(8,128)S(1)}, f32[2,64,256]{2,1,0:T(8,128)S(1)}, u32[]{:S(2)}, u32[]{:S(2)}) collective-permute-start(f32[2,64,256]{2,1,0:T(8,128)S(1)} %get-tuple-element.59), channel_id=1, source_target_pairs={{0,64},{64,0},{128,192},{192,128},{1,65},{65,1},{129,193},{193,129... | collective-permute-start | bytes 393224 | tf_op jit(solution)/shard_map/ppermute | solution.py:307
  120.0 8.8 %collective-permute-start.15 = (f32[2,64,256]{2,1,0:T(8,128)S(1)}, f32[2,64,256]{2,1,0:T(8,128)S(1)}, u32[]{:S(2)}, u32[]{:S(2)}) collective-permute-start(f32[2,64,256]{2,1,0:T(8,128)S(1)} %get-tuple-element.60), channel_id=1, source_target_pairs={{0,128},{64,192},{128,0},{192,64},{1,129},{65,193},{129,1},{193,65... | collective-permute-start | bytes 393224 | tf_op jit(solution)/shard_map/ppermute | solution.py:307
  122.4 9.0 %collective-permute-start.16 = (f32[2,64,256]{2,1,0:T(8,128)S(1)}, f32[2,64,256]{2,1,0:T(8,128)S(1)}, u32[]{:S(2)}, u32[]{:S(2)}) collective-permute-start(f32[2,64,256]{2,1,0:T(8,128)S(1)} %get-tuple-element.61), channel_id=1, source_target_pairs={{0,192},{64,128},{128,64},{192,0},{1,193},{65,129},{129,65},{193,1... | collective-permute-start | bytes 393224 | tf_op jit(solution)/shard_map/ppermute | solution.py:307

commit v2 on v1

--- a/solution.py
+++ b/solution.py
@@ -21,7 +21,6 @@
 BF16 = jnp.bfloat16
 LIMIT = 24 * 2**20
 VMEM = pl.BlockSpec(memory_space=pltpu.VMEM)
-SMEM = pl.BlockSpec(memory_space=pltpu.SMEM)
 
 
 def run(body, args, outs, scratch=(), flops=0):
@@ -29,7 +28,7 @@
     return pl.pallas_call(
         body,
         out_shape=[jax.ShapeDtypeStruct(s, t) for s, t in outs],
-        in_specs=[SMEM] + [VMEM] * (len(args) - 1),
+        in_specs=[VMEM] * len(args),
         out_specs=[VMEM] * len(outs),
         scratch_shapes=[pltpu.VMEM(s, t) for s, t in scratch],
         cost_estimate=pl.CostEstimate(flops=flops, bytes_accessed=nbytes, transcendentals=0),
@@ -37,6 +36,14 @@
     )(*args)
 
 
+def section():
+    return lax.axis_index("section")
+
+
+def core():
+    return lax.axis_index(CORE)
+
+
 def split(x):
     high = x.astype(BF16)
     return high, (x - high.astype(F32)).astype(BF16)
@@ -76,7 +83,7 @@
     return gate * (1.0 + preact * (1.0 - gate))
 
 
-def prepare_body(s_ref, f_ref, forward_ref, mine_ref, yours_ref, back):
+def prepare_body(f_ref, forward_ref, mine_ref, yours_ref, back):
     for b in range(3):
         rows = slice(b * C, b * C + C)
         low_rows = slice(192 + b * C, 192 + b * C + C)
@@ -86,15 +93,15 @@
         forward_ref[low_rows] = low
         taps = [f_ref[0, (2 - a) * 9 + (2 - b) * 3 + 2 - cc] for a in range(3) for cc in range(3)]
         back[rows] = jnp.concatenate(taps, axis=0).T
-    c = s_ref[1]
+    c = core()
     mine_ref[...] = back[pl.ds(pl.multiple_of(c * 96, 32), 96)]
     yours_ref[...] = back[pl.ds(pl.multiple_of((1 - c) * 96, 32), 96)]
 
 
-def slope_body(ks, s_ref, act_ref, inner_ref, outer_ref, taps_ref, *refs):
-    c = s_ref[1]
+def slope_body(ks, act_ref, inner_ref, outer_ref, taps_ref, *refs):
+    c = core()
     for i, k in enumerate(ks):
-        m = s_ref[0] ^ k
+        m = section() ^ k
         out, vh_ref, vl_ref = refs[3 * i : 3 * i + 3]
         for e in range(4):
             if e == 0:
@@ -127,18 +134,18 @@
     outer_ref[2] = jnp.where(c == 0, first, last)
 
 
-def pick_body(s_ref, d0, d1, d2, d3, cot_ref, s3_ref, inner_ref, outer_ref):
-    m = s_ref[0]
+def pick_body(d0, d1, d2, d3, cot_ref, s3_ref, inner_ref, outer_ref):
+    m = section()
     refs = (d0, d1, d2, d3)
     top = [cot_ref[m, d] * chosen(m ^ 3, refs, d) for d in range(2)]
     for d in range(2):
         s3_ref[d] = top[d]
-    ends(s_ref[1], top, lambda d: chosen(m ^ 2, refs, d), inner_ref, outer_ref)
-
-
-def taps_body(s_ref, mine_ref, yours_ref, one_ref, three_ref, far0_ref, far1_ref, other_ref, out_ref):
-    s = s_ref[0]
-    c = s_ref[1]
+    ends(core(), top, lambda d: chosen(m ^ 2, refs, d), inner_ref, outer_ref)
+
+
+def taps_body(mine_ref, yours_ref, one_ref, three_ref, far0_ref, far1_ref, other_ref, out_ref):
+    s = section()
+    c = core()
 
     def put(layer, row, x):
         high, low = split(x)
@@ -158,9 +165,9 @@
     put(s ^ 2, yours, other_ref[192:288])
 
 
-def upper(layer, s_ref, inner_ref, outer_ref, factors, mid_ref, taps_ref, ig_ref, vh, vl, wh, wl):
-    m = s_ref[0]
-    c = s_ref[1]
+def upper(layer, inner_ref, outer_ref, factors, mid_ref, taps_ref, ig_ref, vh, vl, wh, wl):
+    m = section()
+    c = core()
 
     def left(e):
         return jnp.where(c == 0, outer_ref[e], inner_ref[e])
@@ -196,32 +203,32 @@
     return [conv(taps_ref[layer], wh[d : d + 3].reshape(576, 256), wl[d : d + 3].reshape(576, 256)) for d in range(2)]
 
 
-def top_body(s_ref, inner_in, outer_in, d0, d1, d2, d3, s3_ref, taps_ref, *refs):
+def top_body(inner_in, outer_in, d0, d1, d2, d3, s3_ref, taps_ref, *refs):
     ig3, s2, ig2, s1, inner_ref, outer_ref, vh, vl, wh, wl = refs
-    m = s_ref[0]
+    m = section()
     factors = (d0, d1, d2, d3)
-    for d, x in enumerate(upper(3, s_ref, inner_in, outer_in, factors, s3_ref, taps_ref, ig3, vh, vl, wh, wl)):
+    for d, x in enumerate(upper(3, inner_in, outer_in, factors, s3_ref, taps_ref, ig3, vh, vl, wh, wl)):
         s2[d] = x
     grads = lower(2, taps_ref, wh, wl)
     slopes = [grads[d] * chosen(m ^ 1, factors, d) for d in range(2)]
     for d in range(2):
         ig2[d] = grads[d]
         s1[d] = slopes[d]
-    ends(s_ref[1], slopes, lambda d: chosen(m, factors, d), inner_ref, outer_ref)
-
-
-def low_body(s_ref, inner_in, outer_in, d0, d1, d2, d3, s3, s2, s1, taps_ref, *refs):
+    ends(core(), slopes, lambda d: chosen(m, factors, d), inner_ref, outer_ref)
+
+
+def low_body(inner_in, outer_in, d0, d1, d2, d3, s3, s2, s1, taps_ref, *refs):
     o, ig1, wh, wl, s0, vh, vl = refs[:4], *refs[4:]
-    m = s_ref[0]
-    for d, x in enumerate(upper(1, s_ref, inner_in, outer_in, (d0, d1, d2, d3), s1, taps_ref, ig1, vh, vl, wh, wl)):
+    m = section()
+    for d, x in enumerate(upper(1, inner_in, outer_in, (d0, d1, d2, d3), s1, taps_ref, ig1, vh, vl, wh, wl)):
         s0[d] = x
     for d in range(2):
         for k in range(N):
             o[k][d] = chosen(m ^ k, (s0, s1, s2, s3), d)
 
 
-def last_body(s_ref, wh, wl, ig3, ig2, ig1, taps_ref, p0, p1, p2, p3, ig0):
-    m = s_ref[0]
+def last_body(wh, wl, ig3, ig2, ig1, taps_ref, p0, p1, p2, p3, ig0):
+    m = section()
     for d, g in enumerate(lower(0, taps_ref, wh, wl)):
         ig0[d] = g
     for d in range(2):
@@ -243,9 +250,9 @@
     return total
 
 
-def filter_body(s_ref, *refs):
+def filter_body(*refs):
     keep_ref, send_ref, acc = refs[12:]
-    c = s_ref[1]
+    c = core()
     for k in range(N):
         term = filter_term(*refs[3 * k : 3 * k + 3])
         acc[...] = term if k == 0 else acc[...] + term
@@ -277,8 +284,8 @@
             fill(send_ref)
 
 
-def finish_body(s_ref, own_ref, other_ref, out_ref, full):
-    c = s_ref[1]
+def finish_body(own_ref, other_ref, out_ref, full):
+    c = core()
     full[pl.ds(pl.multiple_of(c * 432, 8), 432)] = own_ref[0:432]
     full[pl.ds(pl.multiple_of((1 - c) * 432, 8), 432)] = other_ref[0:432]
     for a in range(3):
@@ -297,8 +304,8 @@
                         out_ref[0, a * 9 + b * 3 + cc, part * 32 : part * 32 + 32] = x
 
 
-def gather_body(s_ref, x0, x1, x2, x3, out_ref):
-    s = s_ref[0]
+def gather_body(x0, x1, x2, x3, out_ref):
+    s = section()
     for k, ref in enumerate((x0, x1, x2, x3)):
         out_ref[0, s ^ k] = ref[...]
 
@@ -324,9 +331,7 @@
 
 
 def window(activations, filters, cotangent):
-    s = lax.axis_index("section")
     c = lax.axis_index(CORE)
-    place = jnp.stack([s, c]).astype(jnp.int32)
     act = activations[0]
     plane = (C, H * W)
     two = ((2, *plane), F32)
@@ -337,7 +342,7 @@
     inner, outer = neighbours(inner, outer)
     forward, mine, yours = run(
         prepare_body,
-        (place, filters),
+        (filters,),
         [((384, 576), BF16), ((96, 576), F32), ((96, 576), F32)],
         [((192, 576), F32)],
         flops=10**6,
@@ -346,7 +351,7 @@
     for ks in ((2,), (1, 3), (0,)):
         out = run(
             functools.partial(slope_body, ks),
-            (place, act, inner, outer, forward),
+            (act, inner, outer, forward),
             [two, ((4, 192, 256), BF16), ((4, 192, 256), BF16)] * len(ks),
             flops=2 * 2 * 192 * 576 * 256 * 3 * len(ks),
         )
@@ -359,16 +364,14 @@
     far0 = met(three_half[:48], 1)
     far1 = met(one[48:], 3)
     other = swapped(jnp.concatenate([one, three_half, far0, far1], axis=0))
-    (taps,) = run(
-        taps_body, (place, mine, yours, one, three_half, far0, far1, other), [((N, 384, 576), BF16)], flops=10**6
-    )
-
-    s3, inner, outer = run(pick_body, (place, *factors, cotangent), [two, three, three], flops=10**6)
+    (taps,) = run(taps_body, (mine, yours, one, three_half, far0, far1, other), [((N, 384, 576), BF16)], flops=10**6)
+
+    s3, inner, outer = run(pick_body, (*factors, cotangent), [two, three, three], flops=10**6)
     inner, outer = neighbours(inner, outer)
     scratch = [((6, 192, 256), BF16)] * 2 + [((4, 192, 256), BF16)] * 2
     ig3, s2, ig2, s1, inner, outer = run(
         top_body,
-        (place, inner, outer, *factors, s3, taps),
+        (inner, outer, *factors, s3, taps),
         [two, two, two, two, three, three],
         scratch,
         flops=2 * 6 * 192 * 576 * 256 * 3,
@@ -376,24 +379,20 @@
     inner, outer = neighbours(inner, outer)
     *packed, ig1, wh, wl = run(
         low_body,
-        (place, inner, outer, *factors, s3, s2, s1, taps),
+        (inner, outer, *factors, s3, s2, s1, taps),
         [two] * 5 + [((4, 192, 256), BF16)] * 2,
         [((2, *plane), F32)] + scratch[:2],
         flops=2 * 4 * 192 * 576 * 256 * 3,
     )
     slopes = handed(packed)
     packed = run(
-        last_body,
-        (place, wh, wl, ig3, ig2, ig1, taps),
-        [two] * 4,
-        [((2, *plane), F32)],
-        flops=2 * 2 * 192 * 576 * 256 * 3,
+        last_body, (wh, wl, ig3, ig2, ig1, taps), [two] * 4, [((2, *plane), F32)], flops=2 * 2 * 192 * 576 * 256 * 3
     )
     grads = handed(packed)
 
     keep, send = run(
         filter_body,
-        (place, *(x for k in range(N) for x in (slopes[k], *shifted[k]))),
+        tuple(x for k in range(N) for x in (slopes[k], *shifted[k])),
         [((512, 128), F32)] * 2,
         [((192, 576), F32)],
         flops=2 * 8 * 192 * 576 * 256 * 3,
@@ -404,10 +403,8 @@
     total = jnp.sum(part, axis=0) * scaling
     part = lax.all_to_all(jnp.broadcast_to(total[None], (32, 16, 128)), PLANE, 0, 0, tiled=True).reshape(512, 128)
     other_part = swapped(part)
-    (filter_grads,) = run(
-        finish_body, (place, part, other_part), [((1, 27, C, C), F32)], [((864, 128), F32)], flops=10**6
-    )
-    (input_grads,) = run(gather_body, (place, *grads), [((1, N, 2, *plane), F32)], flops=10**6)
+    (filter_grads,) = run(finish_body, (part, other_part), [((1, 27, C, C), F32)], [((864, 128), F32)], flops=10**6)
+    (input_grads,) = run(gather_body, (*grads,), [((1, N, 2, *plane), F32)], flops=10**6)
     return input_grads, filter_grads
 
 

time: 135 us -> 129 us (0.956)
  Pallas kernels: 18.9 us -> 12.4 us
    pallas_call x12, Pallas kernels: 18.9 us -> 12.4 us  [run(): pl.pallas_call(body, out_shape=[jax.ShapeDtypeStruct(s, t) for s, t in ou...]
  transfers between devices with their start and end apart: 22 -> 22, of which waited for: 13 -> 13; matrix products, arithmetic and copies ran while one was open for 1% -> 1% of each run, Pallas kernels for 7% -> 4%
where the time goes in v2:
time: 129 us
  blocking collectives  45.8 us (36%)
  starting transfers between devices  36.5 us (28%)
  waiting for transfers between devices  30.9 us (24%)
  Pallas kernels  12.4 us (10%)
  local copies, waits for them, and re-layouts  2.34 us (2%)
    all_to_all x1, blocking collectives, window(): part = lax.all_to_all(part, PLANE, 0, 0, tiled=True)  30.7 us
    ppermute x13, waiting for transfers between devices, met(): return lax.ppermute(x, 'section', [(i, i ^ k) for i in range(N)])  19.9 us
    ppermute x13, starting transfers between devices, met(): return lax.ppermute(x, 'section', [(i, i ^ k) for i in range(N)])  17.8 us
    all_to_all x1, blocking collectives, window(): lax.all_to_all(jnp.broadcast_to(total[None], (32, 16, 128)), PLANE, 0, 0,...  15.1 us
    ppermute x3, starting transfers between devices, neighbours(): outer = lax.ppermute(outer, DEPTH, pairs + [(j, i) for i, j in pairs])  14.4 us
    pallas_call x12, Pallas kernels, run(): pl.pallas_call(body, out_shape=[jax.ShapeDtypeStruct(s, t) for s, t in ou...  12.4 us
    ppermute x3, waiting for transfers between devices, neighbours(): outer = lax.ppermute(outer, DEPTH, pairs + [(j, i) for i, j in pairs])  9.51 us
    ppermute x6, starting transfers between devices, swapped(): return lax.ppermute(x, CORE, [(0, 1), (1, 0)])  4.35 us
  transfers between devices with their start and end apart: 22, of which 13 were waited for; matrix products, arithmetic and copies ran while one was open for 1% of the time, Pallas kernels for 4%

profile of v2, /device:TPU:1, one launch (start us, length us, event | category | flops | bytes accessed | tf_op | source)
XLA Modules:
  0.0 128.9 jit_solution(6953075676684578131)
XLA Ops:
  0.6 0.0 copy-start
  0.6 0.0 copy-start.1
  0.7 1.2 copy-done.1
  1.9 0.5 shard_map.50
  2.3 3.4 %collective-permute-start.8 = (f32[96,576]{1,0:T(8,128)S(1)}, f32[96,576]{1,0:T(8,128)S(1)}, u32[]{:S(2)}, u32[]{:S(2)}) collective-permute-start(f32[96,576]{1,0:T(8,128)S(1)} %get-tuple-element.47.mine_ref), channel_id=1, source_target_pairs={{0,192},{64,128},{128,64},{192,0},{1,193},{65,129},{129,65},{193,1... | collective-permute-start | bytes 663560 | tf_op jit(solution)/shard_map/ppermute | solution.py:314
  5.7 0.0 collective-permute-start.7
  5.7 4.6 %collective-permute-done.8.three_ref = f32[96,576]{1,0:T(8,128)S(1)} collective-permute-done((f32[96,576]{1,0:T(8,128)S(1)}, f32[96,576]{1,0:T(8,128)S(1)}, u32[]{:S(2)}, u32[]{:S(2)}) %collective-permute-start.8) | collective-permute-done | bytes 221216 | tf_op jit(solution)/shard_map/ppermute | solution.py:314
  10.4 1.0 collective-permute-start.9
  11.4 0.9 collective-permute-done.7.one_ref
  12.3 1.7 %collective-permute-start.10 = (f32[48,576]{1,0:T(8,128)S(1)}, f32[48,576]{1,0:T(8,128)S(1)}, u32[]{:S(2)}, u32[]{:S(2)}) collective-permute-start(f32[48,576]{1,0:T(8,128)S(1)} %slice.9), channel_id=1, source_target_pairs={{0,192},{64,128},{128,64},{192,0},{1,193},{65,129},{129,65},{193,1... | collective-permute-start | bytes 331784 | tf_op jit(solution)/shard_map/ppermute | solution.py:314
  14.0 1.1 dynamic-slice_bitcast_fusion
  15.1 4.9 %collective-permute-start.1 = (f32[4,64,256]{2,1,0:T(8,128)S(1)}, f32[4,64,256]{2,1,0:T(8,128)S(1)}, u32[]{:S(2)}, u32[]{:S(2)}) collective-permute-start(f32[4,64,256]{2,1,0:T(8,128)S(1)} %get-tuple-element.76), channel_id=1, source_target_pairs={{1,2},{3,4},{5,6},{7,8},{9,10},{11,12},{13,14},{15,16},{17,18},{19... | collective-permute-start | bytes 786440 | tf_op jit(solution)/shard_map/ppermute | solution.py:329
  20.0 0.1 collective-permute-start
  20.1 0.0 collective-permute-done.9.far0_ref
  20.1 0.0 collective-permute-done.10.far1_ref
  20.1 0.1 pad_maximum_fusion
  20.2 0.8 collective-permute-start.11
  20.9 3.1 %collective-permute-done.1.outer_ref = f32[4,64,256]{2,1,0:T(8,128)S(1)} collective-permute-done((f32[4,64,256]{2,1,0:T(8,128)S(1)}, f32[4,64,256]{2,1,0:T(8,128)S(1)}, u32[]{:S(2)}, u32[]{:S(2)}) %collective-permute-start.1) | collective-permute-done | bytes 262176 | tf_op jit(solution)/shard_map/ppermute | solution.py:329
  24.0 0.0 collective-permute-done.inner_ref
  24.0 0.9 shard_map.53
  24.9 0.0 copy-start.2
  24.9 1.3 collective-permute-start.3
  26.2 1.3 %shard_map.52 = (f32[2,64,256]{2,1,0:T(8,128)S(1)}, bf16[4,192,256]{2,1,0:T(8,128)(2,1)S(1)}, bf16[4,192,256]{2,1,0:T(8,128)(2,1)S(1)}, f32[2,64,256]{2,1,0:T(8,...) custom-call(f32[4,2,64,256]{3,2,1,0:T(8,128)S(1)} %bitcast.8, ...), custom_call_target="tpu_custom_call" | custom-call | flops 679477248 | bytes 1490944 | tf_op jit(solution)/shard_map/pallas_call | solution.py:28
  27.5 0.8 collective-permute-start.2
  28.3 1.7 %collective-permute-start.4 = (f32[2,64,256]{2,1,0:T(8,128)S(1)}, f32[2,64,256]{2,1,0:T(8,128)S(1)}, u32[]{:S(2)}, u32[]{:S(2)}) collective-permute-start(f32[2,64,256]{2,1,0:T(8,128)S(1)} %get-tuple-element.43), channel_id=1, source_target_pairs={{0,192},{64,128},{128,64},{192,0},{1,193},{65,129},{129,65},{193,1... | collective-permute-start | bytes 393224 | tf_op jit(solution)/shard_map/ppermute | solution.py:314
  30.0 0.9 shard_map.51
  30.9 0.0 collective-permute-done.3.d2
  30.9 1.5 %collective-permute-done.2.d1 = f32[2,64,256]{2,1,0:T(8,128)S(1)} collective-permute-done((f32[2,64,256]{2,1,0:T(8,128)S(1)}, f32[2,64,256]{2,1,0:T(8,128)S(1)}, u32[]{:S(2)}, u32[]{:S(2)}) %collective-permute-start.2) | collective-permute-done | bytes 131104 | tf_op jit(solution)/shard_map/ppermute | solution.py:314
  32.4 1.1 collective-permute-done.4.d3
  33.5 0.1 shard_map.54
  33.6 0.1 collective-permute-start.5
  33.7 5.2 %collective-permute-start.6 = (f32[3,64,256]{2,1,0:T(8,128)S(1)}, f32[3,64,256]{2,1,0:T(8,128)S(1)}, u32[]{:S(2)}, u32[]{:S(2)}) collective-permute-start(f32[3,64,256]{2,1,0:T(8,128)S(1)} %get-tuple-element.45), channel_id=1, source_target_pairs={{1,2},{3,4},{5,6},{7,8},{9,10},{11,12},{13,14},{15,16},{17,18},{19... | collective-permute-start | bytes 589832 | tf_op jit(solution)/shard_map/ppermute | solution.py:329
  38.9 0.0 collective-permute-done.11.other_ref
  38.9 0.3 shard_map.55.taps_ref
  39.2 0.0 collective-permute-done.5.inner_in
  39.2 3.0 %collective-permute-done.6.outer_in = f32[3,64,256]{2,1,0:T(8,128)S(1)} collective-permute-done((f32[3,64,256]{2,1,0:T(8,128)S(1)}, f32[3,64,256]{2,1,0:T(8,128)S(1)}, u32[]{:S(2)}, u32[]{:S(2)}) %collective-permute-start.6) | collective-permute-done | bytes 196640 | tf_op jit(solution)/shard_map/ppermute | solution.py:329
  42.2 2.0 %shard_map.56 = (f32[2,64,256]{2,1,0:T(8,128)S(1)}, f32[2,64,256]{2,1,0:T(8,128)S(1)}, f32[2,64,256]{2,1,0:T(8,128)S(1)}, f32[2,64,256]{2,1,0:T(8,128)S(1)}, f32...) custom-call(f32[3,64,256]{2,1,0:T(8,128)S(1)} %collective-permute-done.5.inner_in, ...), custom_call_target="tpu_custom_call" | custom-call | flops 1019215872 | bytes 2818048 | tf_op jit(solution)/shard_map/pallas_call | solution.py:28
  44.2 0.1 collective-permute-start.12
  44.3 4.3 %collective-permute-start.13 = (f32[3,64,256]{2,1,0:T(8,128)S(1)}, f32[3,64,256]{2,1,0:T(8,128)S(1)}, u32[]{:S(2)}, u32[]{:S(2)}) collective-permute-start(f32[3,64,256]{2,1,0:T(8,128)S(1)} %get-tuple-element.50), channel_id=1, source_target_pairs={{1,2},{3,4},{5,6},{7,8},{9,10},{11,12},{13,14},{15,16},{17,18},{19... | collective-permute-start | bytes 589832 | tf_op jit(solution)/shard_map/ppermute | solution.py:329
  48.6 0.0 collective-permute-done.12.inner_in
  48.6 3.4 %collective-permute-done.13.outer_in = f32[3,64,256]{2,1,0:T(8,128)S(1)} collective-permute-done((f32[3,64,256]{2,1,0:T(8,128)S(1)}, f32[3,64,256]{2,1,0:T(8,128)S(1)}, u32[]{:S(2)}, u32[]{:S(2)}) %collective-permute-start.13) | collective-permute-done | bytes 196640 | tf_op jit(solution)/shard_map/ppermute | solution.py:329
  52.0 1.5 %shard_map.57 = (f32[2,64,256]{2,1,0:T(8,128)S(1)}, f32[2,64,256]{2,1,0:T(8,128)S(1)}, f32[2,64,256]{2,1,0:T(8,128)S(1)}, f32[2,64,256]{2,1,0:T(8,128)S(1)}, f32...) custom-call(f32[3,64,256]{2,1,0:T(8,128)S(1)} %collective-permute-done.12.inner_in, ...), custom_call_target="tpu_custom_call" | custom-call | flops 679477248 | bytes 3080192 | tf_op jit(solution)/shard_map/pallas_call | solution.py:28
  53.5 1.0 collective-permute-start.17
  54.5 2.0 %collective-permute-start.18 = (f32[2,64,256]{2,1,0:T(8,128)S(1)}, f32[2,64,256]{2,1,0:T(8,128)S(1)}, u32[]{:S(2)}, u32[]{:S(2)}) collective-permute-start(f32[2,64,256]{2,1,0:T(8,128)S(1)} %get-tuple-element.68), channel_id=1, source_target_pairs={{0,128},{64,192},{128,0},{192,64},{1,129},{65,193},{129,1},{193,65... | collective-permute-start | bytes 393224 | tf_op jit(solution)/shard_map/ppermute | solution.py:314
  56.5 1.0 collective-permute-start.19
  57.4 0.0 collective-permute-done.17.refs_3_
  57.4 2.8 %collective-permute-done.18.refs_6_ = f32[2,64,256]{2,1,0:T(8,128)S(1)} collective-permute-done((f32[2,64,256]{2,1,0:T(8,128)S(1)}, f32[2,64,256]{2,1,0:T(8,128)S(1)}, u32[]{:S(2)}, u32[]{:S(2)}) %collective-permute-start.18) | collective-permute-done | bytes 131104 | tf_op jit(solution)/shard_map/ppermute | solution.py:314
  60.2 1.4 %collective-permute-done.19.refs_9_ = f32[2,64,256]{2,1,0:T(8,128)S(1)} collective-permute-done((f32[2,64,256]{2,1,0:T(8,128)S(1)}, f32[2,64,256]{2,1,0:T(8,128)S(1)}, u32[]{:S(2)}, u32[]{:S(2)}) %collective-permute-start.19) | collective-permute-done | bytes 131104 | tf_op jit(solution)/shard_map/ppermute | solution.py:314
  61.6 2.3 %shard_map.60 = (f32[512,128]{1,0:T(8,128)S(1)}, f32[512,128]{1,0:T(8,128)S(1)}) custom-call(f32[2,64,256]{2,1,0:T(8,128)S(1)} %get-tuple-element.62.refs_0_, bf16[4,192,256]{2,1,0:T(8,128)(2,1)S(1)} %get-tuple-element.63.refs_1_, bf16[4,192,256]{2,1,0:T(8,128)(2,1)S(1)} %get-tuple-element.64.refs_2_, f32[2,64,256]{2,1,0:T(8,128)S(1)} %collective-permute-done.17.refs_3_, ...), custom_call_target="tpu_custom_call" | custom-call | flops 1358954496 | bytes 3670016 | tf_op jit(solution)/shard_map/pallas_call | solution.py:28
  64.0 0.1 collective-permute-start.20
  64.1 1.5 %collective-permute-done.20 = f32[512,128]{1,0:T(8,128)S(1)} collective-permute-done((f32[512,128]{1,0:T(8,128)S(1)}, f32[512,128]{1,0:T(8,128)S(1)}, u32[]{:S(2)}, u32[]{:S(2)}) %collective-permute-start.20) | collective-permute-done | bytes 262176 | tf_op jit(solution)/shard_map/ppermute | solution.py:322
  65.6 30.7 %all_to_all.10 = f32[32,16,128]{2,1,0:T(8,128)S(1)} all-to-all(f32[32,16,128]{2,1,0:T(8,128)S(1)} %bitcast.12), channel_id=1, replica_groups=mesh['section'=4,'depth_0'=8,'depth_1'=4,'depth_2'=2] {'depth_0','depth_1'}, dimensions={0} | all-to-all | bytes 524288 | tf_op jit(solution)/shard_map/all_to_all | solution.py:401
  96.4 15.1 %all_to_all.11 = f32[32,16,128]{2,1,0:T(8,128)S(1)} all-to-all(f32[32,16,128]{2,1,0:T(8,128)S(1)} %broadcast_in_dim.2), channel_id=1, replica_groups=mesh['section'=4,'depth_0'=8,'depth_1'=4,'depth_2'=2] {'depth_0','depth_1'}, dimensions={0} | all-to-all | bytes 524288 | tf_op jit(solution)/shard_map/all_to_all | solution.py:404
  111.5 3.2 %collective-permute-start.21 = (f32[512,128]{1,0:T(8,128)S(1)}, f32[512,128]{1,0:T(8,128)S(1)}, u32[]{:S(2)}, u32[]{:S(2)}) collective-permute-start(f32[512,128]{1,0:T(8,128)S(1)} %bitcast.10), channel_id=1, source_target_pairs={{0,1},{1,0},{2,3},{3,2},{4,5},{5,4},{6,7},{7,6},{8,9},{9,8},{10,11... | collective-permute-start | bytes 786440 | tf_op jit(solution)/shard_map/ppermute | solution.py:322
  114.7 0.7 shard_map.58
  115.4 0.1 collective-permute-start.14
  115.5 2.4 %collective-permute-start.15 = (f32[2,64,256]{2,1,0:T(8,128)S(1)}, f32[2,64,256]{2,1,0:T(8,128)S(1)}, u32[]{:S(2)}, u32[]{:S(2)}) collective-permute-start(f32[2,64,256]{2,1,0:T(8,128)S(1)} %get-tuple-element.60), channel_id=1, source_target_pairs={{0,128},{64,192},{128,0},{192,64},{1,129},{65,193},{129,1},{193,65... | collective-permute-start | bytes 393224 | tf_op jit(solution)/shard_map/ppermute | solution.py:314
  117.9 1.4 %collective-permute-start.16 = (f32[2,64,256]{2,1,0:T(8,128)S(1)}, f32[2,64,256]{2,1,0:T(8,128)S(1)}, u32[]{:S(2)}, u32[]{:S(2)}) collective-permute-start(f32[2,64,256]{2,1,0:T(8,128)S(1)} %get-tuple-element.61), channel_id=1, source_target_pairs={{0,192},{64,128},{128,64},{192,0},{1,193},{65,129},{129,65},{193,1... | collective-permute-start | bytes 393224 | tf_op jit(solution)/shard_map/ppermute | solution.py:314
  119.4 1.2 collective-permute-done.14.x1
  120.6 3.8 %collective-permute-done.15.x2 = f32[2,64,256]{2,1,0:T(8,128)S(1)} collective-permute-done((f32[2,64,256]{2,1,0:T(8,128)S(1)}, f32[2,64,256]{2,1,0:T(8,128)S(1)}, u32[]{:S(2)}, u32[]{:S(2)}) %collective-permute-start.15) | collective-permute-done | bytes 131104 | tf_op jit(solution)/shard_map/ppermute | solution.py:314
  124.4 2.5 %collective-permute-done.16.x3 = f32[2,64,256]{2,1,0:T(8,128)S(1)} collective-permute-done((f32[2,64,256]{2,1,0:T(8,128)S(1)}, f32[2,64,256]{2,1,0:T(8,128)S(1)}, u32[]{:S(2)}, u32[]{:S(2)}) %collective-permute-start.16) | collective-permute-done | bytes 131104 | tf_op jit(solution)/shard_map/ppermute | solution.py:314
  126.9 0.8 shard_map.59
  127.8 0.0 collective-permute-done.21.other_ref
  127.8 1.1 shard_map.61
  (8 shorter events, 0.1 us)
Async XLA Ops:
  0.6 23.4 %copy-start = (f32[1,4,2,64,256]{4,3,2,1,0:T(8,128)S(1)}, f32[1,4,2,64,256]{4,3,2,1,0:T(8,128)}, u32[]{:S(2)}) copy-start(f32[1,4,2,64,256]{4,3,2,1,0:T(8,128)} %param.3) | copy-start | bytes 1572868
  0.6 1.2 copy-start.1
  2.3 8.0 %collective-permute-start.8 = (f32[96,576]{1,0:T(8,128)S(1)}, f32[96,576]{1,0:T(8,128)S(1)}, u32[]{:S(2)}, u32[]{:S(2)}) collective-permute-start(f32[96,576]{1,0:T(8,128)S(1)} %get-tuple-element.47.mine_ref), channel_id=1, source_target_pairs={{0,192},{64,128},{128,64},{192,0},{1,193},{65,129},{129,65},{193,1... | collective-permute-start | bytes 663560 | tf_op jit(solution)/shard_map/ppermute | solution.py:314
  5.7 6.6 %collective-permute-start.7 = (f32[96,576]{1,0:T(8,128)S(1)}, f32[96,576]{1,0:T(8,128)S(1)}, u32[]{:S(2)}, u32[]{:S(2)}) collective-permute-start(f32[96,576]{1,0:T(8,128)S(1)} %get-tuple-element.47.mine_ref), channel_id=1, source_target_pairs={{0,64},{64,0},{128,192},{192,128},{1,65},{65,1},{129,193},{193,129... | collective-permute-start | bytes 663560 | tf_op jit(solution)/shard_map/ppermute | solution.py:314
  10.4 9.7 %collective-permute-start.9 = (f32[48,576]{1,0:T(8,128)S(1)}, f32[48,576]{1,0:T(8,128)S(1)}, u32[]{:S(2)}, u32[]{:S(2)}) collective-permute-start(f32[48,576]{1,0:T(8,128)S(1)} %slice.8), channel_id=1, source_target_pairs={{0,64},{64,0},{128,192},{192,128},{1,65},{65,1},{129,193},{193,129... | collective-permute-start | bytes 331784 | tf_op jit(solution)/shard_map/ppermute | solution.py:314
  12.3 7.8 %collective-permute-start.10 = (f32[48,576]{1,0:T(8,128)S(1)}, f32[48,576]{1,0:T(8,128)S(1)}, u32[]{:S(2)}, u32[]{:S(2)}) collective-permute-start(f32[48,576]{1,0:T(8,128)S(1)} %slice.9), channel_id=1, source_target_pairs={{0,192},{64,128},{128,64},{192,0},{1,193},{65,129},{129,65},{193,1... | collective-permute-start | bytes 331784 | tf_op jit(solution)/shard_map/ppermute | solution.py:314
  15.1 8.9 %collective-permute-start.1 = (f32[4,64,256]{2,1,0:T(8,128)S(1)}, f32[4,64,256]{2,1,0:T(8,128)S(1)}, u32[]{:S(2)}, u32[]{:S(2)}) collective-permute-start(f32[4,64,256]{2,1,0:T(8,128)S(1)} %get-tuple-element.76), channel_id=1, source_target_pairs={{1,2},{3,4},{5,6},{7,8},{9,10},{11,12},{13,14},{15,16},{17,18},{19... | collective-permute-start | bytes 786440 | tf_op jit(solution)/shard_map/ppermute | solution.py:329
  20.0 4.0 %collective-permute-start = (f32[4,64,256]{2,1,0:T(8,128)S(1)}, f32[4,64,256]{2,1,0:T(8,128)S(1)}, u32[]{:S(2)}, u32[]{:S(2)}) collective-permute-start(f32[4,64,256]{2,1,0:T(8,128)S(1)} %get-tuple-element.77), channel_id=1, source_target_pairs={{0,1},{1,0},{2,3},{3,2},{4,5},{5,4},{6,7},{7,6},{8,9},{9,8},{10,11... | collective-permute-start | bytes 786440 | tf_op jit(solution)/shard_map/ppermute | solution.py:322
  20.2 18.7 %collective-permute-start.11 = (f32[288,576]{1,0:T(8,128)S(1)}, f32[288,576]{1,0:T(8,128)S(1)}, u32[]{:S(2)}, u32[]{:S(2)}) collective-permute-start(f32[288,576]{1,0:T(8,128)S(1)} %pad_maximum_fusion), channel_id=1, source_target_pairs={{0,1},{1,0},{2,3},{3,2},{4,5},{5,4},{6,7},{7,6},{8,9},{9,8},{10,11... | collective-permute-start | bytes 1990664 | tf_op jit(solution)/shard_map/ppermute | solution.py:322
  24.9 8.6 %copy-start.2 = (f32[4,2,64,256]{3,2,1,0:T(8,128)S(1)}, f32[4,2,64,256]{3,2,1,0:T(8,128)}, u32[]{:S(2)}) copy-start(f32[4,2,64,256]{3,2,1,0:T(8,128)} %cot_ref.1) | copy-start | bytes 1572868
  24.9 6.0 %collective-permute-start.3 = (f32[2,64,256]{2,1,0:T(8,128)S(1)}, f32[2,64,256]{2,1,0:T(8,128)S(1)}, u32[]{:S(2)}, u32[]{:S(2)}) collective-permute-start(f32[2,64,256]{2,1,0:T(8,128)S(1)} %get-tuple-element.42), channel_id=1, source_target_pairs={{0,128},{64,192},{128,0},{192,64},{1,129},{65,193},{129,1},{193,65... | collective-permute-start | bytes 393224 | tf_op jit(solution)/shard_map/ppermute | solution.py:314
  27.5 4.9 %collective-permute-start.2 = (f32[2,64,256]{2,1,0:T(8,128)S(1)}, f32[2,64,256]{2,1,0:T(8,128)S(1)}, u32[]{:S(2)}, u32[]{:S(2)}) collective-permute-start(f32[2,64,256]{2,1,0:T(8,128)S(1)} %get-tuple-element.41), channel_id=1, source_target_pairs={{0,64},{64,0},{128,192},{192,128},{1,65},{65,1},{129,193},{193,129... | collective-permute-start | bytes 393224 | tf_op jit(solution)/shard_map/ppermute | solution.py:314
  28.3 5.2 %collective-permute-start.4 = (f32[2,64,256]{2,1,0:T(8,128)S(1)}, f32[2,64,256]{2,1,0:T(8,128)S(1)}, u32[]{:S(2)}, u32[]{:S(2)}) collective-permute-start(f32[2,64,256]{2,1,0:T(8,128)S(1)} %get-tuple-element.43), channel_id=1, source_target_pairs={{0,192},{64,128},{128,64},{192,0},{1,193},{65,129},{129,65},{193,1... | collective-permute-start | bytes 393224 | tf_op jit(solution)/shard_map/ppermute | solution.py:314
  33.6 5.6 %collective-permute-start.5 = (f32[3,64,256]{2,1,0:T(8,128)S(1)}, f32[3,64,256]{2,1,0:T(8,128)S(1)}, u32[]{:S(2)}, u32[]{:S(2)}) collective-permute-start(f32[3,64,256]{2,1,0:T(8,128)S(1)} %get-tuple-element.44), channel_id=1, source_target_pairs={{0,1},{1,0},{2,3},{3,2},{4,5},{5,4},{6,7},{7,6},{8,9},{9,8},{10,11... | collective-permute-start | bytes 589832 | tf_op jit(solution)/shard_map/ppermute | solution.py:322
  33.7 8.6 %collective-permute-start.6 = (f32[3,64,256]{2,1,0:T(8,128)S(1)}, f32[3,64,256]{2,1,0:T(8,128)S(1)}, u32[]{:S(2)}, u32[]{:S(2)}) collective-permute-start(f32[3,64,256]{2,1,0:T(8,128)S(1)} %get-tuple-element.45), channel_id=1, source_target_pairs={{1,2},{3,4},{5,6},{7,8},{9,10},{11,12},{13,14},{15,16},{17,18},{19... | collective-permute-start | bytes 589832 | tf_op jit(solution)/shard_map/ppermute | solution.py:329
  44.2 4.4 %collective-permute-start.12 = (f32[3,64,256]{2,1,0:T(8,128)S(1)}, f32[3,64,256]{2,1,0:T(8,128)S(1)}, u32[]{:S(2)}, u32[]{:S(2)}) collective-permute-start(f32[3,64,256]{2,1,0:T(8,128)S(1)} %get-tuple-element.49), channel_id=1, source_target_pairs={{0,1},{1,0},{2,3},{3,2},{4,5},{5,4},{6,7},{7,6},{8,9},{9,8},{10,11... | collective-permute-start | bytes 589832 | tf_op jit(solution)/shard_map/ppermute | solution.py:322
  44.3 7.7 %collective-permute-start.13 = (f32[3,64,256]{2,1,0:T(8,128)S(1)}, f32[3,64,256]{2,1,0:T(8,128)S(1)}, u32[]{:S(2)}, u32[]{:S(2)}) collective-permute-start(f32[3,64,256]{2,1,0:T(8,128)S(1)} %get-tuple-element.50), channel_id=1, source_target_pairs={{1,2},{3,4},{5,6},{7,8},{9,10},{11,12},{13,14},{15,16},{17,18},{19... | collective-permute-start | bytes 589832 | tf_op jit(solution)/shard_map/ppermute | solution.py:329
  53.5 3.9 %collective-permute-start.17 = (f32[2,64,256]{2,1,0:T(8,128)S(1)}, f32[2,64,256]{2,1,0:T(8,128)S(1)}, u32[]{:S(2)}, u32[]{:S(2)}) collective-permute-start(f32[2,64,256]{2,1,0:T(8,128)S(1)} %get-tuple-element.65), channel_id=1, source_target_pairs={{0,64},{64,0},{128,192},{192,128},{1,65},{65,1},{129,193},{193,129... | collective-permute-start | bytes 393224 | tf_op jit(solution)/shard_map/ppermute | solution.py:314
  54.5 5.8 %collective-permute-start.18 = (f32[2,64,256]{2,1,0:T(8,128)S(1)}, f32[2,64,256]{2,1,0:T(8,128)S(1)}, u32[]{:S(2)}, u32[]{:S(2)}) collective-permute-start(f32[2,64,256]{2,1,0:T(8,128)S(1)} %get-tuple-element.68), channel_id=1, source_target_pairs={{0,128},{64,192},{128,0},{192,64},{1,129},{65,193},{129,1},{193,65... | collective-permute-start | bytes 393224 | tf_op jit(solution)/shard_map/ppermute | solution.py:314
  56.5 5.2 %collective-permute-start.19 = (f32[2,64,256]{2,1,0:T(8,128)S(1)}, f32[2,64,256]{2,1,0:T(8,128)S(1)}, u32[]{:S(2)}, u32[]{:S(2)}) collective-permute-start(f32[2,64,256]{2,1,0:T(8,128)S(1)} %get-tuple-element.71), channel_id=1, source_target_pairs={{0,192},{64,128},{128,64},{192,0},{1,193},{65,129},{129,65},{193,1... | collective-permute-start | bytes 393224 | tf_op jit(solution)/shard_map/ppermute | solution.py:314
  64.0 1.6 %collective-permute-start.20 = (f32[512,128]{1,0:T(8,128)S(1)}, f32[512,128]{1,0:T(8,128)S(1)}, u32[]{:S(2)}, u32[]{:S(2)}) collective-permute-start(f32[512,128]{1,0:T(8,128)S(1)} %get-tuple-element.75), channel_id=1, source_target_pairs={{0,1},{1,0},{2,3},{3,2},{4,5},{5,4},{6,7},{7,6},{8,9},{9,8},{10,11... | collective-permute-start | bytes 786440 | tf_op jit(solution)/shard_map/ppermute | solution.py:322
  111.5 16.3 %collective-permute-start.21 = (f32[512,128]{1,0:T(8,128)S(1)}, f32[512,128]{1,0:T(8,128)S(1)}, u32[]{:S(2)}, u32[]{:S(2)}) collective-permute-start(f32[512,128]{1,0:T(8,128)S(1)} %bitcast.10), channel_id=1, source_target_pairs={{0,1},{1,0},{2,3},{3,2},{4,5},{5,4},{6,7},{7,6},{8,9},{9,8},{10,11... | collective-permute-start | bytes 786440 | tf_op jit(solution)/shard_map/ppermute | solution.py:322
  115.4 5.1 %collective-permute-start.14 = (f32[2,64,256]{2,1,0:T(8,128)S(1)}, f32[2,64,256]{2,1,0:T(8,128)S(1)}, u32[]{:S(2)}, u32[]{:S(2)}) collective-permute-start(f32[2,64,256]{2,1,0:T(8,128)S(1)} %get-tuple-element.59), channel_id=1, source_target_pairs={{0,64},{64,0},{128,192},{192,128},{1,65},{65,1},{129,193},{193,129... | collective-permute-start | bytes 393224 | tf_op jit(solution)/shard_map/ppermute | solution.py:314
  115.5 8.9 %collective-permute-start.15 = (f32[2,64,256]{2,1,0:T(8,128)S(1)}, f32[2,64,256]{2,1,0:T(8,128)S(1)}, u32[]{:S(2)}, u32[]{:S(2)}) collective-permute-start(f32[2,64,256]{2,1,0:T(8,128)S(1)} %get-tuple-element.60), channel_id=1, source_target_pairs={{0,128},{64,192},{128,0},{192,64},{1,129},{65,193},{129,1},{193,65... | collective-permute-start | bytes 393224 | tf_op jit(solution)/shard_map/ppermute | solution.py:314
  117.9 9.0 %collective-permute-start.16 = (f32[2,64,256]{2,1,0:T(8,128)S(1)}, f32[2,64,256]{2,1,0:T(8,128)S(1)}, u32[]{:S(2)}, u32[]{:S(2)}) collective-permute-start(f32[2,64,256]{2,1,0:T(8,128)S(1)} %get-tuple-element.61), channel_id=1, source_target_pairs={{0,192},{64,128},{128,64},{192,0},{1,193},{65,129},{129,65},{193,1... | collective-permute-start | bytes 393224 | tf_op jit(solution)/shard_map/ppermute | solution.py:314

commit v3 on v2

--- a/solution.py
+++ b/solution.py
@@ -125,22 +125,26 @@
     return out
 
 
-def ends(c, planes, face_at, inner_ref, outer_ref):
-    for d in range(2):
-        inner_ref[d] = planes[d]
-        outer_ref[d] = planes[d]
-    first, last = face_at(0), face_at(1)
-    inner_ref[2] = jnp.where(c == 0, last, first)
-    outer_ref[2] = jnp.where(c == 0, first, last)
-
-
-def pick_body(d0, d1, d2, d3, cot_ref, s3_ref, inner_ref, outer_ref):
+def by_core(even, odd):
+    return jnp.where(core() == 0, even, odd)
+
+
+def pick_body(d0, d1, d2, d3, cot_ref, s3_ref, inner_ref, outer_ref, one_ref, two_ref):
     m = section()
     refs = (d0, d1, d2, d3)
     top = [cot_ref[m, d] * chosen(m ^ 3, refs, d) for d in range(2)]
+    face = [chosen(m ^ 1, refs, d) for d in range(2)]
     for d in range(2):
         s3_ref[d] = top[d]
-    ends(core(), top, lambda d: chosen(m ^ 2, refs, d), inner_ref, outer_ref)
+        below = chosen(m ^ 2, refs, d)
+        for ref in (inner_ref, outer_ref):
+            ref[d] = top[d]
+            ref[2 + d] = below
+    inner_ref[4] = by_core(face[1], face[0])
+    outer_ref[4] = by_core(face[0], face[1])
+    even = lax.rem(lax.axis_index("depth_1"), 2) == 0
+    one_ref[0] = jnp.where(even, top[1], top[0])
+    two_ref[0] = jnp.where(even, top[0], top[1])
 
 
 def taps_body(mine_ref, yours_ref, one_ref, three_ref, far0_ref, far1_ref, other_ref, out_ref):
@@ -165,71 +169,70 @@
     put(s ^ 2, yours, other_ref[192:288])
 
 
-def upper(layer, inner_ref, outer_ref, factors, mid_ref, taps_ref, ig_ref, vh, vl, wh, wl):
-    m = section()
-    c = core()
-
-    def left(e):
-        return jnp.where(c == 0, outer_ref[e], inner_ref[e])
-
-    def right(e):
-        return jnp.where(c == 0, inner_ref[e], outer_ref[e])
-
-    for e in range(6):
-        x = left(e) if e < 2 else (mid_ref[e - 2] if e < 4 else right(e - 4))
-        high, low = split(across(x))
-        vh[e] = high
-        vl[e] = low
-    slopes = []
-    for d in range(4):
-        g = conv(taps_ref[layer], vh[d : d + 3].reshape(576, 256), vl[d : d + 3].reshape(576, 256))
-        if d == 0:
-            factor = left(2)
-        elif d == 3:
-            factor = right(2)
-        else:
-            factor = chosen(m ^ (layer - 1), factors, d - 1)
-        slope = g * factor
-        if 0 < d < 3:
-            ig_ref[d - 1] = g
-            slopes.append(slope)
-        high, low = split(across(slope))
-        wh[d] = high
-        wl[d] = low
-    return slopes
-
-
-def lower(layer, taps_ref, wh, wl):
-    return [conv(taps_ref[layer], wh[d : d + 3].reshape(576, 256), wl[d : d + 3].reshape(576, 256)) for d in range(2)]
-
-
-def top_body(inner_in, outer_in, d0, d1, d2, d3, s3_ref, taps_ref, *refs):
-    ig3, s2, ig2, s1, inner_ref, outer_ref, vh, vl, wh, wl = refs
+def store(x, high_ref, low_ref, at):
+    high, low = split(across(x))
+    high_ref[at] = high
+    low_ref[at] = low
+
+
+def convs(taps_ref, layer, high_ref, low_ref, count):
+    return [
+        conv(taps_ref[layer], high_ref[d : d + 3].reshape(576, 256), low_ref[d : d + 3].reshape(576, 256))
+        for d in range(count)
+    ]
+
+
+def chain_body(inner_in, outer_in, one_in, two_in, d0, d1, d2, d3, s3, taps_ref, *refs):
+    o, ig3, ig2, ig1, s0, inner_ref, outer_ref, s2, s1, ah, al, bh, bl, ch, cl = refs[:4], *refs[4:]
     m = section()
     factors = (d0, d1, d2, d3)
-    for d, x in enumerate(upper(3, inner_in, outer_in, factors, s3_ref, taps_ref, ig3, vh, vl, wh, wl)):
-        s2[d] = x
-    grads = lower(2, taps_ref, wh, wl)
-    slopes = [grads[d] * chosen(m ^ 1, factors, d) for d in range(2)]
-    for d in range(2):
-        ig2[d] = grads[d]
-        s1[d] = slopes[d]
-    ends(core(), slopes, lambda d: chosen(m, factors, d), inner_ref, outer_ref)
-
-
-def low_body(inner_in, outer_in, d0, d1, d2, d3, s3, s2, s1, taps_ref, *refs):
-    o, ig1, wh, wl, s0, vh, vl = refs[:4], *refs[4:]
-    m = section()
-    for d, x in enumerate(upper(1, inner_in, outer_in, (d0, d1, d2, d3), s1, taps_ref, ig1, vh, vl, wh, wl)):
-        s0[d] = x
+    even = lax.rem(lax.axis_index("depth_1"), 2) == 0
+
+    def left(e):
+        return by_core(outer_in[e], inner_in[e])
+
+    def right(e):
+        return by_core(inner_in[e], outer_in[e])
+
+    planes = [jnp.where(even, two_in[0], one_in[0]), left(0), left(1), s3[0], s3[1]]
+    planes += [right(0), right(1), jnp.where(even, one_in[0], two_in[0])]
+    for e, x in enumerate(planes):
+        store(x, ah, al, e)
+    for e, g in enumerate(convs(taps_ref, 3, ah, al, 6)):
+        if e < 2:
+            slope = g * left(2 + e)
+        elif e > 3:
+            slope = g * right(e - 2)
+        else:
+            slope = g * chosen(m ^ 2, factors, e - 2)
+            ig3[e - 2] = g
+            s2[e - 2] = slope
+        store(slope, bh, bl, e)
+    for e, g in enumerate(convs(taps_ref, 2, bh, bl, 4)):
+        if e == 0:
+            slope = g * left(4)
+        elif e == 3:
+            slope = g * right(4)
+        else:
+            slope = g * chosen(m ^ 1, factors, e - 1)
+            ig2[e - 1] = g
+            s1[e - 1] = slope
+        store(slope, ch, cl, e)
+    for d, g in enumerate(convs(taps_ref, 1, ch, cl, 2)):
+        ig1[d] = g
+        s0[d] = g * chosen(m, factors, d)
     for d in range(2):
         for k in range(N):
             o[k][d] = chosen(m ^ k, (s0, s1, s2, s3), d)
-
-
-def last_body(wh, wl, ig3, ig2, ig1, taps_ref, p0, p1, p2, p3, ig0):
+    inner_ref[0] = by_core(s0[1], s0[0])
+    outer_ref[0] = by_core(s0[0], s0[1])
+
+
+def last_body(inner_in, outer_in, s0, ig3, ig2, ig1, taps_ref, p0, p1, p2, p3, ig0, vh, vl):
     m = section()
-    for d, g in enumerate(lower(0, taps_ref, wh, wl)):
+    for e, x in enumerate((by_core(outer_in[0], inner_in[0]), s0[0], s0[1], by_core(inner_in[0], outer_in[0]))):
+        store(x, vh, vl, e)
+    for d, g in enumerate(convs(taps_ref, 0, vh, vl, 2)):
         ig0[d] = g
     for d in range(2):
         for k, p in enumerate((p0, p1, p2, p3)):
@@ -330,12 +333,20 @@
     return inner, outer
 
 
+def skipped(one, two):
+    count = lax.axis_size(DEPTH)
+    out = []
+    for x, first in ((one, 0), (two, 2)):
+        pairs = [(i + c, i + c + 2) for i in range(first, count - 2, 4) for c in range(2)]
+        out.append(lax.ppermute(x, DEPTH, pairs + [(j, i) for i, j in pairs]))
+    return out
+
+
 def window(activations, filters, cotangent):
     c = lax.axis_index(CORE)
     act = activations[0]
     plane = (C, H * W)
     two = ((2, *plane), F32)
-    three = ((3, *plane), F32)
 
     inner = lax.dynamic_index_in_dim(act, 1 - c, 1, keepdims=False)
     outer = lax.dynamic_index_in_dim(act, c, 1, keepdims=False)
@@ -366,27 +377,29 @@
     other = swapped(jnp.concatenate([one, three_half, far0, far1], axis=0))
     (taps,) = run(taps_body, (mine, yours, one, three_half, far0, far1, other), [((N, 384, 576), BF16)], flops=10**6)
 
-    s3, inner, outer = run(pick_body, (*factors, cotangent), [two, three, three], flops=10**6)
+    one_plane = ((1, *plane), F32)
+    five = ((5, *plane), F32)
+    s3, inner, outer, one, two_apart = run(
+        pick_body, (*factors, cotangent), [two, five, five, one_plane, one_plane], flops=10**6
+    )
     inner, outer = neighbours(inner, outer)
-    scratch = [((6, 192, 256), BF16)] * 2 + [((4, 192, 256), BF16)] * 2
-    ig3, s2, ig2, s1, inner, outer = run(
-        top_body,
-        (inner, outer, *factors, s3, taps),
-        [two, two, two, two, three, three],
-        scratch,
-        flops=2 * 6 * 192 * 576 * 256 * 3,
-    )
+    one, two_apart = skipped(one, two_apart)
+    shifted_planes = [((e, 192, 256), BF16) for e in (8, 8, 6, 6, 4, 4)]
+    *packed, ig3, ig2, ig1, s0, inner, outer = run(
+        chain_body,
+        (inner, outer, one, two_apart, *factors, s3, taps),
+        [two] * 8 + [one_plane] * 2,
+        [((2, *plane), F32)] * 2 + shifted_planes,
+        flops=2 * 12 * 192 * 576 * 256 * 3,
+    )
+    slopes = handed(packed)
     inner, outer = neighbours(inner, outer)
-    *packed, ig1, wh, wl = run(
-        low_body,
-        (inner, outer, *factors, s3, s2, s1, taps),
-        [two] * 5 + [((4, 192, 256), BF16)] * 2,
-        [((2, *plane), F32)] + scratch[:2],
-        flops=2 * 4 * 192 * 576 * 256 * 3,
-    )
-    slopes = handed(packed)
     packed = run(
-        last_body, (wh, wl, ig3, ig2, ig1, taps), [two] * 4, [((2, *plane), F32)], flops=2 * 2 * 192 * 576 * 256 * 3
+        last_body,
+        (inner, outer, s0, ig3, ig2, ig1, taps),
+        [two] * 4,
+        [((2, *plane), F32)] + shifted_planes[4:],
+        flops=2 * 2 * 192 * 576 * 256 * 3,
     )
     grads = handed(packed)
 
@@ -401,7 +414,8 @@
     part = lax.all_to_all(part, PLANE, 0, 0, tiled=True)
     scaling = 1.0 / math.sqrt(N * 2 * lax.axis_size(DEPTH) * H * W)
     total = jnp.sum(part, axis=0) * scaling
-    part = lax.all_to_all(jnp.broadcast_to(total[None], (32, 16, 128)), PLANE, 0, 0, tiled=True).reshape(512, 128)
+    part = lax.all_to_all(jnp.broadcast_to(total[None], (32, 16, 128)), PLANE, 0, 0, tiled=True)
+    part = part.reshape(512, 128)
     other_part = swapped(part)
     (filter_grads,) = run(finish_body, (part, other_part), [((1, 27, C, C), F32)], [((864, 128), F32)], flops=10**6)
     (input_grads,) = run(gather_body, (*grads,), [((1, N, 2, *plane), F32)], flops=10**6)

time: 129 us -> 127 us (0.984)
  the two profiles are of different devices: /device:TPU:1 before, /device:TPU:25 now
where the time goes in v3:
time: 127 us
  starting transfers between devices  38.4 us (30%)
  waiting for transfers between devices  36.9 us (29%)
  blocking collectives  35.7 us (28%)
  Pallas kernels  12.4 us (10%)
  local copies, waits for them, and re-layouts  2.34 us (2%)
    ppermute x13, waiting for transfers between devices, met(): return lax.ppermute(x, 'section', [(i, i ^ k) for i in range(N)])  24 us
    all_to_all x1, blocking collectives, window(): part = lax.all_to_all(part, PLANE, 0, 0, tiled=True)  20.4 us
    ppermute x13, starting transfers between devices, met(): return lax.ppermute(x, 'section', [(i, i ^ k) for i in range(N)])  15.8 us
    all_to_all x1, blocking collectives, window(): lax.all_to_all(jnp.broadcast_to(total[None], (32, 16, 128)), PLANE, 0, 0,...  15.2 us
    ppermute x3, starting transfers between devices, neighbours(): outer = lax.ppermute(outer, DEPTH, pairs + [(j, i) for i, j in pairs])  14 us
    pallas_call x11, Pallas kernels, run(): pl.pallas_call(body, out_shape=[jax.ShapeDtypeStruct(s, t) for s, t in ou...  12.4 us
    ppermute x3, waiting for transfers between devices, neighbours(): outer = lax.ppermute(outer, DEPTH, pairs + [(j, i) for i, j in pairs])  7.48 us
    ppermute x6, starting transfers between devices, swapped(): return lax.ppermute(x, CORE, [(0, 1), (1, 0)])  6 us
  transfers between devices with their start and end apart: 24, of which 16 were waited for; matrix products, arithmetic and copies ran while one was open for 1% of the time, Pallas kernels for 4%

profile of v3, /device:TPU:25, one launch (start us, length us, event | category | flops | bytes accessed | tf_op | source)
XLA Modules:
  0.0 126.8 jit_solution(2569215304636910143)
XLA Ops:
  0.6 0.0 copy-start
  0.7 1.2 copy-done.1
  1.9 0.5 shard_map.50
  2.3 2.6 %collective-permute-start.10 = (f32[96,576]{1,0:T(8,128)S(1)}, f32[96,576]{1,0:T(8,128)S(1)}, u32[]{:S(2)}, u32[]{:S(2)}) collective-permute-start(f32[96,576]{1,0:T(8,128)S(1)} %get-tuple-element.48.mine_ref), channel_id=1, source_target_pairs={{0,192},{64,128},{128,64},{192,0},{1,193},{65,129},{129,65},{193,1... | collective-permute-start | bytes 663560 | tf_op jit(solution)/shard_map/ppermute | solution.py:317
  4.9 0.0 collective-permute-start.9
  4.9 5.6 %collective-permute-done.10.three_ref = f32[96,576]{1,0:T(8,128)S(1)} collective-permute-done((f32[96,576]{1,0:T(8,128)S(1)}, f32[96,576]{1,0:T(8,128)S(1)}, u32[]{:S(2)}, u32[]{:S(2)}) %collective-permute-start.10) | collective-permute-done | bytes 221216 | tf_op jit(solution)/shard_map/ppermute | solution.py:317
  10.5 0.1 collective-permute-start.11
  10.6 0.9 collective-permute-done.9.one_ref
  11.5 1.7 %collective-permute-start.12 = (f32[48,576]{1,0:T(8,128)S(1)}, f32[48,576]{1,0:T(8,128)S(1)}, u32[]{:S(2)}, u32[]{:S(2)}) collective-permute-start(f32[48,576]{1,0:T(8,128)S(1)} %slice.9), channel_id=1, source_target_pairs={{0,192},{64,128},{128,64},{192,0},{1,193},{65,129},{129,65},{193,1... | collective-permute-start | bytes 331784 | tf_op jit(solution)/shard_map/ppermute | solution.py:317
  13.2 1.1 dynamic-slice_bitcast_fusion
  14.3 4.9 %collective-permute-start.1 = (f32[4,64,256]{2,1,0:T(8,128)S(1)}, f32[4,64,256]{2,1,0:T(8,128)S(1)}, u32[]{:S(2)}, u32[]{:S(2)}) collective-permute-start(f32[4,64,256]{2,1,0:T(8,128)S(1)} %get-tuple-element.74), channel_id=1, source_target_pairs={{1,2},{3,4},{5,6},{7,8},{9,10},{11,12},{13,14},{15,16},{17,18},{19... | collective-permute-start | bytes 786440 | tf_op jit(solution)/shard_map/ppermute | solution.py:332
  19.2 0.1 collective-permute-start
  19.3 0.0 collective-permute-done.11.far0_ref
  19.3 0.0 collective-permute-done.12.far1_ref
  19.3 0.1 pad_maximum_fusion
  19.4 0.6 collective-permute-start.13
  19.9 4.2 %collective-permute-done.1.outer_ref = f32[4,64,256]{2,1,0:T(8,128)S(1)} collective-permute-done((f32[4,64,256]{2,1,0:T(8,128)S(1)}, f32[4,64,256]{2,1,0:T(8,128)S(1)}, u32[]{:S(2)}, u32[]{:S(2)}) %collective-permute-start.1) | collective-permute-done | bytes 262176 | tf_op jit(solution)/shard_map/ppermute | solution.py:332
  24.1 0.0 collective-permute-done.inner_ref
  24.1 0.9 shard_map.53
  24.9 0.0 copy-start.2
  25.0 1.3 %collective-permute-start.3 = (f32[2,64,256]{2,1,0:T(8,128)S(1)}, f32[2,64,256]{2,1,0:T(8,128)S(1)}, u32[]{:S(2)}, u32[]{:S(2)}) collective-permute-start(f32[2,64,256]{2,1,0:T(8,128)S(1)} %get-tuple-element.41), channel_id=1, source_target_pairs={{0,128},{64,192},{128,0},{192,64},{1,129},{65,193},{129,1},{193,65... | collective-permute-start | bytes 393224 | tf_op jit(solution)/shard_map/ppermute | solution.py:317
  26.2 1.3 %shard_map.52 = (f32[2,64,256]{2,1,0:T(8,128)S(1)}, bf16[4,192,256]{2,1,0:T(8,128)(2,1)S(1)}, bf16[4,192,256]{2,1,0:T(8,128)(2,1)S(1)}, f32[2,64,256]{2,1,0:T(8,...) custom-call(f32[4,2,64,256]{3,2,1,0:T(8,128)S(1)} %bitcast.8, ...), custom_call_target="tpu_custom_call" | custom-call | flops 679477248 | bytes 1490944 | tf_op jit(solution)/shard_map/pallas_call | solution.py:28
  27.6 0.5 collective-permute-start.2
  28.1 1.7 %collective-permute-start.4 = (f32[2,64,256]{2,1,0:T(8,128)S(1)}, f32[2,64,256]{2,1,0:T(8,128)S(1)}, u32[]{:S(2)}, u32[]{:S(2)}) collective-permute-start(f32[2,64,256]{2,1,0:T(8,128)S(1)} %get-tuple-element.42), channel_id=1, source_target_pairs={{0,192},{64,128},{128,64},{192,0},{1,193},{65,129},{129,65},{193,1... | collective-permute-start | bytes 393224 | tf_op jit(solution)/shard_map/ppermute | solution.py:317
  29.8 0.9 shard_map.51
  30.7 1.3 collective-permute-done.3.d2
  31.9 1.2 collective-permute-done.2.d1
  33.2 0.8 collective-permute-done.4.d3
  33.9 0.1 shard_map.54
  34.0 1.4 %collective-permute-start.5 = (f32[5,64,256]{2,1,0:T(8,128)S(1)}, f32[5,64,256]{2,1,0:T(8,128)S(1)}, u32[]{:S(2)}, u32[]{:S(2)}) collective-permute-start(f32[5,64,256]{2,1,0:T(8,128)S(1)} %get-tuple-element.43), channel_id=1, source_target_pairs={{0,1},{1,0},{2,3},{3,2},{4,5},{5,4},{6,7},{7,6},{8,9},{9,8},{10,11... | collective-permute-start | bytes 983048 | tf_op jit(solution)/shard_map/ppermute | solution.py:325
  35.5 4.7 %collective-permute-start.6 = (f32[5,64,256]{2,1,0:T(8,128)S(1)}, f32[5,64,256]{2,1,0:T(8,128)S(1)}, u32[]{:S(2)}, u32[]{:S(2)}) collective-permute-start(f32[5,64,256]{2,1,0:T(8,128)S(1)} %get-tuple-element.44), channel_id=1, source_target_pairs={{1,2},{3,4},{5,6},{7,8},{9,10},{11,12},{13,14},{15,16},{17,18},{19... | collective-permute-start | bytes 983048 | tf_op jit(solution)/shard_map/ppermute | solution.py:332
  40.2 0.1 collective-permute-start.7
  40.3 2.5 %collective-permute-start.8 = (f32[1,64,256]{2,1,0:T(8,128)S(1)}, f32[1,64,256]{2,1,0:T(8,128)S(1)}, u32[]{:S(2)}, u32[]{:S(2)}) collective-permute-start(f32[1,64,256]{2,1,0:T(8,128)S(1)} %get-tuple-element.46), channel_id=1, source_target_pairs={{2,4},{3,5},{6,8},{7,9},{10,12},{11,13},{14,16},{15,17},{18,20},{1... | collective-permute-start | bytes 196616 | tf_op jit(solution)/shard_map/ppermute | solution.py:341
  42.9 0.0 collective-permute-done.13.other_ref
  42.9 0.3 shard_map.55.taps_ref
  43.2 1.4 %collective-permute-done.7.one_in = f32[1,64,256]{2,1,0:T(8,128)S(1)} collective-permute-done((f32[1,64,256]{2,1,0:T(8,128)S(1)}, f32[1,64,256]{2,1,0:T(8,128)S(1)}, u32[]{:S(2)}, u32[]{:S(2)}) %collective-permute-start.7) | collective-permute-done | bytes 65568 | tf_op jit(solution)/shard_map/ppermute | solution.py:341
  44.6 2.9 %collective-permute-done.8.two_in = f32[1,64,256]{2,1,0:T(8,128)S(1)} collective-permute-done((f32[1,64,256]{2,1,0:T(8,128)S(1)}, f32[1,64,256]{2,1,0:T(8,128)S(1)}, u32[]{:S(2)}, u32[]{:S(2)}) %collective-permute-start.8) | collective-permute-done | bytes 65568 | tf_op jit(solution)/shard_map/ppermute | solution.py:341
  47.4 3.4 %shard_map.56 = (f32[2,64,256]{2,1,0:T(8,128)S(1)}, f32[2,64,256]{2,1,0:T(8,128)S(1)}, f32[2,64,256]{2,1,0:T(8,128)S(1)}, f32[2,64,256]{2,1,0:T(8,128)S(1)}, f32...) custom-call(f32[5,64,256]{2,1,0:T(8,128)S(1)} %collective-permute-do, ...), custom_call_target="tpu_custom_call" | custom-call | flops 2038431744 | bytes 3211264 | tf_op jit(solution)/shard_map/pallas_call | solution.py:28
  50.8 0.6 collective-permute-start.19
  51.4 2.2 %collective-permute-start.20 = (f32[2,64,256]{2,1,0:T(8,128)S(1)}, f32[2,64,256]{2,1,0:T(8,128)S(1)}, u32[]{:S(2)}, u32[]{:S(2)}) collective-permute-start(f32[2,64,256]{2,1,0:T(8,128)S(1)} %get-tuple-element.66), channel_id=1, source_target_pairs={{0,128},{64,192},{128,0},{192,64},{1,129},{65,193},{129,1},{193,65... | collective-permute-start | bytes 393224 | tf_op jit(solution)/shard_map/ppermute | solution.py:317
  53.7 1.1 collective-permute-start.21
  54.8 1.3 %collective-permute-done.19.refs_3_ = f32[2,64,256]{2,1,0:T(8,128)S(1)} collective-permute-done((f32[2,64,256]{2,1,0:T(8,128)S(1)}, f32[2,64,256]{2,1,0:T(8,128)S(1)}, u32[]{:S(2)}, u32[]{:S(2)}) %collective-permute-start.19) | collective-permute-done | bytes 131104 | tf_op jit(solution)/shard_map/ppermute | solution.py:317
  56.1 3.9 %collective-permute-done.20.refs_6_ = f32[2,64,256]{2,1,0:T(8,128)S(1)} collective-permute-done((f32[2,64,256]{2,1,0:T(8,128)S(1)}, f32[2,64,256]{2,1,0:T(8,128)S(1)}, u32[]{:S(2)}, u32[]{:S(2)}) %collective-permute-start.20) | collective-permute-done | bytes 131104 | tf_op jit(solution)/shard_map/ppermute | solution.py:317
  60.0 2.5 %collective-permute-done.21.refs_9_ = f32[2,64,256]{2,1,0:T(8,128)S(1)} collective-permute-done((f32[2,64,256]{2,1,0:T(8,128)S(1)}, f32[2,64,256]{2,1,0:T(8,128)S(1)}, u32[]{:S(2)}, u32[]{:S(2)}) %collective-permute-start.21) | collective-permute-done | bytes 131104 | tf_op jit(solution)/shard_map/ppermute | solution.py:317
  62.5 2.3 %shard_map.59 = (f32[512,128]{1,0:T(8,128)S(1)}, f32[512,128]{1,0:T(8,128)S(1)}) custom-call(f32[2,64,256]{2,1,0:T(8,128)S(1)} %get-tuple-element.60.refs_0_, bf16[4,192,256]{2,1,0:T(8,128)(2,1)S(1)} %get-tuple-element.61.refs_1_, bf16[4,192,256]{2,1,0:T(8,128)(2,1)S(1)} %get-tuple-element.62.refs_2_, f32[2,64,256]{2,1,0:T(8,128)S(1)} %collective-permute-done.19.refs_3_, ...), custom_call_target="tpu_custom_call" | custom-call | flops 1358954496 | bytes 3670016 | tf_op jit(solution)/shard_map/pallas_call | solution.py:28
  64.8 0.9 collective-permute-start.22
  65.8 1.2 collective-permute-done.22
  67.0 20.4 %all_to_all.10 = f32[32,16,128]{2,1,0:T(8,128)S(1)} all-to-all(f32[32,16,128]{2,1,0:T(8,128)S(1)} %bitcast.12), channel_id=1, replica_groups=mesh['section'=4,'depth_0'=8,'depth_1'=4,'depth_2'=2] {'depth_0','depth_1'}, dimensions={0} | all-to-all | bytes 524288 | tf_op jit(solution)/shard_map/all_to_all | solution.py:414
  87.5 15.2 %all_to_all.11 = f32[32,16,128]{2,1,0:T(8,128)S(1)} all-to-all(f32[32,16,128]{2,1,0:T(8,128)S(1)} %broadcast_in_dim.2), channel_id=1, replica_groups=mesh['section'=4,'depth_0'=8,'depth_1'=4,'depth_2'=2] {'depth_0','depth_1'}, dimensions={0} | all-to-all | bytes 524288 | tf_op jit(solution)/shard_map/all_to_all | solution.py:417
  102.7 3.0 %collective-permute-start.23 = (f32[512,128]{1,0:T(8,128)S(1)}, f32[512,128]{1,0:T(8,128)S(1)}, u32[]{:S(2)}, u32[]{:S(2)}) collective-permute-start(f32[512,128]{1,0:T(8,128)S(1)} %bitcast.10), channel_id=1, source_target_pairs={{0,1},{1,0},{2,3},{3,2},{4,5},{5,4},{6,7},{7,6},{8,9},{9,8},{10,11... | collective-permute-start | bytes 786440 | tf_op jit(solution)/shard_map/ppermute | solution.py:325
  105.7 0.0 collective-permute-start.14
  105.7 4.3 %collective-permute-start.15 = (f32[1,64,256]{2,1,0:T(8,128)S(1)}, f32[1,64,256]{2,1,0:T(8,128)S(1)}, u32[]{:S(2)}, u32[]{:S(2)}) collective-permute-start(f32[1,64,256]{2,1,0:T(8,128)S(1)} %get-tuple-element.51), channel_id=1, source_target_pairs={{1,2},{3,4},{5,6},{7,8},{9,10},{11,12},{13,14},{15,16},{17,18},{19... | collective-permute-start | bytes 196616 | tf_op jit(solution)/shard_map/ppermute | solution.py:332
  110.0 0.0 collective-permute-done.14.inner_in
  110.1 3.3 %collective-permute-done.15.outer_in = f32[1,64,256]{2,1,0:T(8,128)S(1)} collective-permute-done((f32[1,64,256]{2,1,0:T(8,128)S(1)}, f32[1,64,256]{2,1,0:T(8,128)S(1)}, u32[]{:S(2)}, u32[]{:S(2)}) %collective-permute-start.15) | collective-permute-done | bytes 65568 | tf_op jit(solution)/shard_map/ppermute | solution.py:332
  113.4 0.9 shard_map.57
  114.2 0.1 collective-permute-start.16
  114.3 2.5 %collective-permute-start.17 = (f32[2,64,256]{2,1,0:T(8,128)S(1)}, f32[2,64,256]{2,1,0:T(8,128)S(1)}, u32[]{:S(2)}, u32[]{:S(2)}) collective-permute-start(f32[2,64,256]{2,1,0:T(8,128)S(1)} %get-tuple-element.58), channel_id=1, source_target_pairs={{0,128},{64,192},{128,0},{192,64},{1,129},{65,193},{129,1},{193,65... | collective-permute-start | bytes 393224 | tf_op jit(solution)/shard_map/ppermute | solution.py:317
  116.9 1.3 %collective-permute-start.18 = (f32[2,64,256]{2,1,0:T(8,128)S(1)}, f32[2,64,256]{2,1,0:T(8,128)S(1)}, u32[]{:S(2)}, u32[]{:S(2)}) collective-permute-start(f32[2,64,256]{2,1,0:T(8,128)S(1)} %get-tuple-element.59), channel_id=1, source_target_pairs={{0,192},{64,128},{128,64},{192,0},{1,193},{65,129},{129,65},{193,1... | collective-permute-start | bytes 393224 | tf_op jit(solution)/shard_map/ppermute | solution.py:317
  118.2 1.7 %collective-permute-done.16.x1 = f32[2,64,256]{2,1,0:T(8,128)S(1)} collective-permute-done((f32[2,64,256]{2,1,0:T(8,128)S(1)}, f32[2,64,256]{2,1,0:T(8,128)S(1)}, u32[]{:S(2)}, u32[]{:S(2)}) %collective-permute-start.16) | collective-permute-done | bytes 131104 | tf_op jit(solution)/shard_map/ppermute | solution.py:317
  119.9 2.6 %collective-permute-done.17.x2 = f32[2,64,256]{2,1,0:T(8,128)S(1)} collective-permute-done((f32[2,64,256]{2,1,0:T(8,128)S(1)}, f32[2,64,256]{2,1,0:T(8,128)S(1)}, u32[]{:S(2)}, u32[]{:S(2)}) %collective-permute-start.17) | collective-permute-done | bytes 131104 | tf_op jit(solution)/shard_map/ppermute | solution.py:317
  122.4 2.4 %collective-permute-done.18.x3 = f32[2,64,256]{2,1,0:T(8,128)S(1)} collective-permute-done((f32[2,64,256]{2,1,0:T(8,128)S(1)}, f32[2,64,256]{2,1,0:T(8,128)S(1)}, u32[]{:S(2)}, u32[]{:S(2)}) %collective-permute-start.18) | collective-permute-done | bytes 131104 | tf_op jit(solution)/shard_map/ppermute | solution.py:317
  124.8 0.8 shard_map.58
  125.6 0.0 collective-permute-done.23.other_ref
  125.6 1.1 shard_map.60
  (11 shorter events, 0.1 us)
Async XLA Ops:
  0.6 23.4 %copy-start = (f32[1,4,2,64,256]{4,3,2,1,0:T(8,128)S(1)}, f32[1,4,2,64,256]{4,3,2,1,0:T(8,128)}, u32[]{:S(2)}) copy-start(f32[1,4,2,64,256]{4,3,2,1,0:T(8,128)} %param.3) | copy-start | bytes 1572868
  0.6 1.2 copy-start.1
  2.3 8.1 %collective-permute-start.10 = (f32[96,576]{1,0:T(8,128)S(1)}, f32[96,576]{1,0:T(8,128)S(1)}, u32[]{:S(2)}, u32[]{:S(2)}) collective-permute-start(f32[96,576]{1,0:T(8,128)S(1)} %get-tuple-element.48.mine_ref), channel_id=1, source_target_pairs={{0,192},{64,128},{128,64},{192,0},{1,193},{65,129},{129,65},{193,1... | collective-permute-start | bytes 663560 | tf_op jit(solution)/shard_map/ppermute | solution.py:317
  4.9 6.6 %collective-permute-start.9 = (f32[96,576]{1,0:T(8,128)S(1)}, f32[96,576]{1,0:T(8,128)S(1)}, u32[]{:S(2)}, u32[]{:S(2)}) collective-permute-start(f32[96,576]{1,0:T(8,128)S(1)} %get-tuple-element.48.mine_ref), channel_id=1, source_target_pairs={{0,64},{64,0},{128,192},{192,128},{1,65},{65,1},{129,193},{193,129... | collective-permute-start | bytes 663560 | tf_op jit(solution)/shard_map/ppermute | solution.py:317
  10.5 8.8 %collective-permute-start.11 = (f32[48,576]{1,0:T(8,128)S(1)}, f32[48,576]{1,0:T(8,128)S(1)}, u32[]{:S(2)}, u32[]{:S(2)}) collective-permute-start(f32[48,576]{1,0:T(8,128)S(1)} %slice.8), channel_id=1, source_target_pairs={{0,64},{64,0},{128,192},{192,128},{1,65},{65,1},{129,193},{193,129... | collective-permute-start | bytes 331784 | tf_op jit(solution)/shard_map/ppermute | solution.py:317
  11.5 7.8 %collective-permute-start.12 = (f32[48,576]{1,0:T(8,128)S(1)}, f32[48,576]{1,0:T(8,128)S(1)}, u32[]{:S(2)}, u32[]{:S(2)}) collective-permute-start(f32[48,576]{1,0:T(8,128)S(1)} %slice.9), channel_id=1, source_target_pairs={{0,192},{64,128},{128,64},{192,0},{1,193},{65,129},{129,65},{193,1... | collective-permute-start | bytes 331784 | tf_op jit(solution)/shard_map/ppermute | solution.py:317
  14.3 9.8 %collective-permute-start.1 = (f32[4,64,256]{2,1,0:T(8,128)S(1)}, f32[4,64,256]{2,1,0:T(8,128)S(1)}, u32[]{:S(2)}, u32[]{:S(2)}) collective-permute-start(f32[4,64,256]{2,1,0:T(8,128)S(1)} %get-tuple-element.74), channel_id=1, source_target_pairs={{1,2},{3,4},{5,6},{7,8},{9,10},{11,12},{13,14},{15,16},{17,18},{19... | collective-permute-start | bytes 786440 | tf_op jit(solution)/shard_map/ppermute | solution.py:332
  19.2 4.9 %collective-permute-start = (f32[4,64,256]{2,1,0:T(8,128)S(1)}, f32[4,64,256]{2,1,0:T(8,128)S(1)}, u32[]{:S(2)}, u32[]{:S(2)}) collective-permute-start(f32[4,64,256]{2,1,0:T(8,128)S(1)} %get-tuple-element.75), channel_id=1, source_target_pairs={{0,1},{1,0},{2,3},{3,2},{4,5},{5,4},{6,7},{7,6},{8,9},{9,8},{10,11... | collective-permute-start | bytes 786440 | tf_op jit(solution)/shard_map/ppermute | solution.py:325
  19.4 23.5 %collective-permute-start.13 = (f32[288,576]{1,0:T(8,128)S(1)}, f32[288,576]{1,0:T(8,128)S(1)}, u32[]{:S(2)}, u32[]{:S(2)}) collective-permute-start(f32[288,576]{1,0:T(8,128)S(1)} %pad_maximum_fusion), channel_id=1, source_target_pairs={{0,1},{1,0},{2,3},{3,2},{4,5},{5,4},{6,7},{7,6},{8,9},{9,8},{10,11... | collective-permute-start | bytes 1990664 | tf_op jit(solution)/shard_map/ppermute | solution.py:325
  24.9 9.0 %copy-start.2 = (f32[4,2,64,256]{3,2,1,0:T(8,128)S(1)}, f32[4,2,64,256]{3,2,1,0:T(8,128)}, u32[]{:S(2)}) copy-start(f32[4,2,64,256]{3,2,1,0:T(8,128)} %cot_ref.1) | copy-start | bytes 1572868
  25.0 6.9 %collective-permute-start.3 = (f32[2,64,256]{2,1,0:T(8,128)S(1)}, f32[2,64,256]{2,1,0:T(8,128)S(1)}, u32[]{:S(2)}, u32[]{:S(2)}) collective-permute-start(f32[2,64,256]{2,1,0:T(8,128)S(1)} %get-tuple-element.41), channel_id=1, source_target_pairs={{0,128},{64,192},{128,0},{192,64},{1,129},{65,193},{129,1},{193,65... | collective-permute-start | bytes 393224 | tf_op jit(solution)/shard_map/ppermute | solution.py:317
  27.6 5.6 %collective-permute-start.2 = (f32[2,64,256]{2,1,0:T(8,128)S(1)}, f32[2,64,256]{2,1,0:T(8,128)S(1)}, u32[]{:S(2)}, u32[]{:S(2)}) collective-permute-start(f32[2,64,256]{2,1,0:T(8,128)S(1)} %get-tuple-element.40), channel_id=1, source_target_pairs={{0,64},{64,0},{128,192},{192,128},{1,65},{65,1},{129,193},{193,129... | collective-permute-start | bytes 393224 | tf_op jit(solution)/shard_map/ppermute | solution.py:317
  28.1 5.8 %collective-permute-start.4 = (f32[2,64,256]{2,1,0:T(8,128)S(1)}, f32[2,64,256]{2,1,0:T(8,128)S(1)}, u32[]{:S(2)}, u32[]{:S(2)}) collective-permute-start(f32[2,64,256]{2,1,0:T(8,128)S(1)} %get-tuple-element.42), channel_id=1, source_target_pairs={{0,192},{64,128},{128,64},{192,0},{1,193},{65,129},{129,65},{193,1... | collective-permute-start | bytes 393224 | tf_op jit(solution)/shard_map/ppermute | solution.py:317
  34.0 13.4 %collective-permute-start.5 = (f32[5,64,256]{2,1,0:T(8,128)S(1)}, f32[5,64,256]{2,1,0:T(8,128)S(1)}, u32[]{:S(2)}, u32[]{:S(2)}) collective-permute-start(f32[5,64,256]{2,1,0:T(8,128)S(1)} %get-tuple-element.43), channel_id=1, source_target_pairs={{0,1},{1,0},{2,3},{3,2},{4,5},{5,4},{6,7},{7,6},{8,9},{9,8},{10,11... | collective-permute-start | bytes 983048 | tf_op jit(solution)/shard_map/ppermute | solution.py:325
  35.5 12.0 %collective-permute-start.6 = (f32[5,64,256]{2,1,0:T(8,128)S(1)}, f32[5,64,256]{2,1,0:T(8,128)S(1)}, u32[]{:S(2)}, u32[]{:S(2)}) collective-permute-start(f32[5,64,256]{2,1,0:T(8,128)S(1)} %get-tuple-element.44), channel_id=1, source_target_pairs={{1,2},{3,4},{5,6},{7,8},{9,10},{11,12},{13,14},{15,16},{17,18},{19... | collective-permute-start | bytes 983048 | tf_op jit(solution)/shard_map/ppermute | solution.py:332
  40.2 4.4 %collective-permute-start.7 = (f32[1,64,256]{2,1,0:T(8,128)S(1)}, f32[1,64,256]{2,1,0:T(8,128)S(1)}, u32[]{:S(2)}, u32[]{:S(2)}) collective-permute-start(f32[1,64,256]{2,1,0:T(8,128)S(1)} %get-tuple-element.45), channel_id=1, source_target_pairs={{0,2},{1,3},{4,6},{5,7},{8,10},{9,11},{12,14},{13,15},{16,18},{17,... | collective-permute-start | bytes 196616 | tf_op jit(solution)/shard_map/ppermute | solution.py:341
  40.3 7.1 %collective-permute-start.8 = (f32[1,64,256]{2,1,0:T(8,128)S(1)}, f32[1,64,256]{2,1,0:T(8,128)S(1)}, u32[]{:S(2)}, u32[]{:S(2)}) collective-permute-start(f32[1,64,256]{2,1,0:T(8,128)S(1)} %get-tuple-element.46), channel_id=1, source_target_pairs={{2,4},{3,5},{6,8},{7,9},{10,12},{11,13},{14,16},{15,17},{18,20},{1... | collective-permute-start | bytes 196616 | tf_op jit(solution)/shard_map/ppermute | solution.py:341
  50.8 5.2 %collective-permute-start.19 = (f32[2,64,256]{2,1,0:T(8,128)S(1)}, f32[2,64,256]{2,1,0:T(8,128)S(1)}, u32[]{:S(2)}, u32[]{:S(2)}) collective-permute-start(f32[2,64,256]{2,1,0:T(8,128)S(1)} %get-tuple-element.63), channel_id=1, source_target_pairs={{0,64},{64,0},{128,192},{192,128},{1,65},{65,1},{129,193},{193,129... | collective-permute-start | bytes 393224 | tf_op jit(solution)/shard_map/ppermute | solution.py:317
  51.4 8.5 %collective-permute-start.20 = (f32[2,64,256]{2,1,0:T(8,128)S(1)}, f32[2,64,256]{2,1,0:T(8,128)S(1)}, u32[]{:S(2)}, u32[]{:S(2)}) collective-permute-start(f32[2,64,256]{2,1,0:T(8,128)S(1)} %get-tuple-element.66), channel_id=1, source_target_pairs={{0,128},{64,192},{128,0},{192,64},{1,129},{65,193},{129,1},{193,65... | collective-permute-start | bytes 393224 | tf_op jit(solution)/shard_map/ppermute | solution.py:317
  53.7 8.8 %collective-permute-start.21 = (f32[2,64,256]{2,1,0:T(8,128)S(1)}, f32[2,64,256]{2,1,0:T(8,128)S(1)}, u32[]{:S(2)}, u32[]{:S(2)}) collective-permute-start(f32[2,64,256]{2,1,0:T(8,128)S(1)} %get-tuple-element.69), channel_id=1, source_target_pairs={{0,192},{64,128},{128,64},{192,0},{1,193},{65,129},{129,65},{193,1... | collective-permute-start | bytes 393224 | tf_op jit(solution)/shard_map/ppermute | solution.py:317
  64.8 2.1 %collective-permute-start.22 = (f32[512,128]{1,0:T(8,128)S(1)}, f32[512,128]{1,0:T(8,128)S(1)}, u32[]{:S(2)}, u32[]{:S(2)}) collective-permute-start(f32[512,128]{1,0:T(8,128)S(1)} %get-tuple-element.73), channel_id=1, source_target_pairs={{0,1},{1,0},{2,3},{3,2},{4,5},{5,4},{6,7},{7,6},{8,9},{9,8},{10,11... | collective-permute-start | bytes 786440 | tf_op jit(solution)/shard_map/ppermute | solution.py:325
  102.7 22.9 %collective-permute-start.23 = (f32[512,128]{1,0:T(8,128)S(1)}, f32[512,128]{1,0:T(8,128)S(1)}, u32[]{:S(2)}, u32[]{:S(2)}) collective-permute-start(f32[512,128]{1,0:T(8,128)S(1)} %bitcast.10), channel_id=1, source_target_pairs={{0,1},{1,0},{2,3},{3,2},{4,5},{5,4},{6,7},{7,6},{8,9},{9,8},{10,11... | collective-permute-start | bytes 786440 | tf_op jit(solution)/shard_map/ppermute | solution.py:325
  105.7 4.4 %collective-permute-start.14 = (f32[1,64,256]{2,1,0:T(8,128)S(1)}, f32[1,64,256]{2,1,0:T(8,128)S(1)}, u32[]{:S(2)}, u32[]{:S(2)}) collective-permute-start(f32[1,64,256]{2,1,0:T(8,128)S(1)} %get-tuple-element.50), channel_id=1, source_target_pairs={{0,1},{1,0},{2,3},{3,2},{4,5},{5,4},{6,7},{7,6},{8,9},{9,8},{10,11... | collective-permute-start | bytes 196616 | tf_op jit(solution)/shard_map/ppermute | solution.py:325
  105.7 7.7 %collective-permute-start.15 = (f32[1,64,256]{2,1,0:T(8,128)S(1)}, f32[1,64,256]{2,1,0:T(8,128)S(1)}, u32[]{:S(2)}, u32[]{:S(2)}) collective-permute-start(f32[1,64,256]{2,1,0:T(8,128)S(1)} %get-tuple-element.51), channel_id=1, source_target_pairs={{1,2},{3,4},{5,6},{7,8},{9,10},{11,12},{13,14},{15,16},{17,18},{19... | collective-permute-start | bytes 196616 | tf_op jit(solution)/shard_map/ppermute | solution.py:332
  114.2 5.6 %collective-permute-start.16 = (f32[2,64,256]{2,1,0:T(8,128)S(1)}, f32[2,64,256]{2,1,0:T(8,128)S(1)}, u32[]{:S(2)}, u32[]{:S(2)}) collective-permute-start(f32[2,64,256]{2,1,0:T(8,128)S(1)} %get-tuple-element.57), channel_id=1, source_target_pairs={{0,64},{64,0},{128,192},{192,128},{1,65},{65,1},{129,193},{193,129... | collective-permute-start | bytes 393224 | tf_op jit(solution)/shard_map/ppermute | solution.py:317
  114.3 8.1 %collective-permute-start.17 = (f32[2,64,256]{2,1,0:T(8,128)S(1)}, f32[2,64,256]{2,1,0:T(8,128)S(1)}, u32[]{:S(2)}, u32[]{:S(2)}) collective-permute-start(f32[2,64,256]{2,1,0:T(8,128)S(1)} %get-tuple-element.58), channel_id=1, source_target_pairs={{0,128},{64,192},{128,0},{192,64},{1,129},{65,193},{129,1},{193,65... | collective-permute-start | bytes 393224 | tf_op jit(solution)/shard_map/ppermute | solution.py:317
  116.9 7.9 %collective-permute-start.18 = (f32[2,64,256]{2,1,0:T(8,128)S(1)}, f32[2,64,256]{2,1,0:T(8,128)S(1)}, u32[]{:S(2)}, u32[]{:S(2)}) collective-permute-start(f32[2,64,256]{2,1,0:T(8,128)S(1)} %get-tuple-element.59), channel_id=1, source_target_pairs={{0,192},{64,128},{128,64},{192,0},{1,193},{65,129},{129,65},{193,1... | collective-permute-start | bytes 393224 | tf_op jit(solution)/shard_map/ppermute | solution.py:317

commit v4 on v3

--- a/solution.py
+++ b/solution.py
@@ -239,26 +239,27 @@
             p[d] = chosen(m ^ k, (ig0, ig1, ig2, ig3), d)
 
 
-def filter_term(ref, vh_ref, vl_ref):
-    nt = (((1,), (1,)), ((), ()))
-    total = None
-    for d in range(2):
-        x = ref[d]
-        high, low = split(jnp.concatenate([up(x), x, down(x)], axis=0))
-        right_high = vh_ref[d : d + 3].reshape(576, 256)
-        right_low = vl_ref[d : d + 3].reshape(576, 256)
-        first = lax.dot_general(jnp.concatenate([high, low], axis=0), right_high, nt, preferred_element_type=F32)
-        z = first[:192] + first[192:] + lax.dot_general(high, right_low, nt, preferred_element_type=F32)
-        total = z if total is None else total + z
-    return total
-
-
 def filter_body(*refs):
     keep_ref, send_ref, acc = refs[12:]
     c = core()
+    nt = (((1,), (1,)), ((), ()))
+    both, high_only, right_high, right_low = [], [], [], []
     for k in range(N):
-        term = filter_term(*refs[3 * k : 3 * k + 3])
-        acc[...] = term if k == 0 else acc[...] + term
+        ref, vh_ref, vl_ref = refs[3 * k : 3 * k + 3]
+        for d in range(2):
+            x = ref[d]
+            high, low = split(jnp.concatenate([up(x), x, down(x)], axis=0))
+            both.append(jnp.concatenate([high, low], axis=0))
+            high_only.append(high)
+            right_high.append(vh_ref[d : d + 3].reshape(576, 256))
+            right_low.append(vl_ref[d : d + 3].reshape(576, 256))
+    first = lax.dot_general(
+        jnp.concatenate(both, axis=1), jnp.concatenate(right_high, axis=1), nt, preferred_element_type=F32
+    )
+    second = lax.dot_general(
+        jnp.concatenate(high_only, axis=1), jnp.concatenate(right_low, axis=1), nt, preferred_element_type=F32
+    )
+    acc[...] = first[:192] + first[192:] + second
 
     def piece(row, size):
         if row < 768:

time: 127 us -> 127 us (level)
  no operation moved by 1% of the time
where the time goes in v4:
time: 127 us
  starting transfers between devices  38.4 us (30%)
  waiting for transfers between devices  36.9 us (29%)
  blocking collectives  35.7 us (28%)
  Pallas kernels  12.4 us (10%)
  local copies, waits for them, and re-layouts  2.34 us (2%)
    ppermute x13, waiting for transfers between devices, met(): return lax.ppermute(x, 'section', [(i, i ^ k) for i in range(N)])  24 us
    all_to_all x1, blocking collectives, window(): part = lax.all_to_all(part, PLANE, 0, 0, tiled=True)  20.4 us
    ppermute x13, starting transfers between devices, met(): return lax.ppermute(x, 'section', [(i, i ^ k) for i in range(N)])  15.8 us
    all_to_all x1, blocking collectives, window(): lax.all_to_all(jnp.broadcast_to(total[None], (32, 16, 128)), PLANE, 0, 0,...  15.2 us
    ppermute x3, starting transfers between devices, neighbours(): outer = lax.ppermute(outer, DEPTH, pairs + [(j, i) for i, j in pairs])  14 us
    pallas_call x11, Pallas kernels, run(): pl.pallas_call(body, out_shape=[jax.ShapeDtypeStruct(s, t) for s, t in ou...  12.4 us
    ppermute x3, waiting for transfers between devices, neighbours(): outer = lax.ppermute(outer, DEPTH, pairs + [(j, i) for i, j in pairs])  7.48 us
    ppermute x6, starting transfers between devices, swapped(): return lax.ppermute(x, CORE, [(0, 1), (1, 0)])  5.98 us
  transfers between devices with their start and end apart: 24, of which 16 were waited for; matrix products, arithmetic and copies ran while one was open for 1% of the time, Pallas kernels for 4%

profile of v4, /device:TPU:25, one launch (start us, length us, event | category | flops | bytes accessed | tf_op | source)
XLA Modules:
  0.0 126.7 jit_solution(11414656720907761478)
XLA Ops:
  0.6 0.0 copy-start
  0.7 1.2 copy-done.1
  1.9 0.5 shard_map.50
  2.3 2.6 %collective-permute-start.10 = (f32[96,576]{1,0:T(8,128)S(1)}, f32[96,576]{1,0:T(8,128)S(1)}, u32[]{:S(2)}, u32[]{:S(2)}) collective-permute-start(f32[96,576]{1,0:T(8,128)S(1)} %get-tuple-element.48.mine_ref), channel_id=1, source_target_pairs={{0,192},{64,128},{128,64},{192,0},{1,193},{65,129},{129,65},{193,1... | collective-permute-start | bytes 663560 | tf_op jit(solution)/shard_map/ppermute | solution.py:318
  4.9 0.0 collective-permute-start.9
  4.9 5.6 %collective-permute-done.10.three_ref = f32[96,576]{1,0:T(8,128)S(1)} collective-permute-done((f32[96,576]{1,0:T(8,128)S(1)}, f32[96,576]{1,0:T(8,128)S(1)}, u32[]{:S(2)}, u32[]{:S(2)}) %collective-permute-start.10) | collective-permute-done | bytes 221216 | tf_op jit(solution)/shard_map/ppermute | solution.py:318
  10.5 0.1 collective-permute-start.11
  10.6 0.9 collective-permute-done.9.one_ref
  11.5 1.7 %collective-permute-start.12 = (f32[48,576]{1,0:T(8,128)S(1)}, f32[48,576]{1,0:T(8,128)S(1)}, u32[]{:S(2)}, u32[]{:S(2)}) collective-permute-start(f32[48,576]{1,0:T(8,128)S(1)} %slice.9), channel_id=1, source_target_pairs={{0,192},{64,128},{128,64},{192,0},{1,193},{65,129},{129,65},{193,1... | collective-permute-start | bytes 331784 | tf_op jit(solution)/shard_map/ppermute | solution.py:318
  13.2 1.1 dynamic-slice_bitcast_fusion
  14.3 4.9 %collective-permute-start.1 = (f32[4,64,256]{2,1,0:T(8,128)S(1)}, f32[4,64,256]{2,1,0:T(8,128)S(1)}, u32[]{:S(2)}, u32[]{:S(2)}) collective-permute-start(f32[4,64,256]{2,1,0:T(8,128)S(1)} %get-tuple-element.74), channel_id=1, source_target_pairs={{1,2},{3,4},{5,6},{7,8},{9,10},{11,12},{13,14},{15,16},{17,18},{19... | collective-permute-start | bytes 786440 | tf_op jit(solution)/shard_map/ppermute | solution.py:333
  19.2 0.1 collective-permute-start
  19.3 0.0 collective-permute-done.11.far0_ref
  19.3 0.0 collective-permute-done.12.far1_ref
  19.3 0.1 pad_maximum_fusion
  19.4 0.6 collective-permute-start.13
  19.9 4.2 %collective-permute-done.1.outer_ref = f32[4,64,256]{2,1,0:T(8,128)S(1)} collective-permute-done((f32[4,64,256]{2,1,0:T(8,128)S(1)}, f32[4,64,256]{2,1,0:T(8,128)S(1)}, u32[]{:S(2)}, u32[]{:S(2)}) %collective-permute-start.1) | collective-permute-done | bytes 262176 | tf_op jit(solution)/shard_map/ppermute | solution.py:333
  24.1 0.0 collective-permute-done.inner_ref
  24.1 0.9 shard_map.53
  24.9 0.0 copy-start.2
  25.0 1.3 %collective-permute-start.3 = (f32[2,64,256]{2,1,0:T(8,128)S(1)}, f32[2,64,256]{2,1,0:T(8,128)S(1)}, u32[]{:S(2)}, u32[]{:S(2)}) collective-permute-start(f32[2,64,256]{2,1,0:T(8,128)S(1)} %get-tuple-element.41), channel_id=1, source_target_pairs={{0,128},{64,192},{128,0},{192,64},{1,129},{65,193},{129,1},{193,65... | collective-permute-start | bytes 393224 | tf_op jit(solution)/shard_map/ppermute | solution.py:318
  26.2 1.3 %shard_map.52 = (f32[2,64,256]{2,1,0:T(8,128)S(1)}, bf16[4,192,256]{2,1,0:T(8,128)(2,1)S(1)}, bf16[4,192,256]{2,1,0:T(8,128)(2,1)S(1)}, f32[2,64,256]{2,1,0:T(8,...) custom-call(f32[4,2,64,256]{3,2,1,0:T(8,128)S(1)} %bitcast.8, ...), custom_call_target="tpu_custom_call" | custom-call | flops 679477248 | bytes 1490944 | tf_op jit(solution)/shard_map/pallas_call | solution.py:28
  27.6 0.5 collective-permute-start.2
  28.1 1.7 %collective-permute-start.4 = (f32[2,64,256]{2,1,0:T(8,128)S(1)}, f32[2,64,256]{2,1,0:T(8,128)S(1)}, u32[]{:S(2)}, u32[]{:S(2)}) collective-permute-start(f32[2,64,256]{2,1,0:T(8,128)S(1)} %get-tuple-element.42), channel_id=1, source_target_pairs={{0,192},{64,128},{128,64},{192,0},{1,193},{65,129},{129,65},{193,1... | collective-permute-start | bytes 393224 | tf_op jit(solution)/shard_map/ppermute | solution.py:318
  29.8 0.9 shard_map.51
  30.7 1.3 collective-permute-done.3.d2
  31.9 1.2 collective-permute-done.2.d1
  33.2 0.8 collective-permute-done.4.d3
  33.9 0.1 shard_map.54
  34.0 1.4 %collective-permute-start.5 = (f32[5,64,256]{2,1,0:T(8,128)S(1)}, f32[5,64,256]{2,1,0:T(8,128)S(1)}, u32[]{:S(2)}, u32[]{:S(2)}) collective-permute-start(f32[5,64,256]{2,1,0:T(8,128)S(1)} %get-tuple-element.43), channel_id=1, source_target_pairs={{0,1},{1,0},{2,3},{3,2},{4,5},{5,4},{6,7},{7,6},{8,9},{9,8},{10,11... | collective-permute-start | bytes 983048 | tf_op jit(solution)/shard_map/ppermute | solution.py:326
  35.5 4.7 %collective-permute-start.6 = (f32[5,64,256]{2,1,0:T(8,128)S(1)}, f32[5,64,256]{2,1,0:T(8,128)S(1)}, u32[]{:S(2)}, u32[]{:S(2)}) collective-permute-start(f32[5,64,256]{2,1,0:T(8,128)S(1)} %get-tuple-element.44), channel_id=1, source_target_pairs={{1,2},{3,4},{5,6},{7,8},{9,10},{11,12},{13,14},{15,16},{17,18},{19... | collective-permute-start | bytes 983048 | tf_op jit(solution)/shard_map/ppermute | solution.py:333
  40.2 0.1 collective-permute-start.7
  40.3 2.5 %collective-permute-start.8 = (f32[1,64,256]{2,1,0:T(8,128)S(1)}, f32[1,64,256]{2,1,0:T(8,128)S(1)}, u32[]{:S(2)}, u32[]{:S(2)}) collective-permute-start(f32[1,64,256]{2,1,0:T(8,128)S(1)} %get-tuple-element.46), channel_id=1, source_target_pairs={{2,4},{3,5},{6,8},{7,9},{10,12},{11,13},{14,16},{15,17},{18,20},{1... | collective-permute-start | bytes 196616 | tf_op jit(solution)/shard_map/ppermute | solution.py:342
  42.9 0.0 collective-permute-done.13.other_ref
  42.9 0.3 shard_map.55.taps_ref
  43.2 1.4 %collective-permute-done.7.one_in = f32[1,64,256]{2,1,0:T(8,128)S(1)} collective-permute-done((f32[1,64,256]{2,1,0:T(8,128)S(1)}, f32[1,64,256]{2,1,0:T(8,128)S(1)}, u32[]{:S(2)}, u32[]{:S(2)}) %collective-permute-start.7) | collective-permute-done | bytes 65568 | tf_op jit(solution)/shard_map/ppermute | solution.py:342
  44.6 2.9 %collective-permute-done.8.two_in = f32[1,64,256]{2,1,0:T(8,128)S(1)} collective-permute-done((f32[1,64,256]{2,1,0:T(8,128)S(1)}, f32[1,64,256]{2,1,0:T(8,128)S(1)}, u32[]{:S(2)}, u32[]{:S(2)}) %collective-permute-start.8) | collective-permute-done | bytes 65568 | tf_op jit(solution)/shard_map/ppermute | solution.py:342
  47.4 0.0 collective-permute-done.5.inner_in
  47.4 3.4 %shard_map.56 = (f32[2,64,256]{2,1,0:T(8,128)S(1)}, f32[2,64,256]{2,1,0:T(8,128)S(1)}, f32[2,64,256]{2,1,0:T(8,128)S(1)}, f32[2,64,256]{2,1,0:T(8,128)S(1)}, f32...) custom-call(f32[5,64,256]{2,1,0:T(8,128)S(1)} %collective-permute-do, ...), custom_call_target="tpu_custom_call" | custom-call | flops 2038431744 | bytes 3211264 | tf_op jit(solution)/shard_map/pallas_call | solution.py:28
  50.8 0.6 collective-permute-start.19
  51.4 2.2 %collective-permute-start.20 = (f32[2,64,256]{2,1,0:T(8,128)S(1)}, f32[2,64,256]{2,1,0:T(8,128)S(1)}, u32[]{:S(2)}, u32[]{:S(2)}) collective-permute-start(f32[2,64,256]{2,1,0:T(8,128)S(1)} %get-tuple-element.66), channel_id=1, source_target_pairs={{0,128},{64,192},{128,0},{192,64},{1,129},{65,193},{129,1},{193,65... | collective-permute-start | bytes 393224 | tf_op jit(solution)/shard_map/ppermute | solution.py:318
  53.7 1.1 collective-permute-start.21
  54.8 1.3 %collective-permute-done.19.refs_3_ = f32[2,64,256]{2,1,0:T(8,128)S(1)} collective-permute-done((f32[2,64,256]{2,1,0:T(8,128)S(1)}, f32[2,64,256]{2,1,0:T(8,128)S(1)}, u32[]{:S(2)}, u32[]{:S(2)}) %collective-permute-start.19) | collective-permute-done | bytes 131104 | tf_op jit(solution)/shard_map/ppermute | solution.py:318
  56.1 3.9 %collective-permute-done.20.refs_6_ = f32[2,64,256]{2,1,0:T(8,128)S(1)} collective-permute-done((f32[2,64,256]{2,1,0:T(8,128)S(1)}, f32[2,64,256]{2,1,0:T(8,128)S(1)}, u32[]{:S(2)}, u32[]{:S(2)}) %collective-permute-start.20) | collective-permute-done | bytes 131104 | tf_op jit(solution)/shard_map/ppermute | solution.py:318
  60.0 2.5 %collective-permute-done.21.refs_9_ = f32[2,64,256]{2,1,0:T(8,128)S(1)} collective-permute-done((f32[2,64,256]{2,1,0:T(8,128)S(1)}, f32[2,64,256]{2,1,0:T(8,128)S(1)}, u32[]{:S(2)}, u32[]{:S(2)}) %collective-permute-start.21) | collective-permute-done | bytes 131104 | tf_op jit(solution)/shard_map/ppermute | solution.py:318
  62.5 2.3 %shard_map.59 = (f32[512,128]{1,0:T(8,128)S(1)}, f32[512,128]{1,0:T(8,128)S(1)}) custom-call(f32[2,64,256]{2,1,0:T(8,128)S(1)} %get-tuple-element.60.refs_0_, bf16[4,192,256]{2,1,0:T(8,128)(2,1)S(1)} %get-tuple-element.61.refs_1_, bf16[4,192,256]{2,1,0:T(8,128)(2,1)S(1)} %get-tuple-element.62.refs_2_, f32[2,64,256]{2,1,0:T(8,128)S(1)} %collective-permute-done.19.refs_3_, ...), custom_call_target="tpu_custom_call" | custom-call | flops 1358954496 | bytes 3670016 | tf_op jit(solution)/shard_map/pallas_call | solution.py:28
  64.8 0.9 collective-permute-start.22
  65.7 1.2 collective-permute-done.22
  66.9 20.4 %all_to_all.10 = f32[32,16,128]{2,1,0:T(8,128)S(1)} all-to-all(f32[32,16,128]{2,1,0:T(8,128)S(1)} %bitcast.12), channel_id=1, replica_groups=mesh['section'=4,'depth_0'=8,'depth_1'=4,'depth_2'=2] {'depth_0','depth_1'}, dimensions={0} | all-to-all | bytes 524288 | tf_op jit(solution)/shard_map/all_to_all | solution.py:415
  87.5 15.2 %all_to_all.11 = f32[32,16,128]{2,1,0:T(8,128)S(1)} all-to-all(f32[32,16,128]{2,1,0:T(8,128)S(1)} %broadcast_in_dim.2), channel_id=1, replica_groups=mesh['section'=4,'depth_0'=8,'depth_1'=4,'depth_2'=2] {'depth_0','depth_1'}, dimensions={0} | all-to-all | bytes 524288 | tf_op jit(solution)/shard_map/all_to_all | solution.py:418
  102.7 3.0 %collective-permute-start.23 = (f32[512,128]{1,0:T(8,128)S(1)}, f32[512,128]{1,0:T(8,128)S(1)}, u32[]{:S(2)}, u32[]{:S(2)}) collective-permute-start(f32[512,128]{1,0:T(8,128)S(1)} %bitcast.10), channel_id=1, source_target_pairs={{0,1},{1,0},{2,3},{3,2},{4,5},{5,4},{6,7},{7,6},{8,9},{9,8},{10,11... | collective-permute-start | bytes 786440 | tf_op jit(solution)/shard_map/ppermute | solution.py:326
  105.7 0.0 collective-permute-start.14
  105.7 4.3 %collective-permute-start.15 = (f32[1,64,256]{2,1,0:T(8,128)S(1)}, f32[1,64,256]{2,1,0:T(8,128)S(1)}, u32[]{:S(2)}, u32[]{:S(2)}) collective-permute-start(f32[1,64,256]{2,1,0:T(8,128)S(1)} %get-tuple-element.51), channel_id=1, source_target_pairs={{1,2},{3,4},{5,6},{7,8},{9,10},{11,12},{13,14},{15,16},{17,18},{19... | collective-permute-start | bytes 196616 | tf_op jit(solution)/shard_map/ppermute | solution.py:333
  110.0 0.0 collective-permute-done.14.inner_in
  110.0 3.3 %collective-permute-done.15.outer_in = f32[1,64,256]{2,1,0:T(8,128)S(1)} collective-permute-done((f32[1,64,256]{2,1,0:T(8,128)S(1)}, f32[1,64,256]{2,1,0:T(8,128)S(1)}, u32[]{:S(2)}, u32[]{:S(2)}) %collective-permute-start.15) | collective-permute-done | bytes 65568 | tf_op jit(solution)/shard_map/ppermute | solution.py:333
  113.3 0.9 shard_map.57
  114.2 0.1 collective-permute-start.16
  114.3 2.5 %collective-permute-start.17 = (f32[2,64,256]{2,1,0:T(8,128)S(1)}, f32[2,64,256]{2,1,0:T(8,128)S(1)}, u32[]{:S(2)}, u32[]{:S(2)}) collective-permute-start(f32[2,64,256]{2,1,0:T(8,128)S(1)} %get-tuple-element.58), channel_id=1, source_target_pairs={{0,128},{64,192},{128,0},{192,64},{1,129},{65,193},{129,1},{193,65... | collective-permute-start | bytes 393224 | tf_op jit(solution)/shard_map/ppermute | solution.py:318
  116.9 1.3 %collective-permute-start.18 = (f32[2,64,256]{2,1,0:T(8,128)S(1)}, f32[2,64,256]{2,1,0:T(8,128)S(1)}, u32[]{:S(2)}, u32[]{:S(2)}) collective-permute-start(f32[2,64,256]{2,1,0:T(8,128)S(1)} %get-tuple-element.59), channel_id=1, source_target_pairs={{0,192},{64,128},{128,64},{192,0},{1,193},{65,129},{129,65},{193,1... | collective-permute-start | bytes 393224 | tf_op jit(solution)/shard_map/ppermute | solution.py:318
  118.2 1.7 %collective-permute-done.16.x1 = f32[2,64,256]{2,1,0:T(8,128)S(1)} collective-permute-done((f32[2,64,256]{2,1,0:T(8,128)S(1)}, f32[2,64,256]{2,1,0:T(8,128)S(1)}, u32[]{:S(2)}, u32[]{:S(2)}) %collective-permute-start.16) | collective-permute-done | bytes 131104 | tf_op jit(solution)/shard_map/ppermute | solution.py:318
  119.8 2.6 %collective-permute-done.17.x2 = f32[2,64,256]{2,1,0:T(8,128)S(1)} collective-permute-done((f32[2,64,256]{2,1,0:T(8,128)S(1)}, f32[2,64,256]{2,1,0:T(8,128)S(1)}, u32[]{:S(2)}, u32[]{:S(2)}) %collective-permute-start.17) | collective-permute-done | bytes 131104 | tf_op jit(solution)/shard_map/ppermute | solution.py:318
  122.4 2.4 %collective-permute-done.18.x3 = f32[2,64,256]{2,1,0:T(8,128)S(1)} collective-permute-done((f32[2,64,256]{2,1,0:T(8,128)S(1)}, f32[2,64,256]{2,1,0:T(8,128)S(1)}, u32[]{:S(2)}, u32[]{:S(2)}) %collective-permute-start.18) | collective-permute-done | bytes 131104 | tf_op jit(solution)/shard_map/ppermute | solution.py:318
  124.7 0.8 shard_map.58
  125.6 1.1 shard_map.60
  (11 shorter events, 0.1 us)
Async XLA Ops:
  0.6 23.4 %copy-start = (f32[1,4,2,64,256]{4,3,2,1,0:T(8,128)S(1)}, f32[1,4,2,64,256]{4,3,2,1,0:T(8,128)}, u32[]{:S(2)}) copy-start(f32[1,4,2,64,256]{4,3,2,1,0:T(8,128)} %param.3) | copy-start | bytes 1572868
  0.6 1.2 copy-start.1
  2.3 8.1 %collective-permute-start.10 = (f32[96,576]{1,0:T(8,128)S(1)}, f32[96,576]{1,0:T(8,128)S(1)}, u32[]{:S(2)}, u32[]{:S(2)}) collective-permute-start(f32[96,576]{1,0:T(8,128)S(1)} %get-tuple-element.48.mine_ref), channel_id=1, source_target_pairs={{0,192},{64,128},{128,64},{192,0},{1,193},{65,129},{129,65},{193,1... | collective-permute-start | bytes 663560 | tf_op jit(solution)/shard_map/ppermute | solution.py:318
  4.9 6.6 %collective-permute-start.9 = (f32[96,576]{1,0:T(8,128)S(1)}, f32[96,576]{1,0:T(8,128)S(1)}, u32[]{:S(2)}, u32[]{:S(2)}) collective-permute-start(f32[96,576]{1,0:T(8,128)S(1)} %get-tuple-element.48.mine_ref), channel_id=1, source_target_pairs={{0,64},{64,0},{128,192},{192,128},{1,65},{65,1},{129,193},{193,129... | collective-permute-start | bytes 663560 | tf_op jit(solution)/shard_map/ppermute | solution.py:318
  10.5 8.8 %collective-permute-start.11 = (f32[48,576]{1,0:T(8,128)S(1)}, f32[48,576]{1,0:T(8,128)S(1)}, u32[]{:S(2)}, u32[]{:S(2)}) collective-permute-start(f32[48,576]{1,0:T(8,128)S(1)} %slice.8), channel_id=1, source_target_pairs={{0,64},{64,0},{128,192},{192,128},{1,65},{65,1},{129,193},{193,129... | collective-permute-start | bytes 331784 | tf_op jit(solution)/shard_map/ppermute | solution.py:318
  11.5 7.8 %collective-permute-start.12 = (f32[48,576]{1,0:T(8,128)S(1)}, f32[48,576]{1,0:T(8,128)S(1)}, u32[]{:S(2)}, u32[]{:S(2)}) collective-permute-start(f32[48,576]{1,0:T(8,128)S(1)} %slice.9), channel_id=1, source_target_pairs={{0,192},{64,128},{128,64},{192,0},{1,193},{65,129},{129,65},{193,1... | collective-permute-start | bytes 331784 | tf_op jit(solution)/shard_map/ppermute | solution.py:318
  14.3 9.8 %collective-permute-start.1 = (f32[4,64,256]{2,1,0:T(8,128)S(1)}, f32[4,64,256]{2,1,0:T(8,128)S(1)}, u32[]{:S(2)}, u32[]{:S(2)}) collective-permute-start(f32[4,64,256]{2,1,0:T(8,128)S(1)} %get-tuple-element.74), channel_id=1, source_target_pairs={{1,2},{3,4},{5,6},{7,8},{9,10},{11,12},{13,14},{15,16},{17,18},{19... | collective-permute-start | bytes 786440 | tf_op jit(solution)/shard_map/ppermute | solution.py:333
  19.2 4.9 %collective-permute-start = (f32[4,64,256]{2,1,0:T(8,128)S(1)}, f32[4,64,256]{2,1,0:T(8,128)S(1)}, u32[]{:S(2)}, u32[]{:S(2)}) collective-permute-start(f32[4,64,256]{2,1,0:T(8,128)S(1)} %get-tuple-element.75), channel_id=1, source_target_pairs={{0,1},{1,0},{2,3},{3,2},{4,5},{5,4},{6,7},{7,6},{8,9},{9,8},{10,11... | collective-permute-start | bytes 786440 | tf_op jit(solution)/shard_map/ppermute | solution.py:326
  19.4 23.5 %collective-permute-start.13 = (f32[288,576]{1,0:T(8,128)S(1)}, f32[288,576]{1,0:T(8,128)S(1)}, u32[]{:S(2)}, u32[]{:S(2)}) collective-permute-start(f32[288,576]{1,0:T(8,128)S(1)} %pad_maximum_fusion), channel_id=1, source_target_pairs={{0,1},{1,0},{2,3},{3,2},{4,5},{5,4},{6,7},{7,6},{8,9},{9,8},{10,11... | collective-permute-start | bytes 1990664 | tf_op jit(solution)/shard_map/ppermute | solution.py:326
  24.9 9.0 %copy-start.2 = (f32[4,2,64,256]{3,2,1,0:T(8,128)S(1)}, f32[4,2,64,256]{3,2,1,0:T(8,128)}, u32[]{:S(2)}) copy-start(f32[4,2,64,256]{3,2,1,0:T(8,128)} %cot_ref.1) | copy-start | bytes 1572868
  25.0 6.9 %collective-permute-start.3 = (f32[2,64,256]{2,1,0:T(8,128)S(1)}, f32[2,64,256]{2,1,0:T(8,128)S(1)}, u32[]{:S(2)}, u32[]{:S(2)}) collective-permute-start(f32[2,64,256]{2,1,0:T(8,128)S(1)} %get-tuple-element.41), channel_id=1, source_target_pairs={{0,128},{64,192},{128,0},{192,64},{1,129},{65,193},{129,1},{193,65... | collective-permute-start | bytes 393224 | tf_op jit(solution)/shard_map/ppermute | solution.py:318
  27.6 5.6 %collective-permute-start.2 = (f32[2,64,256]{2,1,0:T(8,128)S(1)}, f32[2,64,256]{2,1,0:T(8,128)S(1)}, u32[]{:S(2)}, u32[]{:S(2)}) collective-permute-start(f32[2,64,256]{2,1,0:T(8,128)S(1)} %get-tuple-element.40), channel_id=1, source_target_pairs={{0,64},{64,0},{128,192},{192,128},{1,65},{65,1},{129,193},{193,129... | collective-permute-start | bytes 393224 | tf_op jit(solution)/shard_map/ppermute | solution.py:318
  28.1 5.8 %collective-permute-start.4 = (f32[2,64,256]{2,1,0:T(8,128)S(1)}, f32[2,64,256]{2,1,0:T(8,128)S(1)}, u32[]{:S(2)}, u32[]{:S(2)}) collective-permute-start(f32[2,64,256]{2,1,0:T(8,128)S(1)} %get-tuple-element.42), channel_id=1, source_target_pairs={{0,192},{64,128},{128,64},{192,0},{1,193},{65,129},{129,65},{193,1... | collective-permute-start | bytes 393224 | tf_op jit(solution)/shard_map/ppermute | solution.py:318
  34.0 13.4 %collective-permute-start.5 = (f32[5,64,256]{2,1,0:T(8,128)S(1)}, f32[5,64,256]{2,1,0:T(8,128)S(1)}, u32[]{:S(2)}, u32[]{:S(2)}) collective-permute-start(f32[5,64,256]{2,1,0:T(8,128)S(1)} %get-tuple-element.43), channel_id=1, source_target_pairs={{0,1},{1,0},{2,3},{3,2},{4,5},{5,4},{6,7},{7,6},{8,9},{9,8},{10,11... | collective-permute-start | bytes 983048 | tf_op jit(solution)/shard_map/ppermute | solution.py:326
  35.5 12.0 %collective-permute-start.6 = (f32[5,64,256]{2,1,0:T(8,128)S(1)}, f32[5,64,256]{2,1,0:T(8,128)S(1)}, u32[]{:S(2)}, u32[]{:S(2)}) collective-permute-start(f32[5,64,256]{2,1,0:T(8,128)S(1)} %get-tuple-element.44), channel_id=1, source_target_pairs={{1,2},{3,4},{5,6},{7,8},{9,10},{11,12},{13,14},{15,16},{17,18},{19... | collective-permute-start | bytes 983048 | tf_op jit(solution)/shard_map/ppermute | solution.py:333
  40.2 4.4 %collective-permute-start.7 = (f32[1,64,256]{2,1,0:T(8,128)S(1)}, f32[1,64,256]{2,1,0:T(8,128)S(1)}, u32[]{:S(2)}, u32[]{:S(2)}) collective-permute-start(f32[1,64,256]{2,1,0:T(8,128)S(1)} %get-tuple-element.45), channel_id=1, source_target_pairs={{0,2},{1,3},{4,6},{5,7},{8,10},{9,11},{12,14},{13,15},{16,18},{17,... | collective-permute-start | bytes 196616 | tf_op jit(solution)/shard_map/ppermute | solution.py:342
  40.3 7.1 %collective-permute-start.8 = (f32[1,64,256]{2,1,0:T(8,128)S(1)}, f32[1,64,256]{2,1,0:T(8,128)S(1)}, u32[]{:S(2)}, u32[]{:S(2)}) collective-permute-start(f32[1,64,256]{2,1,0:T(8,128)S(1)} %get-tuple-element.46), channel_id=1, source_target_pairs={{2,4},{3,5},{6,8},{7,9},{10,12},{11,13},{14,16},{15,17},{18,20},{1... | collective-permute-start | bytes 196616 | tf_op jit(solution)/shard_map/ppermute | solution.py:342
  50.8 5.2 %collective-permute-start.19 = (f32[2,64,256]{2,1,0:T(8,128)S(1)}, f32[2,64,256]{2,1,0:T(8,128)S(1)}, u32[]{:S(2)}, u32[]{:S(2)}) collective-permute-start(f32[2,64,256]{2,1,0:T(8,128)S(1)} %get-tuple-element.63), channel_id=1, source_target_pairs={{0,64},{64,0},{128,192},{192,128},{1,65},{65,1},{129,193},{193,129... | collective-permute-start | bytes 393224 | tf_op jit(solution)/shard_map/ppermute | solution.py:318
  51.4 8.5 %collective-permute-start.20 = (f32[2,64,256]{2,1,0:T(8,128)S(1)}, f32[2,64,256]{2,1,0:T(8,128)S(1)}, u32[]{:S(2)}, u32[]{:S(2)}) collective-permute-start(f32[2,64,256]{2,1,0:T(8,128)S(1)} %get-tuple-element.66), channel_id=1, source_target_pairs={{0,128},{64,192},{128,0},{192,64},{1,129},{65,193},{129,1},{193,65... | collective-permute-start | bytes 393224 | tf_op jit(solution)/shard_map/ppermute | solution.py:318
  53.7 8.8 %collective-permute-start.21 = (f32[2,64,256]{2,1,0:T(8,128)S(1)}, f32[2,64,256]{2,1,0:T(8,128)S(1)}, u32[]{:S(2)}, u32[]{:S(2)}) collective-permute-start(f32[2,64,256]{2,1,0:T(8,128)S(1)} %get-tuple-element.69), channel_id=1, source_target_pairs={{0,192},{64,128},{128,64},{192,0},{1,193},{65,129},{129,65},{193,1... | collective-permute-start | bytes 393224 | tf_op jit(solution)/shard_map/ppermute | solution.py:318
  64.8 2.1 %collective-permute-start.22 = (f32[512,128]{1,0:T(8,128)S(1)}, f32[512,128]{1,0:T(8,128)S(1)}, u32[]{:S(2)}, u32[]{:S(2)}) collective-permute-start(f32[512,128]{1,0:T(8,128)S(1)} %get-tuple-element.73), channel_id=1, source_target_pairs={{0,1},{1,0},{2,3},{3,2},{4,5},{5,4},{6,7},{7,6},{8,9},{9,8},{10,11... | collective-permute-start | bytes 786440 | tf_op jit(solution)/shard_map/ppermute | solution.py:326
  102.7 22.9 %collective-permute-start.23 = (f32[512,128]{1,0:T(8,128)S(1)}, f32[512,128]{1,0:T(8,128)S(1)}, u32[]{:S(2)}, u32[]{:S(2)}) collective-permute-start(f32[512,128]{1,0:T(8,128)S(1)} %bitcast.10), channel_id=1, source_target_pairs={{0,1},{1,0},{2,3},{3,2},{4,5},{5,4},{6,7},{7,6},{8,9},{9,8},{10,11... | collective-permute-start | bytes 786440 | tf_op jit(solution)/shard_map/ppermute | solution.py:326
  105.7 4.4 %collective-permute-start.14 = (f32[1,64,256]{2,1,0:T(8,128)S(1)}, f32[1,64,256]{2,1,0:T(8,128)S(1)}, u32[]{:S(2)}, u32[]{:S(2)}) collective-permute-start(f32[1,64,256]{2,1,0:T(8,128)S(1)} %get-tuple-element.50), channel_id=1, source_target_pairs={{0,1},{1,0},{2,3},{3,2},{4,5},{5,4},{6,7},{7,6},{8,9},{9,8},{10,11... | collective-permute-start | bytes 196616 | tf_op jit(solution)/shard_map/ppermute | solution.py:326
  105.7 7.7 %collective-permute-start.15 = (f32[1,64,256]{2,1,0:T(8,128)S(1)}, f32[1,64,256]{2,1,0:T(8,128)S(1)}, u32[]{:S(2)}, u32[]{:S(2)}) collective-permute-start(f32[1,64,256]{2,1,0:T(8,128)S(1)} %get-tuple-element.51), channel_id=1, source_target_pairs={{1,2},{3,4},{5,6},{7,8},{9,10},{11,12},{13,14},{15,16},{17,18},{19... | collective-permute-start | bytes 196616 | tf_op jit(solution)/shard_map/ppermute | solution.py:333
  114.2 5.6 %collective-permute-start.16 = (f32[2,64,256]{2,1,0:T(8,128)S(1)}, f32[2,64,256]{2,1,0:T(8,128)S(1)}, u32[]{:S(2)}, u32[]{:S(2)}) collective-permute-start(f32[2,64,256]{2,1,0:T(8,128)S(1)} %get-tuple-element.57), channel_id=1, source_target_pairs={{0,64},{64,0},{128,192},{192,128},{1,65},{65,1},{129,193},{193,129... | collective-permute-start | bytes 393224 | tf_op jit(solution)/shard_map/ppermute | solution.py:318
  114.3 8.1 %collective-permute-start.17 = (f32[2,64,256]{2,1,0:T(8,128)S(1)}, f32[2,64,256]{2,1,0:T(8,128)S(1)}, u32[]{:S(2)}, u32[]{:S(2)}) collective-permute-start(f32[2,64,256]{2,1,0:T(8,128)S(1)} %get-tuple-element.58), channel_id=1, source_target_pairs={{0,128},{64,192},{128,0},{192,64},{1,129},{65,193},{129,1},{193,65... | collective-permute-start | bytes 393224 | tf_op jit(solution)/shard_map/ppermute | solution.py:318
  116.9 7.9 %collective-permute-start.18 = (f32[2,64,256]{2,1,0:T(8,128)S(1)}, f32[2,64,256]{2,1,0:T(8,128)S(1)}, u32[]{:S(2)}, u32[]{:S(2)}) collective-permute-start(f32[2,64,256]{2,1,0:T(8,128)S(1)} %get-tuple-element.59), channel_id=1, source_target_pairs={{0,192},{64,128},{128,64},{192,0},{1,193},{65,129},{129,65},{193,1... | collective-permute-start | bytes 393224 | tf_op jit(solution)/shard_map/ppermute | solution.py:318

commit v5 on v4

--- a/solution.py
+++ b/solution.py
@@ -147,7 +147,11 @@
     two_ref[0] = jnp.where(even, top[0], top[1])
 
 
-def taps_body(mine_ref, yours_ref, one_ref, three_ref, far0_ref, far1_ref, other_ref, out_ref):
+def above_body(one_ref, three_ref, out_ref):
+    out_ref[...] = jnp.where(lax.rem(section(), 2) == 0, one_ref[...], three_ref[...])
+
+
+def taps_body(mine_ref, yours_ref, one_ref, three_ref, far_ref, other_ref, out_ref):
     s = section()
     c = core()
 
@@ -163,7 +167,7 @@
     put(s, yours, yours_ref[...])
     put(s ^ 1, mine, one_ref[...])
     put(s ^ 3, mine, three_ref[...])
-    put(s ^ 2, mine, jnp.concatenate([far0_ref[...], far1_ref[...]], axis=0))
+    put(s ^ 2, mine, far_ref[...])
     put(s ^ 1, yours, other_ref[0:96])
     put(s ^ 3, yours, other_ref[96:192])
     put(s ^ 2, yours, other_ref[192:288])
@@ -373,10 +377,10 @@
 
     one = met(mine, 1)
     three_half = met(mine, 3)
-    far0 = met(three_half[:48], 1)
-    far1 = met(one[48:], 3)
-    other = swapped(jnp.concatenate([one, three_half, far0, far1], axis=0))
-    (taps,) = run(taps_body, (mine, yours, one, three_half, far0, far1, other), [((N, 384, 576), BF16)], flops=10**6)
+    (above,) = run(above_body, (one, three_half), [((96, 576), F32)], flops=10**6)
+    far = lax.ppermute(above, "section", [(i, (i - 1) % N) for i in range(N)])
+    other = swapped(jnp.concatenate([one, three_half, far], axis=0))
+    (taps,) = run(taps_body, (mine, yours, one, three_half, far, other), [((N, 384, 576), BF16)], flops=10**6)
 
     one_plane = ((1, *plane), F32)
     five = ((5, *plane), F32)

time: 127 us -> 125 us (0.984)
    ppermute x13 -> x11, starting transfers between devices: 15.8 us -> 13.9 us  [met(): return lax.ppermute(x, 'section', [(i, i ^ k) for i in range(N)])]
    ppermute x0 -> x1, starting transfers between devices: none -> 1.57 us  [window(): far = lax.ppermute(above, 'section', [(i, (i - 1) % N) for i in range(N)])]
    ppermute x3, starting transfers between devices: 14 us -> 12.6 us  [neighbours(): outer = lax.ppermute(outer, DEPTH, pairs + [(j, i) for i, j in pairs])]
    ppermute x3, waiting for transfers between devices: 7.48 us -> 6.16 us  [neighbours(): outer = lax.ppermute(outer, DEPTH, pairs + [(j, i) for i, j in pairs])]
    ppermute x13 -> x11, waiting for transfers between devices: 24 us -> 24.8 us  [met(): return lax.ppermute(x, 'section', [(i, i ^ k) for i in range(N)])]
    pallas_call x11 -> x12, Pallas kernels: 12.4 us -> 12.5 us  [run(): pl.pallas_call(body, out_shape=[jax.ShapeDtypeStruct(s, t) for s, t in ou...]
  transfers between devices with their start and end apart: 24 -> 23, of which waited for: 16 -> 15; matrix products, arithmetic and copies ran while one was open for 1% -> 0% of each run, Pallas kernels for 4% -> 4%
where the time goes in v5:
time: 125 us
  starting transfers between devices  38.2 us (31%)
  waiting for transfers between devices  36.4 us (29%)
  blocking collectives  35.7 us (29%)
  Pallas kernels  12.5 us (10%)
  local copies, waits for them, and re-layouts  1.29 us (1%)
    ppermute x11, waiting for transfers between devices, met(): return lax.ppermute(x, 'section', [(i, i ^ k) for i in range(N)])  24.8 us
    all_to_all x1, blocking collectives, window(): part = lax.all_to_all(part, PLANE, 0, 0, tiled=True)  20.4 us
    all_to_all x1, blocking collectives, window(): lax.all_to_all(jnp.broadcast_to(total[None], (32, 16, 128)), PLANE, 0, 0,...  15.2 us
    ppermute x11, starting transfers between devices, met(): return lax.ppermute(x, 'section', [(i, i ^ k) for i in range(N)])  13.9 us
    ppermute x3, starting transfers between devices, neighbours(): outer = lax.ppermute(outer, DEPTH, pairs + [(j, i) for i, j in pairs])  12.6 us
    pallas_call x12, Pallas kernels, run(): pl.pallas_call(body, out_shape=[jax.ShapeDtypeStruct(s, t) for s, t in ou...  12.5 us
    ppermute x6, starting transfers between devices, swapped(): return lax.ppermute(x, CORE, [(0, 1), (1, 0)])  6.45 us
    ppermute x3, waiting for transfers between devices, neighbours(): outer = lax.ppermute(outer, DEPTH, pairs + [(j, i) for i, j in pairs])  6.16 us
  transfers between devices with their start and end apart: 23, of which 15 were waited for; matrix products, arithmetic and copies ran while one was open for 0% of the time, Pallas kernels for 4%

profile of v5, /device:TPU:25, one launch (start us, length us, event | category | flops | bytes accessed | tf_op | source)
XLA Modules:
  0.0 125.0 jit_solution(630480996106325888)
XLA Ops:
  0.6 0.0 copy-start
  0.6 1.2 copy-done.1
  1.9 0.5 shard_map.50
  2.3 2.6 %collective-permute-start.10 = (f32[96,576]{1,0:T(8,128)S(1)}, f32[96,576]{1,0:T(8,128)S(1)}, u32[]{:S(2)}, u32[]{:S(2)}) collective-permute-start(f32[96,576]{1,0:T(8,128)S(1)} %get-tuple-element.48.mine_ref), channel_id=1, source_target_pairs={{0,192},{64,128},{128,64},{192,0},{1,193},{65,129},{129,65},{193,1... | collective-permute-start | bytes 663560 | tf_op jit(solution)/shard_map/ppermute | solution.py:322
  4.9 0.0 collective-permute-start.9
  4.9 5.6 %collective-permute-done.10.three_ref = f32[96,576]{1,0:T(8,128)S(1)} collective-permute-done((f32[96,576]{1,0:T(8,128)S(1)}, f32[96,576]{1,0:T(8,128)S(1)}, u32[]{:S(2)}, u32[]{:S(2)}) %collective-permute-start.10) | collective-permute-done | bytes 221216 | tf_op jit(solution)/shard_map/ppermute | solution.py:322
  10.5 1.0 collective-permute-done.9.one_ref
  11.5 1.6 %collective-permute-start.11 = (f32[96,576]{1,0:T(8,128)S(1)}, f32[96,576]{1,0:T(8,128)S(1)}, u32[]{:S(2)}, u32[]{:S(2)}) collective-permute-start(f32[96,576]{1,0:T(8,128)S(1)} %shard_map.55), channel_id=1, source_target_pairs={{0,192},{64,0},{128,64},{192,128},{1,193},{65,1},{129,65},{193,129... | collective-permute-start | bytes 663560 | tf_op jit(solution)/shard_map/ppermute | solution.py:381
  13.1 4.9 %collective-permute-start.1 = (f32[4,64,256]{2,1,0:T(8,128)S(1)}, f32[4,64,256]{2,1,0:T(8,128)S(1)}, u32[]{:S(2)}, u32[]{:S(2)}) collective-permute-start(f32[4,64,256]{2,1,0:T(8,128)S(1)} %get-tuple-element.74), channel_id=1, source_target_pairs={{1,2},{3,4},{5,6},{7,8},{9,10},{11,12},{13,14},{15,16},{17,18},{19... | collective-permute-start | bytes 786440 | tf_op jit(solution)/shard_map/ppermute | solution.py:337
  18.0 0.1 collective-permute-start
  18.1 0.0 collective-permute-done.11.far_ref
  18.1 0.1 pad_maximum_fusion
  18.2 1.9 %collective-permute-start.12 = (f32[288,576]{1,0:T(8,128)S(1)}, f32[288,576]{1,0:T(8,128)S(1)}, u32[]{:S(2)}, u32[]{:S(2)}) collective-permute-start(f32[288,576]{1,0:T(8,128)S(1)} %pad_maximum_fusion), channel_id=1, source_target_pairs={{0,1},{1,0},{2,3},{3,2},{4,5},{5,4},{6,7},{7,6},{8,9},{9,8},{10,11... | collective-permute-start | bytes 1990664 | tf_op jit(solution)/shard_map/ppermute | solution.py:330
  20.1 2.8 %collective-permute-done.1.outer_ref = f32[4,64,256]{2,1,0:T(8,128)S(1)} collective-permute-done((f32[4,64,256]{2,1,0:T(8,128)S(1)}, f32[4,64,256]{2,1,0:T(8,128)S(1)}, u32[]{:S(2)}, u32[]{:S(2)}) %collective-permute-start.1) | collective-permute-done | bytes 262176 | tf_op jit(solution)/shard_map/ppermute | solution.py:337
  22.9 0.0 collective-permute-done.inner_ref
  22.9 0.9 shard_map.53
  23.8 0.0 copy-start.2
  23.8 0.4 collective-permute-start.3
  24.3 1.3 %shard_map.52 = (f32[2,64,256]{2,1,0:T(8,128)S(1)}, bf16[4,192,256]{2,1,0:T(8,128)(2,1)S(1)}, bf16[4,192,256]{2,1,0:T(8,128)(2,1)S(1)}, f32[2,64,256]{2,1,0:T(8,...) custom-call(f32[4,2,64,256]{3,2,1,0:T(8,128)S(1)} %bitcast.8, ...), custom_call_target="tpu_custom_call" | custom-call | flops 679477248 | bytes 1490944 | tf_op jit(solution)/shard_map/pallas_call | solution.py:28
  25.6 0.3 collective-permute-start.2
  25.9 2.6 %collective-permute-start.4 = (f32[2,64,256]{2,1,0:T(8,128)S(1)}, f32[2,64,256]{2,1,0:T(8,128)S(1)}, u32[]{:S(2)}, u32[]{:S(2)}) collective-permute-start(f32[2,64,256]{2,1,0:T(8,128)S(1)} %get-tuple-element.42), channel_id=1, source_target_pairs={{0,192},{64,128},{128,64},{192,0},{1,193},{65,129},{129,65},{193,1... | collective-permute-start | bytes 393224 | tf_op jit(solution)/shard_map/ppermute | solution.py:322
  28.6 0.9 shard_map.51
  29.4 1.3 %collective-permute-done.3.d2 = f32[2,64,256]{2,1,0:T(8,128)S(1)} collective-permute-done((f32[2,64,256]{2,1,0:T(8,128)S(1)}, f32[2,64,256]{2,1,0:T(8,128)S(1)}, u32[]{:S(2)}, u32[]{:S(2)}) %collective-permute-start.3) | collective-permute-done | bytes 131104 | tf_op jit(solution)/shard_map/ppermute | solution.py:322
  30.8 0.1 collective-permute-done.2.d1
  30.9 2.7 %collective-permute-done.4.d3 = f32[2,64,256]{2,1,0:T(8,128)S(1)} collective-permute-done((f32[2,64,256]{2,1,0:T(8,128)S(1)}, f32[2,64,256]{2,1,0:T(8,128)S(1)}, u32[]{:S(2)}, u32[]{:S(2)}) %collective-permute-start.4) | collective-permute-done | bytes 131104 | tf_op jit(solution)/shard_map/ppermute | solution.py:322
  33.6 0.0 copy-done.2
  33.6 0.1 shard_map.54
  33.8 0.6 collective-permute-start.5
  34.3 3.4 %collective-permute-start.6 = (f32[5,64,256]{2,1,0:T(8,128)S(1)}, f32[5,64,256]{2,1,0:T(8,128)S(1)}, u32[]{:S(2)}, u32[]{:S(2)}) collective-permute-start(f32[5,64,256]{2,1,0:T(8,128)S(1)} %get-tuple-element.44), channel_id=1, source_target_pairs={{1,2},{3,4},{5,6},{7,8},{9,10},{11,12},{13,14},{15,16},{17,18},{19... | collective-permute-start | bytes 983048 | tf_op jit(solution)/shard_map/ppermute | solution.py:337
  37.7 0.1 collective-permute-start.7
  37.8 3.6 %collective-permute-start.8 = (f32[1,64,256]{2,1,0:T(8,128)S(1)}, f32[1,64,256]{2,1,0:T(8,128)S(1)}, u32[]{:S(2)}, u32[]{:S(2)}) collective-permute-start(f32[1,64,256]{2,1,0:T(8,128)S(1)} %get-tuple-element.46), channel_id=1, source_target_pairs={{2,4},{3,5},{6,8},{7,9},{10,12},{11,13},{14,16},{15,17},{18,20},{1... | collective-permute-start | bytes 196616 | tf_op jit(solution)/shard_map/ppermute | solution.py:346
  41.4 0.0 collective-permute-done.12.other_ref
  41.4 0.3 shard_map.56.taps_ref
  41.7 1.7 %collective-permute-done.7.one_in = f32[1,64,256]{2,1,0:T(8,128)S(1)} collective-permute-done((f32[1,64,256]{2,1,0:T(8,128)S(1)}, f32[1,64,256]{2,1,0:T(8,128)S(1)}, u32[]{:S(2)}, u32[]{:S(2)}) %collective-permute-start.7) | collective-permute-done | bytes 65568 | tf_op jit(solution)/shard_map/ppermute | solution.py:346
  43.4 2.5 %collective-permute-done.8.two_in = f32[1,64,256]{2,1,0:T(8,128)S(1)} collective-permute-done((f32[1,64,256]{2,1,0:T(8,128)S(1)}, f32[1,64,256]{2,1,0:T(8,128)S(1)}, u32[]{:S(2)}, u32[]{:S(2)}) %collective-permute-start.8) | collective-permute-done | bytes 65568 | tf_op jit(solution)/shard_map/ppermute | solution.py:346
  45.9 0.0 collective-permute-done.5.inner_in
  46.0 0.0 collective-permute-done.6.outer_in
  46.0 3.4 %shard_map.57 = (f32[2,64,256]{2,1,0:T(8,128)S(1)}, f32[2,64,256]{2,1,0:T(8,128)S(1)}, f32[2,64,256]{2,1,0:T(8,128)S(1)}, f32[2,64,256]{2,1,0:T(8,128)S(1)}, f32...) custom-call(f32[5,64,256]{2,1,0:T(8,128)S(1)} %collective-permute-do, ...), custom_call_target="tpu_custom_call" | custom-call | flops 2038431744 | bytes 3211264 | tf_op jit(solution)/shard_map/pallas_call | solution.py:28
  49.3 0.4 collective-permute-start.18
  49.7 2.8 %collective-permute-start.19 = (f32[2,64,256]{2,1,0:T(8,128)S(1)}, f32[2,64,256]{2,1,0:T(8,128)S(1)}, u32[]{:S(2)}, u32[]{:S(2)}) collective-permute-start(f32[2,64,256]{2,1,0:T(8,128)S(1)} %get-tuple-element.66), channel_id=1, source_target_pairs={{0,128},{64,192},{128,0},{192,64},{1,129},{65,193},{129,1},{193,65... | collective-permute-start | bytes 393224 | tf_op jit(solution)/shard_map/ppermute | solution.py:322
  52.5 0.8 collective-permute-start.20
  53.3 0.0 collective-permute-done.18.refs_3_
  53.3 5.5 %collective-permute-done.19.refs_6_ = f32[2,64,256]{2,1,0:T(8,128)S(1)} collective-permute-done((f32[2,64,256]{2,1,0:T(8,128)S(1)}, f32[2,64,256]{2,1,0:T(8,128)S(1)}, u32[]{:S(2)}, u32[]{:S(2)}) %collective-permute-start.19) | collective-permute-done | bytes 131104 | tf_op jit(solution)/shard_map/ppermute | solution.py:322
  58.8 2.5 %collective-permute-done.20.refs_9_ = f32[2,64,256]{2,1,0:T(8,128)S(1)} collective-permute-done((f32[2,64,256]{2,1,0:T(8,128)S(1)}, f32[2,64,256]{2,1,0:T(8,128)S(1)}, u32[]{:S(2)}, u32[]{:S(2)}) %collective-permute-start.20) | collective-permute-done | bytes 131104 | tf_op jit(solution)/shard_map/ppermute | solution.py:322
  61.3 2.3 %shard_map.60 = (f32[512,128]{1,0:T(8,128)S(1)}, f32[512,128]{1,0:T(8,128)S(1)}) custom-call(f32[2,64,256]{2,1,0:T(8,128)S(1)} %get-tuple-element.60.refs_0_, bf16[4,192,256]{2,1,0:T(8,128)(2,1)S(1)} %get-tuple-element.61.refs_1_, bf16[4,192,256]{2,1,0:T(8,128)(2,1)S(1)} %get-tuple-element.62.refs_2_, f32[2,64,256]{2,1,0:T(8,128)S(1)} %collective-permute-done.18.refs_3_, ...), custom_call_target="tpu_custom_call" | custom-call | flops 1358954496 | bytes 3670016 | tf_op jit(solution)/shard_map/pallas_call | solution.py:28
  63.6 0.9 collective-permute-start.21
  64.5 1.2 collective-permute-done.21
  65.8 20.4 %all_to_all.10 = f32[32,16,128]{2,1,0:T(8,128)S(1)} all-to-all(f32[32,16,128]{2,1,0:T(8,128)S(1)} %bitcast.12), channel_id=1, replica_groups=mesh['section'=4,'depth_0'=8,'depth_1'=4,'depth_2'=2] {'depth_0','depth_1'}, dimensions={0} | all-to-all | bytes 524288 | tf_op jit(solution)/shard_map/all_to_all | solution.py:419
  86.2 15.2 %all_to_all.11 = f32[32,16,128]{2,1,0:T(8,128)S(1)} all-to-all(f32[32,16,128]{2,1,0:T(8,128)S(1)} %broadcast_in_dim.2), channel_id=1, replica_groups=mesh['section'=4,'depth_0'=8,'depth_1'=4,'depth_2'=2] {'depth_0','depth_1'}, dimensions={0} | all-to-all | bytes 524288 | tf_op jit(solution)/shard_map/all_to_all | solution.py:422
  101.5 3.0 %collective-permute-start.22 = (f32[512,128]{1,0:T(8,128)S(1)}, f32[512,128]{1,0:T(8,128)S(1)}, u32[]{:S(2)}, u32[]{:S(2)}) collective-permute-start(f32[512,128]{1,0:T(8,128)S(1)} %bitcast.10), channel_id=1, source_target_pairs={{0,1},{1,0},{2,3},{3,2},{4,5},{5,4},{6,7},{7,6},{8,9},{9,8},{10,11... | collective-permute-start | bytes 786440 | tf_op jit(solution)/shard_map/ppermute | solution.py:330
  104.5 0.0 collective-permute-start.13
  104.5 4.3 %collective-permute-start.14 = (f32[1,64,256]{2,1,0:T(8,128)S(1)}, f32[1,64,256]{2,1,0:T(8,128)S(1)}, u32[]{:S(2)}, u32[]{:S(2)}) collective-permute-start(f32[1,64,256]{2,1,0:T(8,128)S(1)} %get-tuple-element.51), channel_id=1, source_target_pairs={{1,2},{3,4},{5,6},{7,8},{9,10},{11,12},{13,14},{15,16},{17,18},{19... | collective-permute-start | bytes 196616 | tf_op jit(solution)/shard_map/ppermute | solution.py:337
  108.8 0.0 collective-permute-done.13.inner_in
  108.8 3.3 %collective-permute-done.14.outer_in = f32[1,64,256]{2,1,0:T(8,128)S(1)} collective-permute-done((f32[1,64,256]{2,1,0:T(8,128)S(1)}, f32[1,64,256]{2,1,0:T(8,128)S(1)}, u32[]{:S(2)}, u32[]{:S(2)}) %collective-permute-start.14) | collective-permute-done | bytes 65568 | tf_op jit(solution)/shard_map/ppermute | solution.py:337
  112.1 0.9 shard_map.58
  113.0 0.1 collective-permute-start.15
  113.1 2.0 %collective-permute-start.16 = (f32[2,64,256]{2,1,0:T(8,128)S(1)}, f32[2,64,256]{2,1,0:T(8,128)S(1)}, u32[]{:S(2)}, u32[]{:S(2)}) collective-permute-start(f32[2,64,256]{2,1,0:T(8,128)S(1)} %get-tuple-element.58), channel_id=1, source_target_pairs={{0,128},{64,192},{128,0},{192,64},{1,129},{65,193},{129,1},{193,65... | collective-permute-start | bytes 393224 | tf_op jit(solution)/shard_map/ppermute | solution.py:322
  115.1 1.9 %collective-permute-start.17 = (f32[2,64,256]{2,1,0:T(8,128)S(1)}, f32[2,64,256]{2,1,0:T(8,128)S(1)}, u32[]{:S(2)}, u32[]{:S(2)}) collective-permute-start(f32[2,64,256]{2,1,0:T(8,128)S(1)} %get-tuple-element.59), channel_id=1, source_target_pairs={{0,192},{64,128},{128,64},{192,0},{1,193},{65,129},{129,65},{193,1... | collective-permute-start | bytes 393224 | tf_op jit(solution)/shard_map/ppermute | solution.py:322
  117.0 1.7 %collective-permute-done.15.x1 = f32[2,64,256]{2,1,0:T(8,128)S(1)} collective-permute-done((f32[2,64,256]{2,1,0:T(8,128)S(1)}, f32[2,64,256]{2,1,0:T(8,128)S(1)}, u32[]{:S(2)}, u32[]{:S(2)}) %collective-permute-start.15) | collective-permute-done | bytes 131104 | tf_op jit(solution)/shard_map/ppermute | solution.py:322
  118.6 2.0 %collective-permute-done.16.x2 = f32[2,64,256]{2,1,0:T(8,128)S(1)} collective-permute-done((f32[2,64,256]{2,1,0:T(8,128)S(1)}, f32[2,64,256]{2,1,0:T(8,128)S(1)}, u32[]{:S(2)}, u32[]{:S(2)}) %collective-permute-start.16) | collective-permute-done | bytes 131104 | tf_op jit(solution)/shard_map/ppermute | solution.py:322
  120.6 2.4 %collective-permute-done.17.x3 = f32[2,64,256]{2,1,0:T(8,128)S(1)} collective-permute-done((f32[2,64,256]{2,1,0:T(8,128)S(1)}, f32[2,64,256]{2,1,0:T(8,128)S(1)}, u32[]{:S(2)}, u32[]{:S(2)}) %collective-permute-start.17) | collective-permute-done | bytes 131104 | tf_op jit(solution)/shard_map/ppermute | solution.py:322
  123.0 0.8 shard_map.59
  123.8 0.0 collective-permute-done.22.other_ref
  123.8 1.1 shard_map.61
  (8 shorter events, 0.2 us)
Async XLA Ops:
  0.6 12.5 %copy-start = (f32[1,4,2,64,256]{4,3,2,1,0:T(8,128)S(1)}, f32[1,4,2,64,256]{4,3,2,1,0:T(8,128)}, u32[]{:S(2)}) copy-start(f32[1,4,2,64,256]{4,3,2,1,0:T(8,128)} %param.3) | copy-start | bytes 1572868
  0.6 1.2 copy-start.1
  2.3 8.1 %collective-permute-start.10 = (f32[96,576]{1,0:T(8,128)S(1)}, f32[96,576]{1,0:T(8,128)S(1)}, u32[]{:S(2)}, u32[]{:S(2)}) collective-permute-start(f32[96,576]{1,0:T(8,128)S(1)} %get-tuple-element.48.mine_ref), channel_id=1, source_target_pairs={{0,192},{64,128},{128,64},{192,0},{1,193},{65,129},{129,65},{193,1... | collective-permute-start | bytes 663560 | tf_op jit(solution)/shard_map/ppermute | solution.py:322
  4.9 6.6 %collective-permute-start.9 = (f32[96,576]{1,0:T(8,128)S(1)}, f32[96,576]{1,0:T(8,128)S(1)}, u32[]{:S(2)}, u32[]{:S(2)}) collective-permute-start(f32[96,576]{1,0:T(8,128)S(1)} %get-tuple-element.48.mine_ref), channel_id=1, source_target_pairs={{0,64},{64,0},{128,192},{192,128},{1,65},{65,1},{129,193},{193,129... | collective-permute-start | bytes 663560 | tf_op jit(solution)/shard_map/ppermute | solution.py:322
  11.5 6.6 %collective-permute-start.11 = (f32[96,576]{1,0:T(8,128)S(1)}, f32[96,576]{1,0:T(8,128)S(1)}, u32[]{:S(2)}, u32[]{:S(2)}) collective-permute-start(f32[96,576]{1,0:T(8,128)S(1)} %shard_map.55), channel_id=1, source_target_pairs={{0,192},{64,0},{128,64},{192,128},{1,193},{65,1},{129,65},{193,129... | collective-permute-start | bytes 663560 | tf_op jit(solution)/shard_map/ppermute | solution.py:381
  13.1 9.8 %collective-permute-start.1 = (f32[4,64,256]{2,1,0:T(8,128)S(1)}, f32[4,64,256]{2,1,0:T(8,128)S(1)}, u32[]{:S(2)}, u32[]{:S(2)}) collective-permute-start(f32[4,64,256]{2,1,0:T(8,128)S(1)} %get-tuple-element.74), channel_id=1, source_target_pairs={{1,2},{3,4},{5,6},{7,8},{9,10},{11,12},{13,14},{15,16},{17,18},{19... | collective-permute-start | bytes 786440 | tf_op jit(solution)/shard_map/ppermute | solution.py:337
  18.0 4.9 %collective-permute-start = (f32[4,64,256]{2,1,0:T(8,128)S(1)}, f32[4,64,256]{2,1,0:T(8,128)S(1)}, u32[]{:S(2)}, u32[]{:S(2)}) collective-permute-start(f32[4,64,256]{2,1,0:T(8,128)S(1)} %get-tuple-element.75), channel_id=1, source_target_pairs={{0,1},{1,0},{2,3},{3,2},{4,5},{5,4},{6,7},{7,6},{8,9},{9,8},{10,11... | collective-permute-start | bytes 786440 | tf_op jit(solution)/shard_map/ppermute | solution.py:330
  18.2 23.2 %collective-permute-start.12 = (f32[288,576]{1,0:T(8,128)S(1)}, f32[288,576]{1,0:T(8,128)S(1)}, u32[]{:S(2)}, u32[]{:S(2)}) collective-permute-start(f32[288,576]{1,0:T(8,128)S(1)} %pad_maximum_fusion), channel_id=1, source_target_pairs={{0,1},{1,0},{2,3},{3,2},{4,5},{5,4},{6,7},{7,6},{8,9},{9,8},{10,11... | collective-permute-start | bytes 1990664 | tf_op jit(solution)/shard_map/ppermute | solution.py:330
  23.8 9.8 %copy-start.2 = (f32[4,2,64,256]{3,2,1,0:T(8,128)S(1)}, f32[4,2,64,256]{3,2,1,0:T(8,128)}, u32[]{:S(2)}) copy-start(f32[4,2,64,256]{3,2,1,0:T(8,128)} %cot_ref.1) | copy-start | bytes 1572868
  23.8 6.9 %collective-permute-start.3 = (f32[2,64,256]{2,1,0:T(8,128)S(1)}, f32[2,64,256]{2,1,0:T(8,128)S(1)}, u32[]{:S(2)}, u32[]{:S(2)}) collective-permute-start(f32[2,64,256]{2,1,0:T(8,128)S(1)} %get-tuple-element.41), channel_id=1, source_target_pairs={{0,128},{64,192},{128,0},{192,64},{1,129},{65,193},{129,1},{193,65... | collective-permute-start | bytes 393224 | tf_op jit(solution)/shard_map/ppermute | solution.py:322
  25.6 5.3 %collective-permute-start.2 = (f32[2,64,256]{2,1,0:T(8,128)S(1)}, f32[2,64,256]{2,1,0:T(8,128)S(1)}, u32[]{:S(2)}, u32[]{:S(2)}) collective-permute-start(f32[2,64,256]{2,1,0:T(8,128)S(1)} %get-tuple-element.40), channel_id=1, source_target_pairs={{0,64},{64,0},{128,192},{192,128},{1,65},{65,1},{129,193},{193,129... | collective-permute-start | bytes 393224 | tf_op jit(solution)/shard_map/ppermute | solution.py:322
  25.9 7.7 %collective-permute-start.4 = (f32[2,64,256]{2,1,0:T(8,128)S(1)}, f32[2,64,256]{2,1,0:T(8,128)S(1)}, u32[]{:S(2)}, u32[]{:S(2)}) collective-permute-start(f32[2,64,256]{2,1,0:T(8,128)S(1)} %get-tuple-element.42), channel_id=1, source_target_pairs={{0,192},{64,128},{128,64},{192,0},{1,193},{65,129},{129,65},{193,1... | collective-permute-start | bytes 393224 | tf_op jit(solution)/shard_map/ppermute | solution.py:322
  33.8 12.2 %collective-permute-start.5 = (f32[5,64,256]{2,1,0:T(8,128)S(1)}, f32[5,64,256]{2,1,0:T(8,128)S(1)}, u32[]{:S(2)}, u32[]{:S(2)}) collective-permute-start(f32[5,64,256]{2,1,0:T(8,128)S(1)} %get-tuple-element.43), channel_id=1, source_target_pairs={{0,1},{1,0},{2,3},{3,2},{4,5},{5,4},{6,7},{7,6},{8,9},{9,8},{10,11... | collective-permute-start | bytes 983048 | tf_op jit(solution)/shard_map/ppermute | solution.py:330
  34.3 11.6 %collective-permute-start.6 = (f32[5,64,256]{2,1,0:T(8,128)S(1)}, f32[5,64,256]{2,1,0:T(8,128)S(1)}, u32[]{:S(2)}, u32[]{:S(2)}) collective-permute-start(f32[5,64,256]{2,1,0:T(8,128)S(1)} %get-tuple-element.44), channel_id=1, source_target_pairs={{1,2},{3,4},{5,6},{7,8},{9,10},{11,12},{13,14},{15,16},{17,18},{19... | collective-permute-start | bytes 983048 | tf_op jit(solution)/shard_map/ppermute | solution.py:337
  37.7 5.7 %collective-permute-start.7 = (f32[1,64,256]{2,1,0:T(8,128)S(1)}, f32[1,64,256]{2,1,0:T(8,128)S(1)}, u32[]{:S(2)}, u32[]{:S(2)}) collective-permute-start(f32[1,64,256]{2,1,0:T(8,128)S(1)} %get-tuple-element.45), channel_id=1, source_target_pairs={{0,2},{1,3},{4,6},{5,7},{8,10},{9,11},{12,14},{13,15},{16,18},{17,... | collective-permute-start | bytes 196616 | tf_op jit(solution)/shard_map/ppermute | solution.py:346
  37.8 8.1 %collective-permute-start.8 = (f32[1,64,256]{2,1,0:T(8,128)S(1)}, f32[1,64,256]{2,1,0:T(8,128)S(1)}, u32[]{:S(2)}, u32[]{:S(2)}) collective-permute-start(f32[1,64,256]{2,1,0:T(8,128)S(1)} %get-tuple-element.46), channel_id=1, source_target_pairs={{2,4},{3,5},{6,8},{7,9},{10,12},{11,13},{14,16},{15,17},{18,20},{1... | collective-permute-start | bytes 196616 | tf_op jit(solution)/shard_map/ppermute | solution.py:346
  49.3 3.9 %collective-permute-start.18 = (f32[2,64,256]{2,1,0:T(8,128)S(1)}, f32[2,64,256]{2,1,0:T(8,128)S(1)}, u32[]{:S(2)}, u32[]{:S(2)}) collective-permute-start(f32[2,64,256]{2,1,0:T(8,128)S(1)} %get-tuple-element.63), channel_id=1, source_target_pairs={{0,64},{64,0},{128,192},{192,128},{1,65},{65,1},{129,193},{193,129... | collective-permute-start | bytes 393224 | tf_op jit(solution)/shard_map/ppermute | solution.py:322
  49.7 9.1 %collective-permute-start.19 = (f32[2,64,256]{2,1,0:T(8,128)S(1)}, f32[2,64,256]{2,1,0:T(8,128)S(1)}, u32[]{:S(2)}, u32[]{:S(2)}) collective-permute-start(f32[2,64,256]{2,1,0:T(8,128)S(1)} %get-tuple-element.66), channel_id=1, source_target_pairs={{0,128},{64,192},{128,0},{192,64},{1,129},{65,193},{129,1},{193,65... | collective-permute-start | bytes 393224 | tf_op jit(solution)/shard_map/ppermute | solution.py:322
  52.5 8.9 %collective-permute-start.20 = (f32[2,64,256]{2,1,0:T(8,128)S(1)}, f32[2,64,256]{2,1,0:T(8,128)S(1)}, u32[]{:S(2)}, u32[]{:S(2)}) collective-permute-start(f32[2,64,256]{2,1,0:T(8,128)S(1)} %get-tuple-element.69), channel_id=1, source_target_pairs={{0,192},{64,128},{128,64},{192,0},{1,193},{65,129},{129,65},{193,1... | collective-permute-start | bytes 393224 | tf_op jit(solution)/shard_map/ppermute | solution.py:322
  63.6 2.1 %collective-permute-start.21 = (f32[512,128]{1,0:T(8,128)S(1)}, f32[512,128]{1,0:T(8,128)S(1)}, u32[]{:S(2)}, u32[]{:S(2)}) collective-permute-start(f32[512,128]{1,0:T(8,128)S(1)} %get-tuple-element.73), channel_id=1, source_target_pairs={{0,1},{1,0},{2,3},{3,2},{4,5},{5,4},{6,7},{7,6},{8,9},{9,8},{10,11... | collective-permute-start | bytes 786440 | tf_op jit(solution)/shard_map/ppermute | solution.py:330
  101.5 22.3 %collective-permute-start.22 = (f32[512,128]{1,0:T(8,128)S(1)}, f32[512,128]{1,0:T(8,128)S(1)}, u32[]{:S(2)}, u32[]{:S(2)}) collective-permute-start(f32[512,128]{1,0:T(8,128)S(1)} %bitcast.10), channel_id=1, source_target_pairs={{0,1},{1,0},{2,3},{3,2},{4,5},{5,4},{6,7},{7,6},{8,9},{9,8},{10,11... | collective-permute-start | bytes 786440 | tf_op jit(solution)/shard_map/ppermute | solution.py:330
  104.5 4.4 %collective-permute-start.13 = (f32[1,64,256]{2,1,0:T(8,128)S(1)}, f32[1,64,256]{2,1,0:T(8,128)S(1)}, u32[]{:S(2)}, u32[]{:S(2)}) collective-permute-start(f32[1,64,256]{2,1,0:T(8,128)S(1)} %get-tuple-element.50), channel_id=1, source_target_pairs={{0,1},{1,0},{2,3},{3,2},{4,5},{5,4},{6,7},{7,6},{8,9},{9,8},{10,11... | collective-permute-start | bytes 196616 | tf_op jit(solution)/shard_map/ppermute | solution.py:330
  104.5 7.7 %collective-permute-start.14 = (f32[1,64,256]{2,1,0:T(8,128)S(1)}, f32[1,64,256]{2,1,0:T(8,128)S(1)}, u32[]{:S(2)}, u32[]{:S(2)}) collective-permute-start(f32[1,64,256]{2,1,0:T(8,128)S(1)} %get-tuple-element.51), channel_id=1, source_target_pairs={{1,2},{3,4},{5,6},{7,8},{9,10},{11,12},{13,14},{15,16},{17,18},{19... | collective-permute-start | bytes 196616 | tf_op jit(solution)/shard_map/ppermute | solution.py:337
  113.0 5.6 %collective-permute-start.15 = (f32[2,64,256]{2,1,0:T(8,128)S(1)}, f32[2,64,256]{2,1,0:T(8,128)S(1)}, u32[]{:S(2)}, u32[]{:S(2)}) collective-permute-start(f32[2,64,256]{2,1,0:T(8,128)S(1)} %get-tuple-element.57), channel_id=1, source_target_pairs={{0,64},{64,0},{128,192},{192,128},{1,65},{65,1},{129,193},{193,129... | collective-permute-start | bytes 393224 | tf_op jit(solution)/shard_map/ppermute | solution.py:322
  113.1 7.5 %collective-permute-start.16 = (f32[2,64,256]{2,1,0:T(8,128)S(1)}, f32[2,64,256]{2,1,0:T(8,128)S(1)}, u32[]{:S(2)}, u32[]{:S(2)}) collective-permute-start(f32[2,64,256]{2,1,0:T(8,128)S(1)} %get-tuple-element.58), channel_id=1, source_target_pairs={{0,128},{64,192},{128,0},{192,64},{1,129},{65,193},{129,1},{193,65... | collective-permute-start | bytes 393224 | tf_op jit(solution)/shard_map/ppermute | solution.py:322
  115.1 7.9 %collective-permute-start.17 = (f32[2,64,256]{2,1,0:T(8,128)S(1)}, f32[2,64,256]{2,1,0:T(8,128)S(1)}, u32[]{:S(2)}, u32[]{:S(2)}) collective-permute-start(f32[2,64,256]{2,1,0:T(8,128)S(1)} %get-tuple-element.59), channel_id=1, source_target_pairs={{0,192},{64,128},{128,64},{192,0},{1,193},{65,129},{129,65},{193,1... | collective-permute-start | bytes 393224 | tf_op jit(solution)/shard_map/ppermute | solution.py:322

commit v6 on v5

--- a/solution.py
+++ b/solution.py
@@ -78,6 +78,11 @@
     return z[C : 2 * C] + down(z[:C]) + up(z[2 * C :])
 
 
+def conv_wide(taps, high, low):
+    z = dot(taps, jnp.concatenate([high, high, low], axis=0))
+    return z[C : 2 * C] + down(z[:C]) + up(z[2 * C :])
+
+
 def silu_slope(preact):
     gate = 1.0 / (1.0 + jnp.exp(-preact))
     return gate * (1.0 + preact * (1.0 - gate))
@@ -86,11 +91,9 @@
 def prepare_body(f_ref, forward_ref, mine_ref, yours_ref, back):
     for b in range(3):
         rows = slice(b * C, b * C + C)
-        low_rows = slice(192 + b * C, 192 + b * C + C)
         taps = [f_ref[0, a * 9 + b * 3 + cc] for a in range(3) for cc in range(3)]
         high, low = split(jnp.concatenate(taps, axis=1))
-        forward_ref[rows] = high
-        forward_ref[low_rows] = low
+        forward_ref[rows] = jnp.concatenate([high, low, high], axis=1)
         taps = [f_ref[0, (2 - a) * 9 + (2 - b) * 3 + 2 - cc] for a in range(3) for cc in range(3)]
         back[rows] = jnp.concatenate(taps, axis=0).T
     c = core()
@@ -114,7 +117,7 @@
             vh_ref[e] = high
             vl_ref[e] = low
         for d in range(2):
-            z = conv(taps_ref[...], vh_ref[d : d + 3].reshape(576, 256), vl_ref[d : d + 3].reshape(576, 256))
+            z = conv_wide(taps_ref[...], vh_ref[d : d + 3].reshape(576, 256), vl_ref[d : d + 3].reshape(576, 256))
             out[d] = silu_slope(z)
 
 
@@ -359,7 +362,7 @@
     forward, mine, yours = run(
         prepare_body,
         (filters,),
-        [((384, 576), BF16), ((96, 576), F32), ((96, 576), F32)],
+        [((192, 1728), BF16), ((96, 576), F32), ((96, 576), F32)],
         [((192, 576), F32)],
         flops=10**6,
     )

time: 125 us -> 126 us (level)
  no operation moved by 1% of the time
where the time goes in v6:
time: 126 us; the launch traced here: 125 us
  starting transfers between devices  38.2 us (30%)
  waiting for transfers between devices  36.8 us (29%)
  blocking collectives  35.7 us (28%)
  Pallas kernels  12.4 us (10%)
  local copies, waits for them, and re-layouts  1.29 us (1%)
    ppermute x11, waiting for transfers between devices, met(): return lax.ppermute(x, 'section', [(i, i ^ k) for i in range(N)])  25.7 us
    all_to_all x1, blocking collectives, window(): part = lax.all_to_all(part, PLANE, 0, 0, tiled=True)  20.4 us
    all_to_all x1, blocking collectives, window(): lax.all_to_all(jnp.broadcast_to(total[None], (32, 16, 128)), PLANE, 0, 0,...  15.2 us
    ppermute x11, starting transfers between devices, met(): return lax.ppermute(x, 'section', [(i, i ^ k) for i in range(N)])  13.9 us
    ppermute x3, starting transfers between devices, neighbours(): outer = lax.ppermute(outer, DEPTH, pairs + [(j, i) for i, j in pairs])  12.4 us
    pallas_call x12, Pallas kernels, run(): pl.pallas_call(body, out_shape=[jax.ShapeDtypeStruct(s, t) for s, t in ou...  12.4 us
    ppermute x6, starting transfers between devices, swapped(): return lax.ppermute(x, CORE, [(0, 1), (1, 0)])  6.44 us
    ppermute x3, waiting for transfers between devices, neighbours(): outer = lax.ppermute(outer, DEPTH, pairs + [(j, i) for i, j in pairs])  6.18 us
  transfers between devices with their start and end apart: 23, of which 15 were waited for; matrix products, arithmetic and copies ran while one was open for 0% of the time, Pallas kernels for 4%

profile of v6, /device:TPU:25, one launch (start us, length us, event | category | flops | bytes accessed | tf_op | source)
XLA Modules:
  0.0 125.3 jit_solution(3463120362811034303)
XLA Ops:
  0.6 0.0 copy-start
  0.6 1.2 copy-done.1
  1.9 0.8 shard_map.50
  2.6 2.6 %collective-permute-start.10 = (f32[96,576]{1,0:T(8,128)S(1)}, f32[96,576]{1,0:T(8,128)S(1)}, u32[]{:S(2)}, u32[]{:S(2)}) collective-permute-start(f32[96,576]{1,0:T(8,128)S(1)} %get-tuple-element.48.mine_ref), channel_id=1, source_target_pairs={{0,192},{64,128},{128,64},{192,0},{1,193},{65,129},{129,65},{193,1... | collective-permute-start | bytes 663560 | tf_op jit(solution)/shard_map/ppermute | solution.py:325
  5.2 0.0 collective-permute-start.9
  5.2 5.6 %collective-permute-done.10.three_ref = f32[96,576]{1,0:T(8,128)S(1)} collective-permute-done((f32[96,576]{1,0:T(8,128)S(1)}, f32[96,576]{1,0:T(8,128)S(1)}, u32[]{:S(2)}, u32[]{:S(2)}) %collective-permute-start.10) | collective-permute-done | bytes 221216 | tf_op jit(solution)/shard_map/ppermute | solution.py:325
  10.8 1.0 collective-permute-done.9.one_ref
  11.8 1.6 %collective-permute-start.11 = (f32[96,576]{1,0:T(8,128)S(1)}, f32[96,576]{1,0:T(8,128)S(1)}, u32[]{:S(2)}, u32[]{:S(2)}) collective-permute-start(f32[96,576]{1,0:T(8,128)S(1)} %shard_map.55), channel_id=1, source_target_pairs={{0,192},{64,0},{128,64},{192,128},{1,193},{65,1},{129,65},{193,129... | collective-permute-start | bytes 663560 | tf_op jit(solution)/shard_map/ppermute | solution.py:384
  13.4 4.9 %collective-permute-start.1 = (f32[4,64,256]{2,1,0:T(8,128)S(1)}, f32[4,64,256]{2,1,0:T(8,128)S(1)}, u32[]{:S(2)}, u32[]{:S(2)}) collective-permute-start(f32[4,64,256]{2,1,0:T(8,128)S(1)} %get-tuple-element.74), channel_id=1, source_target_pairs={{1,2},{3,4},{5,6},{7,8},{9,10},{11,12},{13,14},{15,16},{17,18},{19... | collective-permute-start | bytes 786440 | tf_op jit(solution)/shard_map/ppermute | solution.py:340
  18.3 0.1 collective-permute-start
  18.4 0.0 collective-permute-done.11.far_ref
  18.4 0.1 pad_maximum_fusion
  18.5 1.9 %collective-permute-start.12 = (f32[288,576]{1,0:T(8,128)S(1)}, f32[288,576]{1,0:T(8,128)S(1)}, u32[]{:S(2)}, u32[]{:S(2)}) collective-permute-start(f32[288,576]{1,0:T(8,128)S(1)} %pad_maximum_fusion), channel_id=1, source_target_pairs={{0,1},{1,0},{2,3},{3,2},{4,5},{5,4},{6,7},{7,6},{8,9},{9,8},{10,11... | collective-permute-start | bytes 1990664 | tf_op jit(solution)/shard_map/ppermute | solution.py:333
  20.4 2.8 %collective-permute-done.1.outer_ref = f32[4,64,256]{2,1,0:T(8,128)S(1)} collective-permute-done((f32[4,64,256]{2,1,0:T(8,128)S(1)}, f32[4,64,256]{2,1,0:T(8,128)S(1)}, u32[]{:S(2)}, u32[]{:S(2)}) %collective-permute-start.1) | collective-permute-done | bytes 262176 | tf_op jit(solution)/shard_map/ppermute | solution.py:340
  23.2 0.0 collective-permute-done.inner_ref
  23.2 0.8 shard_map.53
  24.0 0.0 copy-start.2
  24.0 0.4 collective-permute-start.3
  24.4 1.1 shard_map.52
  25.6 0.3 collective-permute-start.2
  25.9 2.6 %collective-permute-start.4 = (f32[2,64,256]{2,1,0:T(8,128)S(1)}, f32[2,64,256]{2,1,0:T(8,128)S(1)}, u32[]{:S(2)}, u32[]{:S(2)}) collective-permute-start(f32[2,64,256]{2,1,0:T(8,128)S(1)} %get-tuple-element.42), channel_id=1, source_target_pairs={{0,192},{64,128},{128,64},{192,0},{1,193},{65,129},{129,65},{193,1... | collective-permute-start | bytes 393224 | tf_op jit(solution)/shard_map/ppermute | solution.py:325
  28.6 0.8 shard_map.51
  29.3 1.6 %collective-permute-done.3.d2 = f32[2,64,256]{2,1,0:T(8,128)S(1)} collective-permute-done((f32[2,64,256]{2,1,0:T(8,128)S(1)}, f32[2,64,256]{2,1,0:T(8,128)S(1)}, u32[]{:S(2)}, u32[]{:S(2)}) %collective-permute-start.3) | collective-permute-done | bytes 131104 | tf_op jit(solution)/shard_map/ppermute | solution.py:325
  31.0 0.3 collective-permute-done.2.d1
  31.2 2.6 %collective-permute-done.4.d3 = f32[2,64,256]{2,1,0:T(8,128)S(1)} collective-permute-done((f32[2,64,256]{2,1,0:T(8,128)S(1)}, f32[2,64,256]{2,1,0:T(8,128)S(1)}, u32[]{:S(2)}, u32[]{:S(2)}) %collective-permute-start.4) | collective-permute-done | bytes 131104 | tf_op jit(solution)/shard_map/ppermute | solution.py:325
  33.8 0.0 copy-done.2
  33.8 0.1 shard_map.54
  33.9 0.6 collective-permute-start.5
  34.5 3.2 %collective-permute-start.6 = (f32[5,64,256]{2,1,0:T(8,128)S(1)}, f32[5,64,256]{2,1,0:T(8,128)S(1)}, u32[]{:S(2)}, u32[]{:S(2)}) collective-permute-start(f32[5,64,256]{2,1,0:T(8,128)S(1)} %get-tuple-element.44), channel_id=1, source_target_pairs={{1,2},{3,4},{5,6},{7,8},{9,10},{11,12},{13,14},{15,16},{17,18},{19... | collective-permute-start | bytes 983048 | tf_op jit(solution)/shard_map/ppermute | solution.py:340
  37.7 0.2 collective-permute-start.7
  37.9 3.7 %collective-permute-start.8 = (f32[1,64,256]{2,1,0:T(8,128)S(1)}, f32[1,64,256]{2,1,0:T(8,128)S(1)}, u32[]{:S(2)}, u32[]{:S(2)}) collective-permute-start(f32[1,64,256]{2,1,0:T(8,128)S(1)} %get-tuple-element.46), channel_id=1, source_target_pairs={{2,4},{3,5},{6,8},{7,9},{10,12},{11,13},{14,16},{15,17},{18,20},{1... | collective-permute-start | bytes 196616 | tf_op jit(solution)/shard_map/ppermute | solution.py:349
  41.6 0.0 collective-permute-done.12.other_ref
  41.6 0.3 shard_map.56.taps_ref
  41.9 1.7 %collective-permute-done.7.one_in = f32[1,64,256]{2,1,0:T(8,128)S(1)} collective-permute-done((f32[1,64,256]{2,1,0:T(8,128)S(1)}, f32[1,64,256]{2,1,0:T(8,128)S(1)}, u32[]{:S(2)}, u32[]{:S(2)}) %collective-permute-start.7) | collective-permute-done | bytes 65568 | tf_op jit(solution)/shard_map/ppermute | solution.py:349
  43.6 2.1 %collective-permute-done.8.two_in = f32[1,64,256]{2,1,0:T(8,128)S(1)} collective-permute-done((f32[1,64,256]{2,1,0:T(8,128)S(1)}, f32[1,64,256]{2,1,0:T(8,128)S(1)}, u32[]{:S(2)}, u32[]{:S(2)}) %collective-permute-start.8) | collective-permute-done | bytes 65568 | tf_op jit(solution)/shard_map/ppermute | solution.py:349
  45.7 0.0 collective-permute-done.5.inner_in
  45.7 0.0 collective-permute-done.6.outer_in
  45.7 3.4 %shard_map.57 = (f32[2,64,256]{2,1,0:T(8,128)S(1)}, f32[2,64,256]{2,1,0:T(8,128)S(1)}, f32[2,64,256]{2,1,0:T(8,128)S(1)}, f32[2,64,256]{2,1,0:T(8,128)S(1)}, f32...) custom-call(f32[5,64,256]{2,1,0:T(8,128)S(1)} %collective-permute-do, ...), custom_call_target="tpu_custom_call" | custom-call | flops 2038431744 | bytes 3211264 | tf_op jit(solution)/shard_map/pallas_call | solution.py:28
  49.1 0.6 collective-permute-start.18
  49.7 2.8 %collective-permute-start.19 = (f32[2,64,256]{2,1,0:T(8,128)S(1)}, f32[2,64,256]{2,1,0:T(8,128)S(1)}, u32[]{:S(2)}, u32[]{:S(2)}) collective-permute-start(f32[2,64,256]{2,1,0:T(8,128)S(1)} %get-tuple-element.66), channel_id=1, source_target_pairs={{0,128},{64,192},{128,0},{192,64},{1,129},{65,193},{129,1},{193,65... | collective-permute-start | bytes 393224 | tf_op jit(solution)/shard_map/ppermute | solution.py:325
  52.4 0.6 collective-permute-start.20
  53.1 0.0 collective-permute-done.18.refs_3_
  53.1 5.7 %collective-permute-done.19.refs_6_ = f32[2,64,256]{2,1,0:T(8,128)S(1)} collective-permute-done((f32[2,64,256]{2,1,0:T(8,128)S(1)}, f32[2,64,256]{2,1,0:T(8,128)S(1)}, u32[]{:S(2)}, u32[]{:S(2)}) %collective-permute-start.19) | collective-permute-done | bytes 131104 | tf_op jit(solution)/shard_map/ppermute | solution.py:325
  58.8 2.5 %collective-permute-done.20.refs_9_ = f32[2,64,256]{2,1,0:T(8,128)S(1)} collective-permute-done((f32[2,64,256]{2,1,0:T(8,128)S(1)}, f32[2,64,256]{2,1,0:T(8,128)S(1)}, u32[]{:S(2)}, u32[]{:S(2)}) %collective-permute-start.20) | collective-permute-done | bytes 131104 | tf_op jit(solution)/shard_map/ppermute | solution.py:325
  61.3 2.3 %shard_map.60 = (f32[512,128]{1,0:T(8,128)S(1)}, f32[512,128]{1,0:T(8,128)S(1)}) custom-call(f32[2,64,256]{2,1,0:T(8,128)S(1)} %get-tuple-element.60.refs_0_, bf16[4,192,256]{2,1,0:T(8,128)(2,1)S(1)} %get-tuple-element.61.refs_1_, bf16[4,192,256]{2,1,0:T(8,128)(2,1)S(1)} %get-tuple-element.62.refs_2_, f32[2,64,256]{2,1,0:T(8,128)S(1)} %collective-permute-done.18.refs_3_, ...), custom_call_target="tpu_custom_call" | custom-call | flops 1358954496 | bytes 3670016 | tf_op jit(solution)/shard_map/pallas_call | solution.py:28
  63.6 0.9 collective-permute-start.21
  64.5 1.2 collective-permute-done.21
  65.7 20.4 %all_to_all.10 = f32[32,16,128]{2,1,0:T(8,128)S(1)} all-to-all(f32[32,16,128]{2,1,0:T(8,128)S(1)} %bitcast.12), channel_id=1, replica_groups=mesh['section'=4,'depth_0'=8,'depth_1'=4,'depth_2'=2] {'depth_0','depth_1'}, dimensions={0} | all-to-all | bytes 524288 | tf_op jit(solution)/shard_map/all_to_all | solution.py:422
  86.2 15.2 %all_to_all.11 = f32[32,16,128]{2,1,0:T(8,128)S(1)} all-to-all(f32[32,16,128]{2,1,0:T(8,128)S(1)} %broadcast_in_dim.2), channel_id=1, replica_groups=mesh['section'=4,'depth_0'=8,'depth_1'=4,'depth_2'=2] {'depth_0','depth_1'}, dimensions={0} | all-to-all | bytes 524288 | tf_op jit(solution)/shard_map/all_to_all | solution.py:425
  101.5 3.0 %collective-permute-start.22 = (f32[512,128]{1,0:T(8,128)S(1)}, f32[512,128]{1,0:T(8,128)S(1)}, u32[]{:S(2)}, u32[]{:S(2)}) collective-permute-start(f32[512,128]{1,0:T(8,128)S(1)} %bitcast.10), channel_id=1, source_target_pairs={{0,1},{1,0},{2,3},{3,2},{4,5},{5,4},{6,7},{7,6},{8,9},{9,8},{10,11... | collective-permute-start | bytes 786440 | tf_op jit(solution)/shard_map/ppermute | solution.py:333
  104.4 0.0 collective-permute-start.13
  104.5 4.3 %collective-permute-start.14 = (f32[1,64,256]{2,1,0:T(8,128)S(1)}, f32[1,64,256]{2,1,0:T(8,128)S(1)}, u32[]{:S(2)}, u32[]{:S(2)}) collective-permute-start(f32[1,64,256]{2,1,0:T(8,128)S(1)} %get-tuple-element.51), channel_id=1, source_target_pairs={{1,2},{3,4},{5,6},{7,8},{9,10},{11,12},{13,14},{15,16},{17,18},{19... | collective-permute-start | bytes 196616 | tf_op jit(solution)/shard_map/ppermute | solution.py:340
  108.8 0.0 collective-permute-done.13.inner_in
  108.8 3.3 %collective-permute-done.14.outer_in = f32[1,64,256]{2,1,0:T(8,128)S(1)} collective-permute-done((f32[1,64,256]{2,1,0:T(8,128)S(1)}, f32[1,64,256]{2,1,0:T(8,128)S(1)}, u32[]{:S(2)}, u32[]{:S(2)}) %collective-permute-start.14) | collective-permute-done | bytes 65568 | tf_op jit(solution)/shard_map/ppermute | solution.py:340
  112.1 0.9 shard_map.58
  113.0 0.1 collective-permute-start.15
  113.1 2.3 %collective-permute-start.16 = (f32[2,64,256]{2,1,0:T(8,128)S(1)}, f32[2,64,256]{2,1,0:T(8,128)S(1)}, u32[]{:S(2)}, u32[]{:S(2)}) collective-permute-start(f32[2,64,256]{2,1,0:T(8,128)S(1)} %get-tuple-element.58), channel_id=1, source_target_pairs={{0,128},{64,192},{128,0},{192,64},{1,129},{65,193},{129,1},{193,65... | collective-permute-start | bytes 393224 | tf_op jit(solution)/shard_map/ppermute | solution.py:325
  115.4 1.5 %collective-permute-start.17 = (f32[2,64,256]{2,1,0:T(8,128)S(1)}, f32[2,64,256]{2,1,0:T(8,128)S(1)}, u32[]{:S(2)}, u32[]{:S(2)}) collective-permute-start(f32[2,64,256]{2,1,0:T(8,128)S(1)} %get-tuple-element.59), channel_id=1, source_target_pairs={{0,192},{64,128},{128,64},{192,0},{1,193},{65,129},{129,65},{193,1... | collective-permute-start | bytes 393224 | tf_op jit(solution)/shard_map/ppermute | solution.py:325
  117.0 1.7 %collective-permute-done.15.x1 = f32[2,64,256]{2,1,0:T(8,128)S(1)} collective-permute-done((f32[2,64,256]{2,1,0:T(8,128)S(1)}, f32[2,64,256]{2,1,0:T(8,128)S(1)}, u32[]{:S(2)}, u32[]{:S(2)}) %collective-permute-start.15) | collective-permute-done | bytes 131104 | tf_op jit(solution)/shard_map/ppermute | solution.py:325
  118.6 2.3 %collective-permute-done.16.x2 = f32[2,64,256]{2,1,0:T(8,128)S(1)} collective-permute-done((f32[2,64,256]{2,1,0:T(8,128)S(1)}, f32[2,64,256]{2,1,0:T(8,128)S(1)}, u32[]{:S(2)}, u32[]{:S(2)}) %collective-permute-start.16) | collective-permute-done | bytes 131104 | tf_op jit(solution)/shard_map/ppermute | solution.py:325
  120.9 2.4 %collective-permute-done.17.x3 = f32[2,64,256]{2,1,0:T(8,128)S(1)} collective-permute-done((f32[2,64,256]{2,1,0:T(8,128)S(1)}, f32[2,64,256]{2,1,0:T(8,128)S(1)}, u32[]{:S(2)}, u32[]{:S(2)}) %collective-permute-start.17) | collective-permute-done | bytes 131104 | tf_op jit(solution)/shard_map/ppermute | solution.py:325
  123.3 0.8 shard_map.59
  124.1 0.0 collective-permute-done.22.other_ref
  124.1 1.1 shard_map.61
  (8 shorter events, 0.2 us)
Async XLA Ops:
  0.6 12.7 %copy-start = (f32[1,4,2,64,256]{4,3,2,1,0:T(8,128)S(1)}, f32[1,4,2,64,256]{4,3,2,1,0:T(8,128)}, u32[]{:S(2)}) copy-start(f32[1,4,2,64,256]{4,3,2,1,0:T(8,128)} %param.3) | copy-start | bytes 1572868
  0.6 1.2 copy-start.1
  2.6 8.1 %collective-permute-start.10 = (f32[96,576]{1,0:T(8,128)S(1)}, f32[96,576]{1,0:T(8,128)S(1)}, u32[]{:S(2)}, u32[]{:S(2)}) collective-permute-start(f32[96,576]{1,0:T(8,128)S(1)} %get-tuple-element.48.mine_ref), channel_id=1, source_target_pairs={{0,192},{64,128},{128,64},{192,0},{1,193},{65,129},{129,65},{193,1... | collective-permute-start | bytes 663560 | tf_op jit(solution)/shard_map/ppermute | solution.py:325
  5.2 6.6 %collective-permute-start.9 = (f32[96,576]{1,0:T(8,128)S(1)}, f32[96,576]{1,0:T(8,128)S(1)}, u32[]{:S(2)}, u32[]{:S(2)}) collective-permute-start(f32[96,576]{1,0:T(8,128)S(1)} %get-tuple-element.48.mine_ref), channel_id=1, source_target_pairs={{0,64},{64,0},{128,192},{192,128},{1,65},{65,1},{129,193},{193,129... | collective-permute-start | bytes 663560 | tf_op jit(solution)/shard_map/ppermute | solution.py:325
  11.8 6.6 %collective-permute-start.11 = (f32[96,576]{1,0:T(8,128)S(1)}, f32[96,576]{1,0:T(8,128)S(1)}, u32[]{:S(2)}, u32[]{:S(2)}) collective-permute-start(f32[96,576]{1,0:T(8,128)S(1)} %shard_map.55), channel_id=1, source_target_pairs={{0,192},{64,0},{128,64},{192,128},{1,193},{65,1},{129,65},{193,129... | collective-permute-start | bytes 663560 | tf_op jit(solution)/shard_map/ppermute | solution.py:384
  13.4 9.8 %collective-permute-start.1 = (f32[4,64,256]{2,1,0:T(8,128)S(1)}, f32[4,64,256]{2,1,0:T(8,128)S(1)}, u32[]{:S(2)}, u32[]{:S(2)}) collective-permute-start(f32[4,64,256]{2,1,0:T(8,128)S(1)} %get-tuple-element.74), channel_id=1, source_target_pairs={{1,2},{3,4},{5,6},{7,8},{9,10},{11,12},{13,14},{15,16},{17,18},{19... | collective-permute-start | bytes 786440 | tf_op jit(solution)/shard_map/ppermute | solution.py:340
  18.3 4.9 %collective-permute-start = (f32[4,64,256]{2,1,0:T(8,128)S(1)}, f32[4,64,256]{2,1,0:T(8,128)S(1)}, u32[]{:S(2)}, u32[]{:S(2)}) collective-permute-start(f32[4,64,256]{2,1,0:T(8,128)S(1)} %get-tuple-element.75), channel_id=1, source_target_pairs={{0,1},{1,0},{2,3},{3,2},{4,5},{5,4},{6,7},{7,6},{8,9},{9,8},{10,11... | collective-permute-start | bytes 786440 | tf_op jit(solution)/shard_map/ppermute | solution.py:333
  18.5 23.1 %collective-permute-start.12 = (f32[288,576]{1,0:T(8,128)S(1)}, f32[288,576]{1,0:T(8,128)S(1)}, u32[]{:S(2)}, u32[]{:S(2)}) collective-permute-start(f32[288,576]{1,0:T(8,128)S(1)} %pad_maximum_fusion), channel_id=1, source_target_pairs={{0,1},{1,0},{2,3},{3,2},{4,5},{5,4},{6,7},{7,6},{8,9},{9,8},{10,11... | collective-permute-start | bytes 1990664 | tf_op jit(solution)/shard_map/ppermute | solution.py:333
  24.0 9.8 %copy-start.2 = (f32[4,2,64,256]{3,2,1,0:T(8,128)S(1)}, f32[4,2,64,256]{3,2,1,0:T(8,128)}, u32[]{:S(2)}) copy-start(f32[4,2,64,256]{3,2,1,0:T(8,128)} %cot_ref.1) | copy-start | bytes 1572868
  24.0 7.0 %collective-permute-start.3 = (f32[2,64,256]{2,1,0:T(8,128)S(1)}, f32[2,64,256]{2,1,0:T(8,128)S(1)}, u32[]{:S(2)}, u32[]{:S(2)}) collective-permute-start(f32[2,64,256]{2,1,0:T(8,128)S(1)} %get-tuple-element.41), channel_id=1, source_target_pairs={{0,128},{64,192},{128,0},{192,64},{1,129},{65,193},{129,1},{193,65... | collective-permute-start | bytes 393224 | tf_op jit(solution)/shard_map/ppermute | solution.py:325
  25.6 5.7 %collective-permute-start.2 = (f32[2,64,256]{2,1,0:T(8,128)S(1)}, f32[2,64,256]{2,1,0:T(8,128)S(1)}, u32[]{:S(2)}, u32[]{:S(2)}) collective-permute-start(f32[2,64,256]{2,1,0:T(8,128)S(1)} %get-tuple-element.40), channel_id=1, source_target_pairs={{0,64},{64,0},{128,192},{192,128},{1,65},{65,1},{129,193},{193,129... | collective-permute-start | bytes 393224 | tf_op jit(solution)/shard_map/ppermute | solution.py:325
  25.9 7.9 %collective-permute-start.4 = (f32[2,64,256]{2,1,0:T(8,128)S(1)}, f32[2,64,256]{2,1,0:T(8,128)S(1)}, u32[]{:S(2)}, u32[]{:S(2)}) collective-permute-start(f32[2,64,256]{2,1,0:T(8,128)S(1)} %get-tuple-element.42), channel_id=1, source_target_pairs={{0,192},{64,128},{128,64},{192,0},{1,193},{65,129},{129,65},{193,1... | collective-permute-start | bytes 393224 | tf_op jit(solution)/shard_map/ppermute | solution.py:325
  33.9 11.7 %collective-permute-start.5 = (f32[5,64,256]{2,1,0:T(8,128)S(1)}, f32[5,64,256]{2,1,0:T(8,128)S(1)}, u32[]{:S(2)}, u32[]{:S(2)}) collective-permute-start(f32[5,64,256]{2,1,0:T(8,128)S(1)} %get-tuple-element.43), channel_id=1, source_target_pairs={{0,1},{1,0},{2,3},{3,2},{4,5},{5,4},{6,7},{7,6},{8,9},{9,8},{10,11... | collective-permute-start | bytes 983048 | tf_op jit(solution)/shard_map/ppermute | solution.py:333
  34.5 11.2 %collective-permute-start.6 = (f32[5,64,256]{2,1,0:T(8,128)S(1)}, f32[5,64,256]{2,1,0:T(8,128)S(1)}, u32[]{:S(2)}, u32[]{:S(2)}) collective-permute-start(f32[5,64,256]{2,1,0:T(8,128)S(1)} %get-tuple-element.44), channel_id=1, source_target_pairs={{1,2},{3,4},{5,6},{7,8},{9,10},{11,12},{13,14},{15,16},{17,18},{19... | collective-permute-start | bytes 983048 | tf_op jit(solution)/shard_map/ppermute | solution.py:340
  37.7 5.9 %collective-permute-start.7 = (f32[1,64,256]{2,1,0:T(8,128)S(1)}, f32[1,64,256]{2,1,0:T(8,128)S(1)}, u32[]{:S(2)}, u32[]{:S(2)}) collective-permute-start(f32[1,64,256]{2,1,0:T(8,128)S(1)} %get-tuple-element.45), channel_id=1, source_target_pairs={{0,2},{1,3},{4,6},{5,7},{8,10},{9,11},{12,14},{13,15},{16,18},{17,... | collective-permute-start | bytes 196616 | tf_op jit(solution)/shard_map/ppermute | solution.py:349
  37.9 7.8 %collective-permute-start.8 = (f32[1,64,256]{2,1,0:T(8,128)S(1)}, f32[1,64,256]{2,1,0:T(8,128)S(1)}, u32[]{:S(2)}, u32[]{:S(2)}) collective-permute-start(f32[1,64,256]{2,1,0:T(8,128)S(1)} %get-tuple-element.46), channel_id=1, source_target_pairs={{2,4},{3,5},{6,8},{7,9},{10,12},{11,13},{14,16},{15,17},{18,20},{1... | collective-permute-start | bytes 196616 | tf_op jit(solution)/shard_map/ppermute | solution.py:349
  49.1 3.9 %collective-permute-start.18 = (f32[2,64,256]{2,1,0:T(8,128)S(1)}, f32[2,64,256]{2,1,0:T(8,128)S(1)}, u32[]{:S(2)}, u32[]{:S(2)}) collective-permute-start(f32[2,64,256]{2,1,0:T(8,128)S(1)} %get-tuple-element.63), channel_id=1, source_target_pairs={{0,64},{64,0},{128,192},{192,128},{1,65},{65,1},{129,193},{193,129... | collective-permute-start | bytes 393224 | tf_op jit(solution)/shard_map/ppermute | solution.py:325
  49.7 9.1 %collective-permute-start.19 = (f32[2,64,256]{2,1,0:T(8,128)S(1)}, f32[2,64,256]{2,1,0:T(8,128)S(1)}, u32[]{:S(2)}, u32[]{:S(2)}) collective-permute-start(f32[2,64,256]{2,1,0:T(8,128)S(1)} %get-tuple-element.66), channel_id=1, source_target_pairs={{0,128},{64,192},{128,0},{192,64},{1,129},{65,193},{129,1},{193,65... | collective-permute-start | bytes 393224 | tf_op jit(solution)/shard_map/ppermute | solution.py:325
  52.4 8.9 %collective-permute-start.20 = (f32[2,64,256]{2,1,0:T(8,128)S(1)}, f32[2,64,256]{2,1,0:T(8,128)S(1)}, u32[]{:S(2)}, u32[]{:S(2)}) collective-permute-start(f32[2,64,256]{2,1,0:T(8,128)S(1)} %get-tuple-element.69), channel_id=1, source_target_pairs={{0,192},{64,128},{128,64},{192,0},{1,193},{65,129},{129,65},{193,1... | collective-permute-start | bytes 393224 | tf_op jit(solution)/shard_map/ppermute | solution.py:325
  63.6 2.1 %collective-permute-start.21 = (f32[512,128]{1,0:T(8,128)S(1)}, f32[512,128]{1,0:T(8,128)S(1)}, u32[]{:S(2)}, u32[]{:S(2)}) collective-permute-start(f32[512,128]{1,0:T(8,128)S(1)} %get-tuple-element.73), channel_id=1, source_target_pairs={{0,1},{1,0},{2,3},{3,2},{4,5},{5,4},{6,7},{7,6},{8,9},{9,8},{10,11... | collective-permute-start | bytes 786440 | tf_op jit(solution)/shard_map/ppermute | solution.py:333
  101.5 22.7 %collective-permute-start.22 = (f32[512,128]{1,0:T(8,128)S(1)}, f32[512,128]{1,0:T(8,128)S(1)}, u32[]{:S(2)}, u32[]{:S(2)}) collective-permute-start(f32[512,128]{1,0:T(8,128)S(1)} %bitcast.10), channel_id=1, source_target_pairs={{0,1},{1,0},{2,3},{3,2},{4,5},{5,4},{6,7},{7,6},{8,9},{9,8},{10,11... | collective-permute-start | bytes 786440 | tf_op jit(solution)/shard_map/ppermute | solution.py:333
  104.4 4.4 %collective-permute-start.13 = (f32[1,64,256]{2,1,0:T(8,128)S(1)}, f32[1,64,256]{2,1,0:T(8,128)S(1)}, u32[]{:S(2)}, u32[]{:S(2)}) collective-permute-start(f32[1,64,256]{2,1,0:T(8,128)S(1)} %get-tuple-element.50), channel_id=1, source_target_pairs={{0,1},{1,0},{2,3},{3,2},{4,5},{5,4},{6,7},{7,6},{8,9},{9,8},{10,11... | collective-permute-start | bytes 196616 | tf_op jit(solution)/shard_map/ppermute | solution.py:333
  104.5 7.7 %collective-permute-start.14 = (f32[1,64,256]{2,1,0:T(8,128)S(1)}, f32[1,64,256]{2,1,0:T(8,128)S(1)}, u32[]{:S(2)}, u32[]{:S(2)}) collective-permute-start(f32[1,64,256]{2,1,0:T(8,128)S(1)} %get-tuple-element.51), channel_id=1, source_target_pairs={{1,2},{3,4},{5,6},{7,8},{9,10},{11,12},{13,14},{15,16},{17,18},{19... | collective-permute-start | bytes 196616 | tf_op jit(solution)/shard_map/ppermute | solution.py:340
  113.0 5.6 %collective-permute-start.15 = (f32[2,64,256]{2,1,0:T(8,128)S(1)}, f32[2,64,256]{2,1,0:T(8,128)S(1)}, u32[]{:S(2)}, u32[]{:S(2)}) collective-permute-start(f32[2,64,256]{2,1,0:T(8,128)S(1)} %get-tuple-element.57), channel_id=1, source_target_pairs={{0,64},{64,0},{128,192},{192,128},{1,65},{65,1},{129,193},{193,129... | collective-permute-start | bytes 393224 | tf_op jit(solution)/shard_map/ppermute | solution.py:325
  113.1 7.8 %collective-permute-start.16 = (f32[2,64,256]{2,1,0:T(8,128)S(1)}, f32[2,64,256]{2,1,0:T(8,128)S(1)}, u32[]{:S(2)}, u32[]{:S(2)}) collective-permute-start(f32[2,64,256]{2,1,0:T(8,128)S(1)} %get-tuple-element.58), channel_id=1, source_target_pairs={{0,128},{64,192},{128,0},{192,64},{1,129},{65,193},{129,1},{193,65... | collective-permute-start | bytes 393224 | tf_op jit(solution)/shard_map/ppermute | solution.py:325
  115.4 7.9 %collective-permute-start.17 = (f32[2,64,256]{2,1,0:T(8,128)S(1)}, f32[2,64,256]{2,1,0:T(8,128)S(1)}, u32[]{:S(2)}, u32[]{:S(2)}) collective-permute-start(f32[2,64,256]{2,1,0:T(8,128)S(1)} %get-tuple-element.59), channel_id=1, source_target_pairs={{0,192},{64,128},{128,64},{192,0},{1,193},{65,129},{129,65},{193,1... | collective-permute-start | bytes 393224 | tf_op jit(solution)/shard_map/ppermute | solution.py:325
